TPU v7x, 512 devices: a 4x2x32 block of a 4x16x32 slice. The times are simulated.
512 devices in a mesh: group: 2 (over y), expert: 32 (over z), tensor: 4 (over x), sub: 2 (over core).
Axes of the slice: x: 4, y: 2, z: 32, core: 2. Of those that a mesh axis runs over, the one named last changes fastest.
The devices are a block of a 4x16x32 slice.
Arguments:
- tokens: bfloat16 [512, 7168], P(('group', 'expert', 'sub')), parts along dimension 0, may hold values from -6 to 6
- expert_ids: int32 [512, 8], P(('group', 'expert', 'sub')), parts along dimension 0, may hold values from 0 to 15, all different within a row; in each aligned block of 4 rows (0 to 3, 4 to 7, ...) at most 3 rows name the same one
- gate_codes: int32 [512, 8], P(('group', 'expert', 'sub')), parts along dimension 0, may hold values from 1 to 63
- w_gate: bfloat16 [32, 1024, 7168], P('expert', ('tensor', 'sub')), may hold values from -0.0625 to 0.0625
- w_up: bfloat16 [32, 1024, 7168], P('expert', ('tensor', 'sub')), may hold values from -0.0625 to 0.0625
- w_down: bfloat16 [32, 1024, 7168], P('expert', ('tensor', 'sub')), may hold values from -0.125 to 0.125
Outputs:
- mixed: bfloat16 [512, 7168], P(('group', 'expert', 'sub'), 'tensor'), parts along dimension 0
There are 2 independent parts, one for each index of `group`. A program takes and returns all parts, laid end to end along the dimension named above; an argument that names none is the same for every part. Nothing has to cross between parts.
Inputs may be any that keep to these rules, and one draw needn't show every extreme that they name: `expert_ids`: the 8 numbers of a row differ; within the rows of one device (aligned blocks of 4 rows) no expert is named by more than 3 rows, a bound that some block reaches.
All inputs are finite; a program needn't handle non-finite values.
Results may differ from a plain program's by a relative error of at most 0.008.
Values may be sent and summed in bfloat16 or wider, within the bound.
No kernel may reach another device: no remote copies, remote signals or barrier semaphores. Data moves between devices by JAX's collectives and lax.ppermute only.
A program may use at most 64 MiB of HBM per device.

v0:
```python
import jax
import jax.numpy as jnp
from jax import lax
from jax.sharding import PartitionSpec as P


def shards(tokens, expert_ids, gate_codes, w_gate, w_up, w_down):
    tok_rows, features = tokens.shape
    per_token = expert_ids.shape[1]
    owners = lax.axis_size("expert")
    sub_count = lax.axis_size("sub")
    tensor_count = lax.axis_size("tensor")
    experts = owners // 2
    capacity = min(tok_rows, tok_rows * per_token // experts + 1)
    flat_ids = expert_ids.reshape(-1)
    matches = (flat_ids[:, None] == jnp.arange(experts, dtype=jnp.int32)[None, :]).astype(jnp.int32)
    before = jnp.cumsum(matches, axis=0) - matches
    slot_index = jnp.sum(before * matches, axis=1)
    position = flat_ids * capacity + slot_index
    onehot = position[:, None] == jnp.arange(experts * capacity, dtype=jnp.int32)[None, :]
    weights = gate_codes.reshape(-1).astype(jnp.float32) / 64.0
    choose = jnp.any(onehot.reshape(tok_rows, per_token, -1), axis=1).astype(jnp.bfloat16)
    combine = jnp.sum(
        jnp.where(onehot, weights[:, None], 0.0).reshape(tok_rows, per_token, -1), axis=1
    )
    packed = jnp.dot(choose.T, tokens, preferred_element_type=jnp.float32).astype(jnp.bfloat16)
    outgoing = jnp.broadcast_to(
        packed.reshape(experts, 1, capacity, features), (experts, 2, capacity, features)
    )
    arrived = lax.all_to_all(
        outgoing.reshape(owners, capacity, features),
        "expert",
        split_axis=0,
        concat_axis=0,
        tiled=True,
    )
    slot_rows = lax.all_gather(arrived, "sub", axis=1, tiled=True).reshape(-1, features)
    contract = (((1,), (1,)), ((), ()))
    gate_act = lax.dot_general(slot_rows, w_gate[0], contract, preferred_element_type=jnp.float32)
    up_act = lax.dot_general(slot_rows, w_up[0], contract, preferred_element_type=jnp.float32)
    hidden = (jax.nn.silu(gate_act) * up_act).astype(jnp.bfloat16)
    partial_value = jnp.dot(hidden, w_down[0], preferred_element_type=jnp.float32).astype(
        jnp.bfloat16
    )
    partial_value = partial_value.reshape(owners, sub_count, capacity, features)
    block = features // tensor_count
    sectioned = partial_value.reshape(owners, sub_count, capacity, tensor_count, block).transpose(
        0, 2, 3, 1, 4
    )
    sectioned = sectioned.reshape(owners, capacity, tensor_count * sub_count, block)
    gathered = lax.all_to_all(sectioned, ("tensor", "sub"), split_axis=2, concat_axis=2, tiled=True)
    run_total = jnp.sum(gathered.astype(jnp.float32), axis=2)
    came_back = lax.all_to_all(
        run_total.astype(jnp.bfloat16), "expert", split_axis=0, concat_axis=0, tiled=True
    ).astype(run_total.dtype)
    summed = jnp.sum(came_back.reshape(experts, 2, capacity, block), axis=1)
    mixed = jnp.dot(
        combine,
        summed.reshape(-1, block),
        precision=lax.Precision.HIGHEST,
        preferred_element_type=jnp.float32,
    )
    return mixed.astype(jnp.bfloat16)


def solution(mesh):
    return jax.shard_map(
        shards,
        mesh=mesh,
        in_specs=(
            P(("group", "expert", "sub"), None),
            P(("group", "expert", "sub"), None),
            P(("group", "expert", "sub"), None),
            P("expert", ("tensor", "sub"), None),
            P("expert", ("tensor", "sub"), None),
            P("expert", ("tensor", "sub"), None),
        ),
        out_specs=P(("group", "expert", "sub"), "tensor"),
        check_vma=False,
    )
```

profile of v0, /device:TPU:40, one launch (start us, length us, event | category | flops | bytes accessed | tf_op | source)
XLA Modules:
  0.0 407.4 jit_solution(4467936220724837105)
XLA Ops:
  6.5 0.0 copy-start
  6.6 0.0 all-gather.2.cloned.1.call-start
  6.6 0.9 eq.30
  7.4 0.1 fusion.20
  7.5 0.1 reduce_window_sum.11
  7.6 0.2 select_reduce_fusion.1
  7.8 0.1 reduce_sum.42
  7.8 0.7 multiply_add_fusion
  8.5 0.1 fusion.19
  8.6 1.2 convolution_convert_fusion.1
  9.8 0.4 broadcast_in_dim.25
  10.3 0.5 broadcast_in_dim.26
  10.8 221.8 %all_to_all.15 = bf16[32,3,7168]{2,1,0:T(4,128)(2,1)S(1)} all-to-all(bf16[32,3,7168]{2,1,0:T(4,128)(2,1)S(1)} %bitcast.29), channel_id=1, replica_groups=mesh['group'=2,'expert'=32,'tensor'=4,'sub'=2] {'expert'}, dimensions={0} | all-to-all | bytes 2752512 | tf_op jit(solution)/shard_map/all_to_all | solution.py:30
  232.6 1.6 copy.21
  234.2 0.1 all-gather.2.cloned.1.call-update
  234.3 12.8 %all-gather.2.cloned.1.call-done = bf16[32,6,7168]{2,0,1:T(8,128)(2,1)} async-done(((bf16[32,3,7168]{2,0,1:T(8,128)(2,1)}), bf16[32,6,7168]{2,0,1:T(8,128)(2,1)}) %all-gather.2.cloned.1.call-update) | async-done | bytes 2752528 | tf_op jit(solution)/shard_map/all_gather | solution.py:37
  247.1 5.1 %copy.22 = bf16[32,6,7168]{2,1,0:T(8,128)(2,1)} copy(bf16[32,6,7168]{2,0,1:T(8,128)(2,1)} %all-gather.2.cloned.1.call-done) | data formatting | bytes 5505024 | tf_op jit(solution)/shard_map/all_gather | solution.py:37
  252.2 4.6 %reshape.60 = bf16[192,7168]{1,0:T(8,128)(2,1)} reshape(bf16[32,6,7168]{2,1,0:T(8,128)(2,1)} %copy.22) | data formatting | bytes 5505024 | tf_op jit(solution)/shard_map/reshape | solution.py:37
  256.9 3.2 fusion.3
  260.1 0.0 copy-done
  260.1 7.0 %convolution_convert_fusion = bf16[192,7168]{1,0:T(8,128)(2,1)} fusion(bf16[1,128,7168]{2,1,0:T(8,128)(2,1)S(1)} %copy-done, bf16[192,7168]{1,0:T(8,128)(2,1)} %reshape.60, bf16[1,128,7168]{2,1,0:T(8,128)(2,1)} %param.10, f32[192,128]{1,0:T(8,128)S(1)} %fusion.3), kind=kOutput, calls=%fused_computation | convolution fusion | flops 706166784 | bytes 9273344 | tf_op jit(solution)/shard_map/dot_general | solution.py:42
  267.0 6.2 %reshape_reshape.3 = bf16[32,2,3,4,1792]{4,3,2,1,0:T(4,128)(2,1)} reshape(bf16[192,7168]{1,0:T(8,128)(2,1)} %convolution_convert_fusion) | data formatting | bytes 5505024 | tf_op jit(solution)/shard_map/reshape;reshape | solution.py:47
  273.3 2.3 copy.29
  275.6 38.4 %all_to_all.16 = bf16[32,3,8,1792]{3,0,1,2:T(8,128)(2,1)} all-to-all(bf16[32,3,8,1792]{3,0,1,2:T(8,128)(2,1)S(1)} %bitcast.28), channel_id=1, replica_groups=mesh['group'=2,'expert'=32,'tensor'=4,'sub'=2] {'tensor','sub'}, dimensions={2} | all-to-all | bytes 5505024 | tf_op jit(solution)/shard_map/all_to_all | solution.py:51
  314.0 2.2 reduce_sum.44
  316.2 1.1 copy.26
  317.3 23.3 %all-to-all-start.2 = ((bf16[32,3,1792]{2,1,0:T(4,128)(2,1)}), bf16[32,3,1792]{2,1,0:T(4,128)(2,1)S(1)}, u32[]{:S(2)}, u32[]{:S(2)}) async-start(bf16[32,3,1792]{2,1,0:T(4,128)(2,1)} %copy.26), calls=%async_computation.2 | async-start | bytes 917504 | tf_op jit(solution)/shard_map/all_to_all | solution.py:53
  340.7 0.1 select_reduce_fusion
  340.7 58.5 %all-to-all-done.2 = bf16[32,3,1792]{2,1,0:T(4,128)(2,1)S(1)} async-done(((bf16[32,3,1792]{2,1,0:T(4,128)(2,1)}), bf16[32,3,1792]{2,1,0:T(4,128)(2,1)S(1)}, u32[]{:S(2)}, u32[]{:S(2)}) %all-to-all-start.2) | async-done | bytes 344096 | tf_op jit(solution)/shard_map/all_to_all | solution.py:53
  399.2 0.3 convert_reduce_fusion
  399.5 0.2 reshape.64
  399.6 0.9 convolution_convert_fusion.2
  (3 shorter events, 0.0 us)
Async XLA Ops:
  6.5 253.5 %copy-start = (bf16[1,128,7168]{2,1,0:T(8,128)(2,1)S(1)}, bf16[1,128,7168]{2,1,0:T(8,128)(2,1)}, u32[]{:S(2)}) copy-start(bf16[1,128,7168]{2,1,0:T(8,128)(2,1)} %param.11) | copy-start | bytes 5505028
  6.6 240.6 %all-gather.2.cloned.1.call-start = ((), (), s32[]{:S(2)}) async-start(), calls=%async_computation.3 | async-start | bytes 4128768 | tf_op jit(solution)/shard_map/all_gather | solution.py:37
  314.0 26.6 %copy-start.1 = (s32[4,8]{1,0:T(4,128)S(1)}, s32[4,8]{1,0:T(4,128)}, u32[]{:S(2)}) copy-start(s32[4,8]{1,0:T(4,128)} %param.8) | copy-start | bytes 388
  317.3 81.9 %all-to-all-start.2 = ((bf16[32,3,1792]{2,1,0:T(4,128)(2,1)}), bf16[32,3,1792]{2,1,0:T(4,128)(2,1)S(1)}, u32[]{:S(2)}, u32[]{:S(2)}) async-start(bf16[32,3,1792]{2,1,0:T(4,128)(2,1)} %copy.26), calls=%async_computation.2 | async-start | bytes 917504 | tf_op jit(solution)/shard_map/all_to_all | solution.py:53
Sparse Core Ops, SparseCore 0:
  234.4 12.6 all-gather.1
where the time goes:
time: 408 us; the launch traced here: 407 us
  blocking collectives  260 us (64%)
  waiting for transfers between devices  71.3 us (17%)
  starting transfers between devices  23.3 us (6%)
  local copies, waits for them, and re-layouts  23.1 us (6%)
  between operations  13.5 us (3%)
  matrix products  12.2 us (3%)
    all_to_all x1, blocking collectives, shards(): lax.all_to_all(outgoing.reshape(owners, capacity, features), 'expert', sp...  222 us
    all_to_all x1, waiting for transfers between devices, shards(): lax.all_to_all(run_total.astype(jnp.bfloat16), 'expert', split_axis=0, co...  58.5 us
    all_to_all x1, blocking collectives, shards(): lax.all_to_all(sectioned, ('tensor', 'sub'), split_axis=2, concat_axis=2,...  38.4 us
    all_to_all x1, starting transfers between devices, shards(): lax.all_to_all(run_total.astype(jnp.bfloat16), 'expert', split_axis=0, co...  23.3 us
    all_gather x1, waiting for transfers between devices, shards(): lax.all_gather(arrived, 'sub', axis=1, tiled=True).reshape(-1, features)  12.8 us
  transfers between devices with their start and end apart: 2, of which 2 were waited for; matrix products, arithmetic and copies ran while one was open for 0% of the time, Pallas kernels for 0%

commit v1 on v0

v1 whole, which is shorter than its diff:
```python
import functools

import jax
import jax.numpy as jnp
from jax import lax
from jax.experimental import pallas as pl
from jax.experimental.pallas import tpu as pltpu
from jax.sharding import PartitionSpec as P

BF = jnp.bfloat16
F32 = jnp.float32
VM = pl.BlockSpec(memory_space=pltpu.VMEM)
CONTRACT = (((1,), (1,)), ((), ()))


def hidden_kernel(x_ref, g_ref, u_ref, h_ref):
    parts, rows, block = x_ref.shape
    gate = jnp.zeros((rows, g_ref.shape[0]), F32)
    up = jnp.zeros((rows, u_ref.shape[0]), F32)
    for k in range(parts):
        cols = pl.ds(k * block, block)
        x = x_ref[k]
        gate += lax.dot_general(x, g_ref[:, cols], CONTRACT, preferred_element_type=F32)
        up += lax.dot_general(x, u_ref[:, cols], CONTRACT, preferred_element_type=F32)
    h_ref[...] = (gate / (1.0 + jnp.exp(-gate)) * up).astype(h_ref.dtype)


def hidden_of(x, g, u):
    parts, rows, block = x.shape
    units = g.shape[0]
    return pl.pallas_call(
        hidden_kernel,
        out_shape=jax.ShapeDtypeStruct((rows, units), BF),
        in_specs=[VM] * 3,
        out_specs=VM,
        cost_estimate=pl.CostEstimate(
            flops=4 * rows * units * parts * block,
            bytes_accessed=2 * (rows + 2 * units) * parts * block,
            transcendentals=rows * units,
        ),
        name="hidden",
    )(x, g, u)


def down_kernel(h_ref, d_ref, o_ref):
    parts, rows, block = o_ref.shape
    h = h_ref[...]
    for k in range(parts):
        o_ref[k] = jnp.dot(
            h, d_ref[:, pl.ds(k * block, block)], preferred_element_type=F32
        ).astype(o_ref.dtype)


def down_add_kernel(h_ref, d_ref, a_ref, o_ref):
    parts, rows, block = o_ref.shape
    h = h_ref[...]
    for k in range(parts):
        own = jnp.dot(h, d_ref[:, pl.ds(k * block, block)], preferred_element_type=F32)
        o_ref[k] = (own + a_ref[k].astype(F32)).astype(o_ref.dtype)


def down_of(h, d, parts, other=None):
    rows, units = h.shape
    block = d.shape[1] // parts
    args = (h, d) if other is None else (h, d, other)
    return pl.pallas_call(
        down_kernel if other is None else down_add_kernel,
        out_shape=jax.ShapeDtypeStruct((parts, rows, block), BF),
        in_specs=[VM] * len(args),
        out_specs=VM,
        cost_estimate=pl.CostEstimate(
            flops=2 * rows * units * parts * block,
            bytes_accessed=2 * (rows + units) * parts * block,
            transcendentals=0,
        ),
        name="down" if other is None else "down_add",
    )(*args)


def shards(tokens, expert_ids, gate_codes, w_gate, w_up, w_down):
    rows, features = tokens.shape
    per_token = expert_ids.shape[1]
    owners = lax.axis_size("expert")
    subs = lax.axis_size("sub")
    parts = lax.axis_size("tensor")
    experts = owners // 2
    capacity = min(rows, rows * per_token // experts + 1)
    block = features // parts
    half = block // 2
    here = lax.axis_index("tensor")
    odd = lax.axis_index("expert") % 2
    swap_sub = [(i, subs - 1 - i) for i in range(subs)]
    swap_pair = [(i, i ^ 1) for i in range(owners)]

    picks = expert_ids[:, :, None] == jnp.arange(experts, dtype=jnp.int32)
    named = jnp.any(picks, axis=1)
    weight = jnp.sum(jnp.where(picks, gate_codes[:, :, None].astype(F32) / 64.0, 0.0), axis=1)
    count = named.astype(jnp.int32)
    slot = [jnp.zeros((experts,), jnp.int32)]
    for t in range(1, rows):
        slot.append(slot[-1] + count[t - 1])
    slot = jnp.stack(slot)
    onehot = named[:, :, None] & (slot[:, :, None] == jnp.arange(capacity, dtype=jnp.int32))
    combine = jnp.where(onehot, weight[:, :, None], 0.0)

    mine = lax.dynamic_slice(tokens, (0, here * block), (rows, block))
    packed = jnp.einsum("tes,tpf->epsf", onehot.astype(BF), mine.reshape(rows, 2, half)).astype(BF)
    arrived = lax.all_to_all(
        packed.reshape(owners, capacity, half), "expert", split_axis=0, concat_axis=0, tiled=True
    )
    slots = owners * capacity
    arrived = arrived.reshape(slots, half)
    partner = lax.ppermute(arrived, "expert", swap_pair)
    low = jnp.where(odd == 0, arrived, partner)
    high = jnp.where(odd == 0, partner, arrived)
    quarter = jnp.concatenate([low, high], axis=1)
    own_rows = lax.all_to_all(
        jnp.broadcast_to(quarter[None], (parts, slots, block)),
        "tensor",
        split_axis=0,
        concat_axis=0,
        tiled=True,
    )
    other_rows = lax.ppermute(own_rows, "sub", swap_sub)
    own_hidden = hidden_of(own_rows, w_gate[0], w_up[0])
    other_hidden = hidden_of(other_rows, w_gate[0], w_up[0])
    other_part = down_of(other_hidden, w_down[0], parts)
    from_other = lax.ppermute(other_part, "sub", swap_sub)
    part = down_of(own_hidden, w_down[0], parts, from_other)
    gathered = lax.all_to_all(part, "tensor", split_axis=0, concat_axis=0, tiled=True)
    total = jnp.sum(gathered.astype(F32), axis=0)
    keep = jnp.where(odd == 0, total[:, :half], total[:, half:])
    give = jnp.where(odd == 0, total[:, half:], total[:, :half]).astype(BF)
    taken = lax.ppermute(give, "expert", swap_pair)
    both = (keep + taken.astype(F32)).astype(BF).reshape(owners, capacity, half)
    back = lax.all_to_all(both, "expert", split_axis=0, concat_axis=0, tiled=True)
    back = back.reshape(experts, 2, capacity, half).astype(F32)
    mixed = jnp.einsum(
        "tes,epsf->tpf", combine, back, precision=lax.Precision.HIGHEST, preferred_element_type=F32
    )
    return mixed.reshape(rows, block).astype(BF)


def solution(mesh):
    spread = P(("group", "expert", "sub"), None)
    weights = P("expert", ("tensor", "sub"), None)
    return jax.shard_map(
        shards,
        mesh=mesh,
        in_specs=(spread, spread, spread, weights, weights, weights),
        out_specs=P(("group", "expert", "sub"), "tensor"),
        check_vma=False,
    )
```

time: 408 us -> 215 us (0.53)
  blocking collectives: 260 us -> 128 us
  waiting for transfers between devices: 71.3 us -> 51.7 us
  local copies, waits for them, and re-layouts: 23.1 us -> 3.6 us
  Pallas kernels: 0 us -> 15.4 us
  between operations: 13.5 us -> 0.17 us
  matrix products: 12.2 us -> 1.12 us
  starting transfers between devices: 23.3 us -> 14 us
    all_to_all x2 -> x3, blocking collectives: 260 us -> 128 us  [the longest x1 84.6 us: shards(): lax.all_to_all(packed.reshape(owners, capacity, half), 'expert', split_ax...]
    all_to_all x1, waiting for transfers between devices: 58.5 us -> 37.9 us  [shards(): lax.all_to_all(both, 'expert', split_axis=0, concat_axis=0, tiled=True)]
    all_to_all x1, starting transfers between devices: 23.3 us -> 5.66 us  [shards(): lax.all_to_all(both, 'expert', split_axis=0, concat_axis=0, tiled=True)]
    pallas_call x0 -> x4, Pallas kernels: none -> 15.4 us  [the longest x2 8.73 us: hidden_of(): pl.pallas_call(hidden_kernel, out_shape=jax.ShapeDtypeStruct((rows, units...]
    ppermute x0 -> x4, waiting for transfers between devices: none -> 13.8 us  [the longest x1 5.47 us: shards(): taken = lax.ppermute(give, 'expert', swap_pair)]
    all_gather x1 -> x0, waiting for transfers between devices: 12.8 us -> none  [shards(): lax.all_gather(arrived, 'sub', axis=1, tiled=True).reshape(-1, features)]
    dot_general x4 -> x2, matrix products: 12.2 us -> 1.12 us  [the longest x1 0.87 us: shards(): jnp.einsum('tes,epsf->tpf', combine, back, precision=lax.Precision.HIGHES...]
    ppermute x0 -> x4, starting transfers between devices: none -> 8.33 us  [the longest x1 2.24 us: shards(): taken = lax.ppermute(give, 'expert', swap_pair)]
  transfers between devices with their start and end apart: 2 -> 5, of which waited for: 2 -> 4; matrix products, arithmetic and copies ran while one was open for 0% -> 0% of each run, Pallas kernels for 0% -> 2%
where the time goes in v1:
time: 215 us
  blocking collectives  128 us (60%)
  waiting for transfers between devices  51.7 us (24%)
  Pallas kernels  15.4 us (7%)
  starting transfers between devices  14 us (7%)
  local copies, waits for them, and re-layouts  3.6 us (2%)
    all_to_all x1, blocking collectives, shards(): lax.all_to_all(packed.reshape(owners, capacity, half), 'expert', split_ax...  84.6 us
    all_to_all x1, waiting for transfers between devices, shards(): lax.all_to_all(both, 'expert', split_axis=0, concat_axis=0, tiled=True)  37.9 us
    all_to_all x1, blocking collectives, shards(): lax.all_to_all(part, 'tensor', split_axis=0, concat_axis=0, tiled=True)  23 us
    all_to_all x1, blocking collectives, shards(): lax.all_to_all(jnp.broadcast_to(quarter[None], (parts, slots, block)), 't...  20.1 us
    pallas_call x2, Pallas kernels, hidden_of(): pl.pallas_call(hidden_kernel, out_shape=jax.ShapeDtypeStruct((rows, units...  8.73 us
    pallas_call x2, Pallas kernels, down_of(): pl.pallas_call(down_kernel if other is None else down_add_kernel, out_sha...  6.63 us
    all_to_all x1, starting transfers between devices, shards(): lax.all_to_all(both, 'expert', split_axis=0, concat_axis=0, tiled=True)  5.66 us
    ppermute x1, waiting for transfers between devices, shards(): taken = lax.ppermute(give, 'expert', swap_pair)  5.47 us
  transfers between devices with their start and end apart: 5, of which 4 were waited for; matrix products, arithmetic and copies ran while one was open for 0% of the time, Pallas kernels for 2%

profile of v1, /device:TPU:40, one launch (start us, length us, event | category | flops | bytes accessed | tf_op | source)
XLA Modules:
  0.0 214.9 jit_solution(16637919696390042804)
XLA Ops:
  0.0 0.8 fusion.1
  0.8 0.0 copy-done
  0.8 0.1 pad_add_fusion
  0.9 0.2 convolution_bitcast_fusion.1
  1.2 0.1 copy.18
  1.3 84.6 %all_to_all.20 = bf16[32,3,896]{2,1,0:T(4,128)(2,1)S(1)} all-to-all(bf16[32,3,896]{2,1,0:T(4,128)(2,1)S(1)} %bitcast.34), channel_id=1, replica_groups=mesh['group'=2,'expert'=32,'tensor'=4,'sub'=2] {'expert'}, dimensions={0} | all-to-all | bytes 344064 | tf_op jit(solution)/shard_map/all_to_all | solution.py:108
  85.9 0.1 reshape.27
  86.1 2.1 collective-permute-start
  88.2 5.2 %collective-permute-done = bf16[96,896]{1,0:T(8,128)(2,1)S(1)} collective-permute-done((bf16[96,896]{1,0:T(8,128)(2,1)S(1)}, bf16[96,896]{1,0:T(8,128)(2,1)S(1)}, u32[]{:S(2)}, u32[]{:S(2)}) %collective-permute-start) | collective-permute-done | bytes 172064 | tf_op jit(solution)/shard_map/ppermute | solution.py:113
  93.5 0.1 broadcast_in_dim.41
  93.6 20.1 %all_to_all.21.x_ref = bf16[4,96,1792]{2,1,0:T(8,128)(2,1)S(1)} all-to-all(bf16[4,96,1792]{2,1,0:T(8,128)(2,1)S(1)} %broadcast_in_dim.41), channel_id=1, replica_groups=mesh['group'=2,'expert'=32,'tensor'=4,'sub'=2] {'tensor'}, dimensions={0} | all-to-all | bytes 2752512 | tf_op jit(solution)/shard_map/all_to_all | solution.py:117
  113.6 1.9 collective-permute-start.1
  115.6 3.1 %collective-permute-done.1.x_ref = bf16[4,96,1792]{2,1,0:T(8,128)(2,1)S(1)} collective-permute-done((bf16[4,96,1792]{2,1,0:T(8,128)(2,1)S(1)}, bf16[4,96,1792]{2,1,0:T(8,128)(2,1)S(1)}, u32[]{:S(2)}, u32[]{:S(2)}) %collective-permute-start.1) | collective-permute-done | bytes 1376288 | tf_op jit(solution)/shard_map/ppermute | solution.py:124
  118.7 1.1 copy-done.3
  119.7 4.4 %hidden.3.h_ref = bf16[96,128]{1,0:T(8,128)(2,1)} custom-call(bf16[4,96,1792]{2,1,0:T(8,128)(2,1)} %copy-done.3, bf16[128,7168]{1,0:T(8,128)(2,1)} %bitcast.29, bf16[128,7168]{1,0:T(8,128)(2,1)} %bitcast.31), custom_call_target="tpu_custom_call" | custom-call | flops 352321536 | bytes 5046272 | tf_op jit(solution)/shard_map/hidden/pallas_call | solution.py:31
  124.1 3.1 %down.1 = bf16[4,96,1792]{2,1,0:T(8,128)(2,1)} custom-call(bf16[96,128]{1,0:T(8,128)(2,1)} %hidden.3.h_ref, bf16[128,7168]{1,0:T(8,128)(2,1)} %bitcast.27), custom_call_target="tpu_custom_call" | custom-call | flops 176160768 | bytes 3211264 | tf_op jit(solution)/shard_map/down/pallas_call | solution.py:66
  127.2 2.1 collective-permute-start.2
  129.3 4.4 %hidden.2.h_ref = bf16[96,128]{1,0:T(8,128)(2,1)} custom-call(bf16[4,96,1792]{2,1,0:T(8,128)(2,1)} %copy-done.1, bf16[128,7168]{1,0:T(8,128)(2,1)} %bitcast.30, bf16[128,7168]{1,0:T(8,128)(2,1)} %bitcast.32), custom_call_target="tpu_custom_call" | custom-call | flops 352321536 | bytes 5046272 | tf_op jit(solution)/shard_map/hidden/pallas_call | solution.py:31
  133.7 1.1 copy-done.2
  134.8 3.5 %down_add.1 = bf16[4,96,1792]{2,1,0:T(8,128)(2,1)} custom-call(bf16[96,128]{1,0:T(8,128)(2,1)} %hidden.2.h_ref, bf16[128,7168]{1,0:T(8,128)(2,1)} %bitcast.28, bf16[4,96,1792]{2,1,0:T(8,128)(2,1)} %copy-done.2), custom_call_target="tpu_custom_call" | custom-call | flops 176160768 | bytes 3211264 | tf_op jit(solution)/shard_map/down_add/pallas_call | solution.py:66
  138.3 23.0 %all_to_all.22 = bf16[4,96,1792]{2,1,0:T(8,128)(2,1)S(1)} all-to-all(bf16[4,96,1792]{2,1,0:T(8,128)(2,1)} %down_add.1), channel_id=1, replica_groups=mesh['group'=2,'expert'=32,'tensor'=4,'sub'=2] {'tensor'}, dimensions={0} | all-to-all | bytes 2752512 | tf_op jit(solution)/shard_map/all_to_all | solution.py:130
  161.2 0.2 convert_reduce_fusion
  161.5 2.2 %collective-permute-start.3 = (bf16[96,896]{1,0:T(8,128)(2,1)S(1)}, bf16[96,896]{1,0:T(8,128)(2,1)S(1)}, u32[]{:S(2)}, u32[]{:S(2)}) collective-permute-start(bf16[96,896]{1,0:T(8,128)(2,1)S(1)} %select_convert_fusion), channel_id=1, source_target_pairs={{0,8},{8,0},{16,24},{24,16},{32,40},{40,32},{48,56},{56,48},{64,72... | collective-permute-start | bytes 516104 | tf_op jit(solution)/shard_map/ppermute | solution.py:134
  163.8 5.5 %collective-permute-done.3 = bf16[96,896]{1,0:T(8,128)(2,1)S(1)} collective-permute-done((bf16[96,896]{1,0:T(8,128)(2,1)S(1)}, bf16[96,896]{1,0:T(8,128)(2,1)S(1)}, u32[]{:S(2)}, u32[]{:S(2)}) %collective-permute-start.3) | collective-permute-done | bytes 172064 | tf_op jit(solution)/shard_map/ppermute | solution.py:134
  169.2 0.1 add_convert_fusion
  169.3 0.8 reshape.28
  170.1 5.7 %all-to-all-start.3 = ((bf16[32,3,896]{2,1,0:T(4,128)(2,1)}), bf16[32,3,896]{2,1,0:T(4,128)(2,1)S(1)}, u32[]{:S(2)}, u32[]{:S(2)}) async-start(bf16[32,3,896]{2,1,0:T(4,128)(2,1)} %reshape.28), calls=%async_computation.3 | async-start | bytes 458752 | tf_op jit(solution)/shard_map/all_to_all | solution.py:136
  175.8 0.1 select_reduce_fusion
  175.9 37.9 %all-to-all-done.3 = bf16[32,3,896]{2,1,0:T(4,128)(2,1)S(1)} async-done(((bf16[32,3,896]{2,1,0:T(4,128)(2,1)}), bf16[32,3,896]{2,1,0:T(4,128)(2,1)S(1)}, u32[]{:S(2)}, u32[]{:S(2)}) %all-to-all-start.3) | async-done | bytes 172064 | tf_op jit(solution)/shard_map/all_to_all | solution.py:136
  213.7 0.1 copy.21
  213.9 0.1 dot_general.12
  214.0 0.9 fusion
  (18 shorter events, 0.2 us)
Async XLA Ops:
  0.0 0.8 copy-start
  86.1 7.3 %collective-permute-start = (bf16[96,896]{1,0:T(8,128)(2,1)S(1)}, bf16[96,896]{1,0:T(8,128)(2,1)S(1)}, u32[]{:S(2)}, u32[]{:S(2)}) collective-permute-start(bf16[96,896]{1,0:T(8,128)(2,1)S(1)} %reshape.27), channel_id=1, source_target_pairs={{0,8},{8,0},{16,24},{24,16},{32,40},{40,32},{48,56},{56,48},{64,72... | collective-permute-start | bytes 516104 | tf_op jit(solution)/shard_map/ppermute | solution.py:113
  113.6 10.5 %copy-start.1 = (bf16[4,96,1792]{2,1,0:T(8,128)(2,1)}, bf16[4,96,1792]{2,1,0:T(8,128)(2,1)S(1)}, u32[]{:S(2)}) copy-start(bf16[4,96,1792]{2,1,0:T(8,128)(2,1)S(1)} %all_to_all.21.x_ref) | copy-start | bytes 4128772
  113.6 5.0 %collective-permute-start.1 = (bf16[4,96,1792]{2,1,0:T(8,128)(2,1)S(1)}, bf16[4,96,1792]{2,1,0:T(8,128)(2,1)S(1)}, u32[]{:S(2)}, u32[]{:S(2)}) collective-permute-start(bf16[4,96,1792]{2,1,0:T(8,128)(2,1)S(1)} %all_to_all.21.x_ref), channel_id=1, source_target_pairs={{0,1},{1,0},{2,3},{3,2},{4,5},{5,4},{6,7},{7,6},{8,9},{9,8},{10,11... | collective-permute-start | bytes 4128776 | tf_op jit(solution)/shard_map/ppermute | solution.py:124
  118.7 1.1 copy-start.3
  127.2 6.4 %collective-permute-start.2 = (bf16[4,96,1792]{2,1,0:T(8,128)(2,1)}, bf16[4,96,1792]{2,1,0:T(8,128)(2,1)S(1)}, u32[]{:S(2)}, u32[]{:S(2)}) collective-permute-start(bf16[4,96,1792]{2,1,0:T(8,128)(2,1)} %down.1), channel_id=1, source_target_pairs={{0,1},{1,0},{2,3},{3,2},{4,5},{5,4},{6,7},{7,6},{8,9},{9,8},{10,11... | collective-permute-start | bytes 4128776 | tf_op jit(solution)/shard_map/ppermute | solution.py:128
  133.7 1.1 copy-start.2
  161.5 14.3 %copy-start.5 = (s32[4,8]{1,0:T(4,128)S(1)}, s32[4,8]{1,0:T(4,128)}, u32[]{:S(2)}) copy-start(s32[4,8]{1,0:T(4,128)} %param.8) | copy-start | bytes 388
  161.5 14.3 %copy-start.4 = (s32[4,8]{1,0:T(4,128)S(1)}, s32[4,8]{1,0:T(4,128)}, u32[]{:S(2)}) copy-start(s32[4,8]{1,0:T(4,128)} %param.7) | copy-start | bytes 388
  161.5 7.7 %collective-permute-start.3 = (bf16[96,896]{1,0:T(8,128)(2,1)S(1)}, bf16[96,896]{1,0:T(8,128)(2,1)S(1)}, u32[]{:S(2)}, u32[]{:S(2)}) collective-permute-start(bf16[96,896]{1,0:T(8,128)(2,1)S(1)} %select_convert_fusion), channel_id=1, source_target_pairs={{0,8},{8,0},{16,24},{24,16},{32,40},{40,32},{48,56},{56,48},{64,72... | collective-permute-start | bytes 516104 | tf_op jit(solution)/shard_map/ppermute | solution.py:134
  170.1 43.7 %all-to-all-start.3 = ((bf16[32,3,896]{2,1,0:T(4,128)(2,1)}), bf16[32,3,896]{2,1,0:T(4,128)(2,1)S(1)}, u32[]{:S(2)}, u32[]{:S(2)}) async-start(bf16[32,3,896]{2,1,0:T(4,128)(2,1)} %reshape.28), calls=%async_computation.3 | async-start | bytes 458752 | tf_op jit(solution)/shard_map/all_to_all | solution.py:136

commit v2 on v1

v2 whole, which is shorter than its diff:
```python
import jax
import jax.numpy as jnp
from jax import lax
from jax.experimental import pallas as pl
from jax.experimental.pallas import tpu as pltpu
from jax.sharding import PartitionSpec as P

BF = jnp.bfloat16
F32 = jnp.float32
VM = pl.BlockSpec(memory_space=pltpu.VMEM)
SM = pl.BlockSpec(memory_space=pltpu.SMEM)
CONTRACT = (((1,), (1,)), ((), ()))


def expert_kernel(odd_ref, x0_ref, x1_ref, g0, u0, d0, g1, u1, d1, keep_ref, give_ref):
    parts, rows, half = x0_ref.shape
    odd = odd_ref[0]

    def cols(k, other):
        which = 1 - odd if other else odd
        return pl.ds(pl.multiple_of((2 * k + which) * half, 128), half)

    hidden = []
    for g, u in ((g0, u0), (g1, u1)):
        gate = jnp.zeros((rows, g.shape[0]), F32)
        up = jnp.zeros((rows, u.shape[0]), F32)
        for k in range(parts):
            for other, x_ref in ((False, x0_ref), (True, x1_ref)):
                x = x_ref[k]
                at = cols(k, other)
                gate += lax.dot_general(x, g[:, at], CONTRACT, preferred_element_type=F32)
                up += lax.dot_general(x, u[:, at], CONTRACT, preferred_element_type=F32)
        hidden.append((gate / (1.0 + jnp.exp(-gate)) * up).astype(BF))
    for other, o_ref in ((True, give_ref), (False, keep_ref)):
        for k in range(parts):
            at = cols(k, other)
            total = jnp.dot(hidden[0], d0[:, at], preferred_element_type=F32)
            total += jnp.dot(hidden[1], d1[:, at], preferred_element_type=F32)
            o_ref[k] = total.astype(BF)


def experts_of(odd, x0, x1, own, other):
    parts, rows, half = x0.shape
    units, features = own[0].shape
    shape = jax.ShapeDtypeStruct((parts, rows, half), BF)
    return pl.pallas_call(
        expert_kernel,
        out_shape=(shape, shape),
        in_specs=[SM] + [VM] * 8,
        out_specs=(VM, VM),
        cost_estimate=pl.CostEstimate(
            flops=12 * rows * units * features,
            bytes_accessed=12 * units * features + 4 * rows * features,
            transcendentals=2 * rows * units,
        ),
        compiler_params=pltpu.CompilerParams(vmem_limit_bytes=24 * 1024 * 1024),
        name="experts",
    )(odd, x0, x1, *own, *other)


def shards(tokens, expert_ids, gate_codes, w_gate, w_up, w_down):
    rows, features = tokens.shape
    per_token = expert_ids.shape[1]
    owners = lax.axis_size("expert")
    subs = lax.axis_size("sub")
    parts = lax.axis_size("tensor")
    experts = owners // 2
    capacity = min(rows, rows * per_token // experts + 1)
    slots = owners * capacity
    block = features // parts
    half = block // 2
    here = lax.axis_index("tensor")
    odd = lax.axis_index("expert") & 1
    swap_sub = [(i, subs - 1 - i) for i in range(subs)]
    swap_pair = [(i, i ^ 1) for i in range(owners)]

    own = (w_gate[0], w_up[0], w_down[0])
    other = [lax.ppermute(w, "sub", swap_sub) for w in own]

    picks = expert_ids[:, :, None] == jnp.arange(experts, dtype=jnp.int32)
    named = jnp.any(picks, axis=1)
    weight = jnp.sum(jnp.where(picks, gate_codes[:, :, None].astype(F32) / 64.0, 0.0), axis=1)
    count = named.astype(jnp.int32)
    slot = [jnp.zeros((experts,), jnp.int32)]
    for t in range(1, rows):
        slot.append(slot[-1] + count[t - 1])
    slot = jnp.stack(slot)
    onehot = named[:, :, None] & (slot[:, :, None] == jnp.arange(capacity, dtype=jnp.int32))
    combine = jnp.where(onehot, weight[:, :, None], 0.0)

    mine = lax.dynamic_slice(tokens, (0, here * block), (rows, block))
    packed = jnp.einsum("tes,tpf->epsf", onehot.astype(BF), mine.reshape(rows, 2, half)).astype(BF)
    arrived = lax.all_to_all(
        packed.reshape(owners, capacity, half), "expert", split_axis=0, concat_axis=0, tiled=True
    )
    arrived = arrived.reshape(slots, half)
    partner = lax.ppermute(arrived, "expert", swap_pair)

    def across(x):
        return lax.all_to_all(x, "tensor", split_axis=0, concat_axis=0, tiled=True)

    x0 = across(jnp.broadcast_to(arrived[None], (parts, slots, half)))
    x1 = across(jnp.broadcast_to(partner[None], (parts, slots, half)))
    keep, give = experts_of(odd.reshape(1), x0, x1, own, other)
    give = jnp.sum(across(give).astype(F32), axis=0).astype(BF)
    taken = lax.ppermute(give, "expert", swap_pair)
    keep = jnp.sum(across(keep).astype(F32), axis=0)
    both = (keep + taken.astype(F32)).astype(BF).reshape(owners, capacity, half)
    back = lax.all_to_all(both, "expert", split_axis=0, concat_axis=0, tiled=True)
    back = back.reshape(experts, 2, capacity, half).astype(F32)
    mixed = jnp.einsum(
        "tes,epsf->tpf", combine, back, precision=lax.Precision.HIGHEST, preferred_element_type=F32
    )
    return mixed.reshape(rows, block).astype(BF)


def solution(mesh):
    spread = P(("group", "expert", "sub"), None)
    weights = P("expert", ("tensor", "sub"), None)
    return jax.shard_map(
        shards,
        mesh=mesh,
        in_specs=(spread, spread, spread, weights, weights, weights),
        out_specs=P(("group", "expert", "sub"), "tensor"),
        check_vma=False,
    )
```

time: 215 us -> 192 us (0.89)
  blocking collectives: 128 us -> 11.4 us
  starting transfers between devices: 14 us -> 74.5 us
  waiting for transfers between devices: 51.7 us -> 89.8 us
  Pallas kernels: 15.4 us -> 6.23 us
  local copies, waits for them, and re-layouts: 3.6 us -> 6.87 us
    all_to_all x3 -> x1, blocking collectives: 128 us -> 11.4 us  [across(): return lax.all_to_all(x, 'tensor', split_axis=0, concat_axis=0, tiled=True)]
    all_to_all x0 -> x4, starting transfers between devices: none -> 57.6 us  [the longest x1 45.8 us: shards(): lax.all_to_all(packed.reshape(owners, capacity, half), 'expert', split_ax...]
    all_to_all x0 -> x4, waiting for transfers between devices: none -> 50.2 us  [the longest x1 32.7 us: shards(): lax.all_to_all(packed.reshape(owners, capacity, half), 'expert', split_ax...]
    pallas_call x4 -> x1, Pallas kernels: 15.4 us -> 6.23 us  [experts_of(): pl.pallas_call(expert_kernel, out_shape=(shape, shape), in_specs=[SM] + [...]
    ppermute x1, waiting for transfers between devices: 5.47 us -> 0.01 us  [shards(): taken = lax.ppermute(give, 'expert', swap_pair)]
    all_to_all x1, waiting for transfers between devices: 37.9 us -> 34.4 us  [shards(): lax.all_to_all(both, 'expert', split_axis=0, concat_axis=0, tiled=True)]
    ppermute x2 -> x3, waiting for transfers between devices: 3.1 us -> 0.01 us  [shards(): other = [lax.ppermute(w, 'sub', swap_sub) for w in own]]
    ppermute x2 -> x3, starting transfers between devices: 4 us -> 6.35 us  [shards(): other = [lax.ppermute(w, 'sub', swap_sub) for w in own]]
  transfers between devices with their start and end apart: 5 -> 10, of which waited for: 4 -> 6; matrix products, arithmetic and copies ran while one was open for 0% -> 1% of each run, Pallas kernels for 2% -> 0%
where the time goes in v2:
time: 192 us; the launch traced here: 191 us
  waiting for transfers between devices  89.8 us (47%)
  starting transfers between devices  74.5 us (39%)
  blocking collectives  11.4 us (6%)
  local copies, waits for them, and re-layouts  6.87 us (4%)
  Pallas kernels  6.23 us (3%)
    all_to_all x1, starting transfers between devices, shards(): lax.all_to_all(packed.reshape(owners, capacity, half), 'expert', split_ax...  45.8 us
    all_to_all x1, waiting for transfers between devices, shards(): lax.all_to_all(both, 'expert', split_axis=0, concat_axis=0, tiled=True)  34.4 us
    all_to_all x1, waiting for transfers between devices, shards(): lax.all_to_all(packed.reshape(owners, capacity, half), 'expert', split_ax...  32.7 us
    all_to_all x3, waiting for transfers between devices, across(): return lax.all_to_all(x, 'tensor', split_axis=0, concat_axis=0, tiled=True)  17.5 us
    all_to_all x3, starting transfers between devices, across(): return lax.all_to_all(x, 'tensor', split_axis=0, concat_axis=0, tiled=True)  11.9 us
    all_to_all x1, blocking collectives, across(): return lax.all_to_all(x, 'tensor', split_axis=0, concat_axis=0, tiled=True)  11.4 us
    ppermute x3, starting transfers between devices, shards(): other = [lax.ppermute(w, 'sub', swap_sub) for w in own]  6.35 us
    pallas_call x1, Pallas kernels, experts_of(): pl.pallas_call(expert_kernel, out_shape=(shape, shape), in_specs=[SM] + [...  6.23 us
  transfers between devices with their start and end apart: 10, of which 6 were waited for; matrix products, arithmetic and copies ran while one was open for 1% of the time, Pallas kernels for 0%

profile of v2, /device:TPU:40, one launch (start us, length us, event | category | flops | bytes accessed | tf_op | source)
XLA Modules:
  0.0 191.3 jit_solution(6852384649557680729)
XLA Ops:
  0.0 0.8 fusion.1
  0.9 0.3 convolution_bitcast_fusion.1
  1.2 0.8 copy.17
  2.0 45.8 %all-to-all-start = ((bf16[32,3,896]{2,1,0:T(4,128)(2,1)}), bf16[32,3,896]{2,1,0:T(4,128)(2,1)S(1)}, u32[]{:S(2)}, u32[]{:S(2)}) async-start(bf16[32,3,896]{2,1,0:T(4,128)(2,1)} %bitcast.6), calls=%async_computation | async-start | bytes 458752 | tf_op jit(solution)/shard_map/all_to_all | solution.py:93
  47.7 2.0 %collective-permute-start.1 = (bf16[128,7168]{1,0:T(8,128)(2,1)}, bf16[128,7168]{1,0:T(8,128)(2,1)}, u32[]{:S(2)}, u32[]{:S(2)}) collective-permute-start(bf16[128,7168]{1,0:T(8,128)(2,1)} %bitcast.28), channel_id=1, source_target_pairs={{0,1},{1,0},{2,3},{3,2},{4,5},{5,4},{6,7},{7,6},{8,9},{9,8},{10,11... | collective-permute-start | bytes 5505032 | tf_op jit(solution)/shard_map/ppermute | solution.py:78
  49.7 2.4 %collective-permute-start.2 = (bf16[128,7168]{1,0:T(8,128)(2,1)}, bf16[128,7168]{1,0:T(8,128)(2,1)}, u32[]{:S(2)}, u32[]{:S(2)}) collective-permute-start(bf16[128,7168]{1,0:T(8,128)(2,1)} %bitcast.30), channel_id=1, source_target_pairs={{0,1},{1,0},{2,3},{3,2},{4,5},{5,4},{6,7},{7,6},{8,9},{9,8},{10,11... | collective-permute-start | bytes 5505032 | tf_op jit(solution)/shard_map/ppermute | solution.py:78
  52.2 2.0 %collective-permute-start.3 = (bf16[128,7168]{1,0:T(8,128)(2,1)}, bf16[128,7168]{1,0:T(8,128)(2,1)}, u32[]{:S(2)}, u32[]{:S(2)}) collective-permute-start(bf16[128,7168]{1,0:T(8,128)(2,1)} %bitcast.32), channel_id=1, source_target_pairs={{0,1},{1,0},{2,3},{3,2},{4,5},{5,4},{6,7},{7,6},{8,9},{9,8},{10,11... | collective-permute-start | bytes 5505032 | tf_op jit(solution)/shard_map/ppermute | solution.py:78
  54.1 32.7 %all-to-all-done = bf16[32,3,896]{2,1,0:T(4,128)(2,1)S(1)} async-done(((bf16[32,3,896]{2,1,0:T(4,128)(2,1)}), bf16[32,3,896]{2,1,0:T(4,128)(2,1)S(1)}, u32[]{:S(2)}, u32[]{:S(2)}) %all-to-all-start) | async-done | bytes 172064 | tf_op jit(solution)/shard_map/all_to_all | solution.py:93
  86.8 0.1 broadcast_in_dim.48
  87.0 0.9 broadcast_in_dim.49
  87.9 4.7 %all-to-all-start.1 = ((bf16[4,96,896]{2,1,0:T(8,128)(2,1)}), bf16[4,96,896]{2,1,0:T(8,128)(2,1)S(1)}, u32[]{:S(2)}, u32[]{:S(2)}) async-start(bf16[4,96,896]{2,1,0:T(8,128)(2,1)} %broadcast_in_dim.49), calls=%async_computation.1 | async-start | bytes 1376256 | tf_op jit(solution)/shard_map/all_to_all | solution.py:100
  92.6 2.1 %collective-permute-start = (bf16[96,896]{1,0:T(8,128)(2,1)S(1)}, bf16[96,896]{1,0:T(8,128)(2,1)S(1)}, u32[]{:S(2)}, u32[]{:S(2)}) collective-permute-start(bf16[96,896]{1,0:T(8,128)(2,1)S(1)} %broadcast_in_dim.48), channel_id=1, source_target_pairs={{0,8},{8,0},{16,24},{24,16},{32,40},{40,32},{48,56},{56,48},{64,72... | collective-permute-start | bytes 516104 | tf_op jit(solution)/shard_map/ppermute | solution.py:97
  94.7 5.2 %collective-permute-done = bf16[96,896]{1,0:T(8,128)(2,1)S(1)} collective-permute-done((bf16[96,896]{1,0:T(8,128)(2,1)S(1)}, bf16[96,896]{1,0:T(8,128)(2,1)S(1)}, u32[]{:S(2)}, u32[]{:S(2)}) %collective-permute-start) | collective-permute-done | bytes 172064 | tf_op jit(solution)/shard_map/ppermute | solution.py:97
  99.9 2.1 %all-to-all-done.1.x0_ref = bf16[4,96,896]{2,1,0:T(8,128)(2,1)S(1)} async-done(((bf16[4,96,896]{2,1,0:T(8,128)(2,1)}), bf16[4,96,896]{2,1,0:T(8,128)(2,1)S(1)}, u32[]{:S(2)}, u32[]{:S(2)}) %all-to-all-start.1) | async-done | bytes 688160 | tf_op jit(solution)/shard_map/all_to_all | solution.py:100
  102.0 0.9 broadcast_in_dim.50
  102.9 3.6 %all-to-all-start.2 = ((bf16[4,96,896]{2,1,0:T(8,128)(2,1)}), bf16[4,96,896]{2,1,0:T(8,128)(2,1)S(1)}, u32[]{:S(2)}, u32[]{:S(2)}) async-start(bf16[4,96,896]{2,1,0:T(8,128)(2,1)} %broadcast_in_dim.50), calls=%async_computation.2 | async-start | bytes 1376256 | tf_op jit(solution)/shard_map/all_to_all | solution.py:100
  106.6 8.8 %all-to-all-done.2.x1_ref = bf16[4,96,896]{2,1,0:T(8,128)(2,1)S(1)} async-done(((bf16[4,96,896]{2,1,0:T(8,128)(2,1)}), bf16[4,96,896]{2,1,0:T(8,128)(2,1)S(1)}, u32[]{:S(2)}, u32[]{:S(2)}) %all-to-all-start.2) | async-done | bytes 688160 | tf_op jit(solution)/shard_map/all_to_all | solution.py:100
  115.4 1.5 copy-done.2
  116.9 1.5 copy-done.3
  118.4 6.2 %experts.1 = (bf16[4,96,896]{2,1,0:T(8,128)(2,1)S(1)}, bf16[4,96,896]{2,1,0:T(8,128)(2,1)S(1)}) custom-call(s32[1]{0:T(128)} %bitcast.odd_ref, bf16[4,96,896]{2,1,0:T(8,128)(2,1)S(1)} %all-to-all-done.1.x0_ref, bf16[4,96,896]{2,1,0:T(8,128)(2,1)S(1)} %all-to-all-done.2.x1_ref, bf16[128,7168]{1,0:T(8,128)(2,1)S(1)} %bitcast.29, ...), custom_call_target="tpu_custom_call" | custom-call | flops 1056964608 | bytes 13762560 | tf_op jit(solution)/shard_map/experts/pallas_call | solution.py:46
  124.7 11.4 %all_to_all.30 = bf16[4,96,896]{2,1,0:T(8,128)(2,1)S(1)} all-to-all(bf16[4,96,896]{2,1,0:T(8,128)(2,1)S(1)} %get-tuple-element.8), channel_id=1, replica_groups=mesh['group'=2,'expert'=32,'tensor'=4,'sub'=2] {'tensor'}, dimensions={0} | all-to-all | bytes 1376256 | tf_op jit(solution)/shard_map/all_to_all | solution.py:100
  136.0 3.6 %all-to-all-start.3 = ((bf16[4,96,896]{2,1,0:T(8,128)(2,1)}), bf16[4,96,896]{2,1,0:T(8,128)(2,1)S(1)}, u32[]{:S(2)}, u32[]{:S(2)}) async-start(bf16[4,96,896]{2,1,0:T(8,128)(2,1)} %copy-done.4), calls=%async_computation.3 | async-start | bytes 1376256 | tf_op jit(solution)/shard_map/all_to_all | solution.py:100
  139.6 0.1 reduce_sum.32
  139.7 2.2 %collective-permute-start.4 = (bf16[96,896]{1,0:T(8,128)(2,1)S(1)}, bf16[96,896]{1,0:T(8,128)(2,1)S(1)}, u32[]{:S(2)}, u32[]{:S(2)}) collective-permute-start(bf16[96,896]{1,0:T(8,128)(2,1)S(1)} %reduce_sum.32), channel_id=1, source_target_pairs={{0,8},{8,0},{16,24},{24,16},{32,40},{40,32},{48,56},{56,48},{64,72... | collective-permute-start | bytes 516104 | tf_op jit(solution)/shard_map/ppermute | solution.py:106
  142.0 6.5 %all-to-all-done.3 = bf16[4,96,896]{2,1,0:T(8,128)(2,1)S(1)} async-done(((bf16[4,96,896]{2,1,0:T(8,128)(2,1)}), bf16[4,96,896]{2,1,0:T(8,128)(2,1)S(1)}, u32[]{:S(2)}, u32[]{:S(2)}) %all-to-all-start.3) | async-done | bytes 688160 | tf_op jit(solution)/shard_map/all_to_all | solution.py:100
  148.6 0.8 reshape.30
  149.4 6.2 %all-to-all-start.5 = ((bf16[32,3,896]{2,1,0:T(4,128)(2,1)}), bf16[32,3,896]{2,1,0:T(4,128)(2,1)S(1)}, u32[]{:S(2)}, u32[]{:S(2)}) async-start(bf16[32,3,896]{2,1,0:T(4,128)(2,1)} %reshape.30), calls=%async_computation.5 | async-start | bytes 458752 | tf_op jit(solution)/shard_map/all_to_all | solution.py:109
  155.6 0.1 select_reduce_fusion
  155.7 34.4 %all-to-all-done.5 = bf16[32,3,896]{2,1,0:T(4,128)(2,1)S(1)} async-done(((bf16[32,3,896]{2,1,0:T(4,128)(2,1)}), bf16[32,3,896]{2,1,0:T(4,128)(2,1)S(1)}, u32[]{:S(2)}, u32[]{:S(2)}) %all-to-all-start.5) | async-done | bytes 172064 | tf_op jit(solution)/shard_map/all_to_all | solution.py:109
  190.2 0.1 copy.20
  190.3 0.1 dot_general.12
  190.4 0.9 fusion
  (24 shorter events, 0.3 us)
Async XLA Ops:
  0.0 0.8 copy-start
  2.0 84.8 %all-to-all-start = ((bf16[32,3,896]{2,1,0:T(4,128)(2,1)}), bf16[32,3,896]{2,1,0:T(4,128)(2,1)S(1)}, u32[]{:S(2)}, u32[]{:S(2)}) async-start(bf16[32,3,896]{2,1,0:T(4,128)(2,1)} %bitcast.6), calls=%async_computation | async-start | bytes 458752 | tf_op jit(solution)/shard_map/all_to_all | solution.py:93
  47.7 58.8 %collective-permute-start.1 = (bf16[128,7168]{1,0:T(8,128)(2,1)}, bf16[128,7168]{1,0:T(8,128)(2,1)}, u32[]{:S(2)}, u32[]{:S(2)}) collective-permute-start(bf16[128,7168]{1,0:T(8,128)(2,1)} %bitcast.28), channel_id=1, source_target_pairs={{0,1},{1,0},{2,3},{3,2},{4,5},{5,4},{6,7},{7,6},{8,9},{9,8},{10,11... | collective-permute-start | bytes 5505032 | tf_op jit(solution)/shard_map/ppermute | solution.py:78
  49.7 56.8 %collective-permute-start.2 = (bf16[128,7168]{1,0:T(8,128)(2,1)}, bf16[128,7168]{1,0:T(8,128)(2,1)}, u32[]{:S(2)}, u32[]{:S(2)}) collective-permute-start(bf16[128,7168]{1,0:T(8,128)(2,1)} %bitcast.30), channel_id=1, source_target_pairs={{0,1},{1,0},{2,3},{3,2},{4,5},{5,4},{6,7},{7,6},{8,9},{9,8},{10,11... | collective-permute-start | bytes 5505032 | tf_op jit(solution)/shard_map/ppermute | solution.py:78
  52.2 54.4 %collective-permute-start.3 = (bf16[128,7168]{1,0:T(8,128)(2,1)}, bf16[128,7168]{1,0:T(8,128)(2,1)}, u32[]{:S(2)}, u32[]{:S(2)}) collective-permute-start(bf16[128,7168]{1,0:T(8,128)(2,1)} %bitcast.32), channel_id=1, source_target_pairs={{0,1},{1,0},{2,3},{3,2},{4,5},{5,4},{6,7},{7,6},{8,9},{9,8},{10,11... | collective-permute-start | bytes 5505032 | tf_op jit(solution)/shard_map/ppermute | solution.py:78
  87.9 27.5 %copy-start.1 = (bf16[1,128,7168]{2,1,0:T(8,128)(2,1)S(1)}, bf16[1,128,7168]{2,1,0:T(8,128)(2,1)}, u32[]{:S(2)}) copy-start(bf16[1,128,7168]{2,1,0:T(8,128)(2,1)} %param.9) | copy-start | bytes 5505028
  87.9 14.2 %all-to-all-start.1 = ((bf16[4,96,896]{2,1,0:T(8,128)(2,1)}), bf16[4,96,896]{2,1,0:T(8,128)(2,1)S(1)}, u32[]{:S(2)}, u32[]{:S(2)}) async-start(bf16[4,96,896]{2,1,0:T(8,128)(2,1)} %broadcast_in_dim.49), calls=%async_computation.1 | async-start | bytes 1376256 | tf_op jit(solution)/shard_map/all_to_all | solution.py:100
  92.6 7.3 %collective-permute-start = (bf16[96,896]{1,0:T(8,128)(2,1)S(1)}, bf16[96,896]{1,0:T(8,128)(2,1)S(1)}, u32[]{:S(2)}, u32[]{:S(2)}) collective-permute-start(bf16[96,896]{1,0:T(8,128)(2,1)S(1)} %broadcast_in_dim.48), channel_id=1, source_target_pairs={{0,8},{8,0},{16,24},{24,16},{32,40},{40,32},{48,56},{56,48},{64,72... | collective-permute-start | bytes 516104 | tf_op jit(solution)/shard_map/ppermute | solution.py:97
  102.9 12.4 %all-to-all-start.2 = ((bf16[4,96,896]{2,1,0:T(8,128)(2,1)}), bf16[4,96,896]{2,1,0:T(8,128)(2,1)S(1)}, u32[]{:S(2)}, u32[]{:S(2)}) async-start(bf16[4,96,896]{2,1,0:T(8,128)(2,1)} %broadcast_in_dim.50), calls=%async_computation.2 | async-start | bytes 1376256 | tf_op jit(solution)/shard_map/all_to_all | solution.py:100
  115.4 1.5 copy-start.2
  116.9 1.5 copy-start.3
  124.6 11.4 %copy-start.4 = (bf16[4,96,896]{2,1,0:T(8,128)(2,1)}, bf16[4,96,896]{2,1,0:T(8,128)(2,1)S(1)}, u32[]{:S(2)}) copy-start(bf16[4,96,896]{2,1,0:T(8,128)(2,1)S(1)} %get-tuple-element.7) | copy-start | bytes 2064388
  136.0 12.4 %all-to-all-start.3 = ((bf16[4,96,896]{2,1,0:T(8,128)(2,1)}), bf16[4,96,896]{2,1,0:T(8,128)(2,1)S(1)}, u32[]{:S(2)}, u32[]{:S(2)}) async-start(bf16[4,96,896]{2,1,0:T(8,128)(2,1)} %copy-done.4), calls=%async_computation.3 | async-start | bytes 1376256 | tf_op jit(solution)/shard_map/all_to_all | solution.py:100
  139.6 16.0 %copy-start.6 = (s32[4,8]{1,0:T(4,128)S(1)}, s32[4,8]{1,0:T(4,128)}, u32[]{:S(2)}) copy-start(s32[4,8]{1,0:T(4,128)} %param.8) | copy-start | bytes 388
  139.6 16.0 %copy-start.5 = (s32[4,8]{1,0:T(4,128)S(1)}, s32[4,8]{1,0:T(4,128)}, u32[]{:S(2)}) copy-start(s32[4,8]{1,0:T(4,128)} %param.7) | copy-start | bytes 388
  139.7 8.8 %collective-permute-start.4 = (bf16[96,896]{1,0:T(8,128)(2,1)S(1)}, bf16[96,896]{1,0:T(8,128)(2,1)S(1)}, u32[]{:S(2)}, u32[]{:S(2)}) collective-permute-start(bf16[96,896]{1,0:T(8,128)(2,1)S(1)} %reduce_sum.32), channel_id=1, source_target_pairs={{0,8},{8,0},{16,24},{24,16},{32,40},{40,32},{48,56},{56,48},{64,72... | collective-permute-start | bytes 516104 | tf_op jit(solution)/shard_map/ppermute | solution.py:106
  149.4 40.7 %all-to-all-start.5 = ((bf16[32,3,896]{2,1,0:T(4,128)(2,1)}), bf16[32,3,896]{2,1,0:T(4,128)(2,1)S(1)}, u32[]{:S(2)}, u32[]{:S(2)}) async-start(bf16[32,3,896]{2,1,0:T(4,128)(2,1)} %reshape.30), calls=%async_computation.5 | async-start | bytes 458752 | tf_op jit(solution)/shard_map/all_to_all | solution.py:109

commit v3 on v2

v3 whole, which is shorter than its diff:
```python
import jax
import jax.numpy as jnp
from jax import lax
from jax.experimental import pallas as pl
from jax.experimental.pallas import tpu as pltpu
from jax.sharding import PartitionSpec as P

BF = jnp.bfloat16
F32 = jnp.float32
I32 = jnp.int32
VM = pl.BlockSpec(memory_space=pltpu.VMEM)
SM = pl.BlockSpec(memory_space=pltpu.SMEM)
ANY = pl.BlockSpec(memory_space=pl.ANY)
CONTRACT = (((1,), (1,)), ((), ()))
MIB = 1024 * 1024


def params(mib):
    return pltpu.CompilerParams(vmem_limit_bytes=mib * MIB)


def split_of(half):
    return -(-half // 256) * 128


def routing(ids_ref, rows):
    row = lax.broadcasted_iota(I32, (rows, 1), 0)
    expert, side, part = row // 4, (row // 2) % 2, row % 2
    tokens, picks = ids_ref.shape
    count = jnp.zeros((rows, 1), I32)
    out = []
    for t in range(tokens):
        hits = [(expert == ids_ref[t, j]).astype(I32) for j in range(picks)]
        named = sum(hits)
        first = named * (count == part).astype(I32)
        third = named * (count == 2).astype(I32)
        out.append((hits, first, third))
        count = count + named
    return out, side, part


def pack_body(block, here_ref, ids_ref, tok_ref, o_ref):
    rows, width = o_ref.shape
    half = block // 2
    low = width - half
    routes, side, part = routing(ids_ref, rows)
    start = pl.multiple_of(here_ref[0] * block, 128)
    tok = tok_ref[:, pl.ds(start, block)].astype(F32)
    main = jnp.zeros((rows, half), F32)
    tail = jnp.zeros((rows, low), F32)
    for t, (_, first, third) in enumerate(routes):
        for p in range(2):
            piece = tok[t : t + 1, p * half : (p + 1) * half]
            here = (side == p).astype(I32)
            main = main + (first * here).astype(F32) * piece
            rest = piece[:, low:]
            if 2 * low > half:
                rest = jnp.concatenate([rest, jnp.zeros((1, 2 * low - half), F32)], axis=1)
            third_here = third * here
            tail = tail + (third_here * (1 - part)).astype(F32) * piece[:, :low]
            tail = tail + (third_here * part).astype(F32) * rest
    o_ref[:, :half] = main.astype(BF)
    o_ref[:, half:] = tail.astype(BF)


def packed_of(here, ids, tokens, owners, block):
    half = block // 2
    width = half + split_of(half)

    def kernel(*refs):
        pack_body(block, *refs)

    return pl.pallas_call(
        kernel,
        out_shape=jax.ShapeDtypeStruct((2 * owners, width), BF),
        in_specs=[SM, SM, VM],
        out_specs=VM,
        compiler_params=params(4),
        name="pack",
    )(here, ids, tokens)


def mix_kernel(ids_ref, code_ref, x_ref, o_ref):
    rows, width = x_ref.shape
    half = o_ref.shape[1] // 2
    low = width - half
    routes, side, part = routing(ids_ref, rows)
    x = x_ref[...].astype(F32)
    for t, (hits, first, third) in enumerate(routes):
        code = sum(hit * code_ref[t, j] for j, hit in enumerate(hits))
        weight = code.astype(F32) / 64.0
        for p in range(2):
            here = (side == p).astype(I32)

            def total(chosen, lo, hi):
                scaled = (chosen * here).astype(F32) * weight * x[:, lo:hi]
                return jnp.sum(scaled, axis=0, keepdims=True)

            main = total(first, 0, half)
            lower = total(third * (1 - part), half, width)
            upper = total(third * part, half, 2 * half - low)
            at = p * half
            o_ref[t : t + 1, at : at + low] = (main[:, :low] + lower).astype(BF)
            o_ref[t : t + 1, at + low : at + half] = (main[:, low:] + upper).astype(BF)


def mixed_of(ids, codes, x, block):
    return pl.pallas_call(
        mix_kernel,
        out_shape=jax.ShapeDtypeStruct((ids.shape[0], block), BF),
        in_specs=[SM, SM, VM],
        out_specs=VM,
        compiler_params=params(4),
        name="mix",
    )(ids, codes, x)


def fetch_kernel(g0, u0, d0, g1, u1, d1, g_ref, u_ref, d_ref, sems):
    copies = []
    for i, (src, dst) in enumerate(
        ((g0, g_ref), (u0, u_ref), (d0, d_ref), (g1, g_ref), (u1, u_ref), (d1, d_ref))
    ):
        units = src.shape[0]
        rows = pl.ds((i // 3) * units, units)
        copies.append(pltpu.make_async_copy(src, dst.at[rows], sems.at[i]))
    for copy in copies:
        copy.start()
    for copy in copies:
        copy.wait()


def fetched(own, other):
    units, features = own[0].shape
    shape = jax.ShapeDtypeStruct((2 * units, features), BF)
    return pl.pallas_call(
        fetch_kernel,
        out_shape=(shape,) * 3,
        in_specs=[ANY] * 6,
        out_specs=(VM,) * 3,
        scratch_shapes=[pltpu.SemaphoreType.DMA((6,))],
        cost_estimate=pl.CostEstimate(
            flops=12 * units * features * 256,
            bytes_accessed=24 * units * features,
            transcendentals=0,
        ),
        compiler_params=params(13),
        name="fetch",
    )(*(pltpu.with_memory_space_constraint(w, pltpu.MemorySpace.HBM) for w in own), *other)


def expert_kernel(here_ref, odd_ref, *refs):
    parts = (len(refs) - 5) // 2
    pieces, (g_ref, u_ref, d_ref, keep_ref, give_ref) = refs[: 2 * parts], refs[2 * parts :]
    owners, _, width = pieces[0].shape
    rows = 2 * owners
    half = d_ref.shape[1] // (2 * parts)
    low = width - half
    units = g_ref.shape[0]
    odd, here = odd_ref[0], here_ref[0]

    def start(k, other):
        side = 1 - odd if other else odd
        return pl.multiple_of((2 * k + side) * half, 128)

    sums = [[jnp.zeros((2 * rows, units), F32) for _ in range(2)] for _ in range(2)]
    for i, x_ref in enumerate(pieces):
        k = lax.rem(here + parts - i % parts, parts)
        x = x_ref[...].reshape(rows, width)
        at = start(k, i >= parts)
        lhs = (
            jnp.concatenate([x[:, :low], x[:, half:]], axis=0),
            jnp.concatenate([x[:, low:half], x[:, half : 2 * half - low]], axis=0),
        )
        for w, w_ref in enumerate((g_ref, u_ref)):
            for c, (lo, size) in enumerate(((0, low), (low, half - low))):
                cols = pl.ds(pl.multiple_of(at + lo, 128), size)
                sums[w][c] += lax.dot_general(
                    lhs[c], w_ref[:, cols], CONTRACT, preferred_element_type=F32
                )

    def joined(a, b):
        third = a[rows:] + pltpu.roll(b[rows:], rows - 1, 0)
        return jnp.concatenate([a[:rows] + b[:rows], third], axis=0)

    gate, up = joined(*sums[0]), joined(*sums[1])
    hidden = gate / (1.0 + jnp.exp(-gate)) * up
    third = hidden[rows:]
    even = lax.broadcasted_iota(I32, (rows, units), 0) % 2 == 0
    lower = jnp.where(even, third, 0.0)
    upper = jnp.where(even, 0.0, pltpu.roll(third, 1, 0))
    lhs = (
        jnp.concatenate([hidden[:rows], lower], axis=0).astype(BF),
        jnp.concatenate([hidden[:rows], upper], axis=0).astype(BF),
    )
    for other, o_ref in ((True, give_ref), (False, keep_ref)):
        for k in range(parts):
            at = start(k, other)
            a = jnp.dot(lhs[0], d_ref[:, pl.ds(at, low)], preferred_element_type=F32)
            cols = pl.ds(pl.multiple_of(at + low, 128), half - low)
            b = jnp.dot(lhs[1], d_ref[:, cols], preferred_element_type=F32)
            o_ref[k, :, :low] = a[:rows].astype(BF)
            o_ref[k, :, low:half] = b[:rows].astype(BF)
            o_ref[k, :, half : 2 * half - low] = (a[rows:, : half - low] + b[rows:]).astype(BF)
            if 2 * low > half:
                o_ref[k, :, 2 * half - low :] = a[rows:, half - low :].astype(BF)


def experts_of(here, odd, pieces, weights):
    parts = len(pieces) // 2
    owners, _, width = pieces[0].shape
    units, features = weights[0].shape
    shape = jax.ShapeDtypeStruct((parts, 2 * owners, width), BF)
    return pl.pallas_call(
        expert_kernel,
        out_shape=(shape, shape),
        in_specs=[SM] * 2 + [VM] * (2 * parts + 3),
        out_specs=(VM, VM),
        cost_estimate=pl.CostEstimate(
            flops=24 * owners * units * features,
            bytes_accessed=6 * units * features,
            transcendentals=4 * owners * units,
        ),
        compiler_params=params(24),
        name="experts",
    )(here, odd, *pieces, *weights)


def shards(tokens, expert_ids, gate_codes, w_gate, w_up, w_down):
    rows, features = tokens.shape
    owners = lax.axis_size("expert")
    subs = lax.axis_size("sub")
    parts = lax.axis_size("tensor")
    experts = owners // 2
    assert min(rows, rows * expert_ids.shape[1] // experts + 1) == 3
    block = features // parts
    width = block // 2 + split_of(block // 2)
    here = lax.axis_index("tensor").reshape(1)
    odd = (lax.axis_index("expert") & 1).reshape(1)
    swap_sub = [(i, subs - 1 - i) for i in range(subs)]
    swap_pair = [(i, i ^ 1) for i in range(owners)]

    def turned(x, k):
        return lax.ppermute(x, "tensor", [(i, (i + k) % parts) for i in range(parts)])

    def across(x):
        return lax.all_to_all(x, "tensor", split_axis=0, concat_axis=0, tiled=True)

    def along(x):
        return lax.all_to_all(x, "expert", split_axis=0, concat_axis=0, tiled=True)

    own = (w_gate[0], w_up[0], w_down[0])
    other = [lax.ppermute(w, "sub", swap_sub) for w in own]
    weights = fetched(own, other)
    packed = packed_of(here, expert_ids, tokens, owners, block).reshape(owners, 2, width)
    arrived = along(packed)
    partner = lax.ppermute(arrived, "expert", swap_pair)
    pieces = [arrived] + [None] * (parts - 1) + [partner] + [None] * (parts - 1)
    steps = sorted(range(1, parts), key=lambda k: min(k, parts - k))
    for k in steps:
        pieces[k] = turned(arrived, k)
    for k in steps:
        pieces[parts + k] = turned(partner, k)
    keep, give = experts_of(here, odd, pieces, weights)
    give = across(give)
    give = jnp.sum(give.astype(F32), axis=0).astype(BF)
    taken = lax.ppermute(give, "expert", swap_pair)
    keep = across(keep)
    both = jnp.sum(keep.astype(F32), axis=0) + taken.astype(F32)
    both = both.astype(BF).reshape(owners, 2, width)
    back = along(both).reshape(2 * owners, width)
    return mixed_of(expert_ids, gate_codes, back, block)


def solution(mesh):
    spread = P(("group", "expert", "sub"), None)
    weights = P("expert", ("tensor", "sub"), None)
    return jax.shard_map(
        shards,
        mesh=mesh,
        in_specs=(spread, spread, spread, weights, weights, weights),
        out_specs=P(("group", "expert", "sub"), "tensor"),
        check_vma=False,
    )
```

time: 192 us -> 190 us (0.990)
  blocking collectives: 11.4 us -> 132 us
  waiting for transfers between devices: 89.8 us -> 8.71 us
  starting transfers between devices: 74.5 us -> 36.2 us
  local copies, waits for them, and re-layouts: 6.87 us -> 1.72 us
  Pallas kernels: 6.23 us -> 10.7 us
    all_to_all x0 -> x2, blocking collectives: none -> 117 us  [along(): return lax.all_to_all(x, 'expert', split_axis=0, concat_axis=0, tiled=True)]
    all_to_all x2 -> x0, waiting for transfers between devices: 67.1 us -> none  [the longest x1 34.4 us: shards(): lax.all_to_all(both, 'expert', split_axis=0, concat_axis=0, tiled=True)]
    all_to_all x2 -> x0, starting transfers between devices: 52 us -> none  [the longest x1 45.8 us: shards(): lax.all_to_all(packed.reshape(owners, capacity, half), 'expert', split_ax...]
    ppermute x0 -> x6, starting transfers between devices: none -> 22 us  [turned(): lax.ppermute(x, 'tensor', [(i, (i + k) % parts) for i in range(parts)])]
    all_to_all x3 -> x1, waiting for transfers between devices: 17.5 us -> 6.85 us  [across(): return lax.all_to_all(x, 'tensor', split_axis=0, concat_axis=0, tiled=True)]
    all_to_all x3 -> x1, starting transfers between devices: 11.9 us -> 3.58 us  [across(): return lax.all_to_all(x, 'tensor', split_axis=0, concat_axis=0, tiled=True)]
    pallas_call x1 -> x4, Pallas kernels: 6.23 us -> 10.7 us  [the longest x1 4.11 us: experts_of(): pl.pallas_call(expert_kernel, out_shape=(shape, shape), in_specs=[SM] * 2...]
    ppermute x1, waiting for transfers between devices: 5.22 us -> 1.84 us  [shards(): partner = lax.ppermute(arrived, 'expert', swap_pair)]
  transfers between devices with their start and end apart: 10 -> 12, of which waited for: 6 -> 2; matrix products, arithmetic and copies ran while one was open for 1% -> 0% of each run, Pallas kernels for 0% -> 3%
where the time goes in v3:
time: 190 us; the launch traced here: 189 us
  blocking collectives  132 us (69%)
  starting transfers between devices  36.2 us (19%)
  Pallas kernels  10.7 us (6%)
  waiting for transfers between devices  8.71 us (5%)
    all_to_all x2, blocking collectives, along(): return lax.all_to_all(x, 'expert', split_axis=0, concat_axis=0, tiled=True)  117 us
    ppermute x6, starting transfers between devices, turned(): lax.ppermute(x, 'tensor', [(i, (i + k) % parts) for i in range(parts)])  22 us
    all_to_all x1, blocking collectives, across(): return lax.all_to_all(x, 'tensor', split_axis=0, concat_axis=0, tiled=True)  14.2 us
    all_to_all x1, waiting for transfers between devices, across(): return lax.all_to_all(x, 'tensor', split_axis=0, concat_axis=0, tiled=True)  6.85 us
    ppermute x3, starting transfers between devices, shards(): other = [lax.ppermute(w, 'sub', swap_sub) for w in own]  6.34 us
    pallas_call x1, Pallas kernels, experts_of(): pl.pallas_call(expert_kernel, out_shape=(shape, shape), in_specs=[SM] * 2...  4.11 us
  transfers between devices with their start and end apart: 12, of which 2 were waited for; matrix products, arithmetic and copies ran while one was open for 0% of the time, Pallas kernels for 3%

profile of v3, /device:TPU:40, one launch (start us, length us, event | category | flops | bytes accessed | tf_op | source)
XLA Modules:
  0.0 189.3 jit_solution(4660969035666184286)
XLA Ops:
  0.0 1.9 %collective-permute-start.7 = (bf16[128,7168]{1,0:T(8,128)(2,1)}, bf16[128,7168]{1,0:T(8,128)(2,1)S(1)}, u32[]{:S(2)}, u32[]{:S(2)}) collective-permute-start(bf16[128,7168]{1,0:T(8,128)(2,1)} %bitcast.5), channel_id=1, source_target_pairs={{0,1},{1,0},{2,3},{3,2},{4,5},{5,4},{6,7},{7,6},{8,9},{9,8},{10,11... | collective-permute-start | bytes 5505032 | tf_op jit(solution)/shard_map/ppermute | solution.py:252
  1.9 2.4 %collective-permute-start.8 = (bf16[128,7168]{1,0:T(8,128)(2,1)}, bf16[128,7168]{1,0:T(8,128)(2,1)}, u32[]{:S(2)}, u32[]{:S(2)}) collective-permute-start(bf16[128,7168]{1,0:T(8,128)(2,1)} %bitcast.7), channel_id=1, source_target_pairs={{0,1},{1,0},{2,3},{3,2},{4,5},{5,4},{6,7},{7,6},{8,9},{9,8},{10,11... | collective-permute-start | bytes 5505032 | tf_op jit(solution)/shard_map/ppermute | solution.py:252
  4.4 2.0 %collective-permute-start.9 = (bf16[128,7168]{1,0:T(8,128)(2,1)}, bf16[128,7168]{1,0:T(8,128)(2,1)}, u32[]{:S(2)}, u32[]{:S(2)}) collective-permute-start(bf16[128,7168]{1,0:T(8,128)(2,1)} %bitcast.9), channel_id=1, source_target_pairs={{0,1},{1,0},{2,3},{3,2},{4,5},{5,4},{6,7},{7,6},{8,9},{9,8},{10,11... | collective-permute-start | bytes 5505032 | tf_op jit(solution)/shard_map/ppermute | solution.py:252
  6.4 0.8 copy-done
  7.2 0.7 copy-done.1
  7.9 1.0 pack.1
  8.9 0.1 reshape.17
  9.0 81.1 %all_to_all.20.refs_0_ = bf16[32,2,1408]{2,1,0:T(2,128)(2,1)S(1)} all-to-all(bf16[32,2,1408]{2,1,0:T(2,128)(2,1)S(1)} %reshape.17), channel_id=1, replica_groups=mesh['group'=2,'expert'=32,'tensor'=4,'sub'=2] {'expert'}, dimensions={0} | all-to-all | bytes 360448 | tf_op jit(solution)/shard_map/all_to_all | solution.py:249
  90.1 2.2 %collective-permute-start.3 = (bf16[32,2,1408]{2,1,0:T(2,128)(2,1)S(1)}, bf16[32,2,1408]{2,1,0:T(2,128)(2,1)S(1)}, u32[]{:S(2)}, u32[]{:S(2)}) collective-permute-start(bf16[32,2,1408]{2,1,0:T(2,128)(2,1)S(1)} %all_to_all.20.refs_0_), channel_id=1, source_target_pairs={{0,8},{8,0},{16,24},{24,16},{32,40},{40,32},{48,56},{56,48},{64,72... | collective-permute-start | bytes 540680 | tf_op jit(solution)/shard_map/ppermute | solution.py:256
  92.3 3.6 %collective-permute-start = (bf16[32,2,1408]{2,1,0:T(2,128)(2,1)S(1)}, bf16[32,2,1408]{2,1,0:T(2,128)(2,1)S(1)}, u32[]{:S(2)}, u32[]{:S(2)}) collective-permute-start(bf16[32,2,1408]{2,1,0:T(2,128)(2,1)S(1)} %all_to_all.20.refs_0_), channel_id=1, source_target_pairs={{0,2},{2,4},{4,6},{6,0},{1,3},{3,5},{5,7},{7,1},{8,10},{10,12},{12... | collective-permute-start | bytes 540680 | tf_op jit(solution)/shard_map/ppermute | solution.py:243
  95.9 1.8 collective-permute-done.3.refs_4_
  97.7 5.2 %collective-permute-start.1 = (bf16[32,2,1408]{2,1,0:T(2,128)(2,1)S(1)}, bf16[32,2,1408]{2,1,0:T(2,128)(2,1)S(1)}, u32[]{:S(2)}, u32[]{:S(2)}) collective-permute-start(bf16[32,2,1408]{2,1,0:T(2,128)(2,1)S(1)} %all_to_all.20.refs_0_), channel_id=1, source_target_pairs={{0,4},{2,6},{4,0},{6,2},{1,5},{3,7},{5,1},{7,3},{8,12},{10,14},{12... | collective-permute-start | bytes 540680 | tf_op jit(solution)/shard_map/ppermute | solution.py:243
  103.0 2.9 %collective-permute-start.2 = (bf16[32,2,1408]{2,1,0:T(2,128)(2,1)S(1)}, bf16[32,2,1408]{2,1,0:T(2,128)(2,1)S(1)}, u32[]{:S(2)}, u32[]{:S(2)}) collective-permute-start(bf16[32,2,1408]{2,1,0:T(2,128)(2,1)S(1)} %all_to_all.20.refs_0_), channel_id=1, source_target_pairs={{0,6},{2,0},{4,2},{6,4},{1,7},{3,1},{5,3},{7,5},{8,14},{10,8},{12,... | collective-permute-start | bytes 540680 | tf_op jit(solution)/shard_map/ppermute | solution.py:243
  106.0 3.0 %collective-permute-start.4 = (bf16[32,2,1408]{2,1,0:T(2,128)(2,1)S(1)}, bf16[32,2,1408]{2,1,0:T(2,128)(2,1)S(1)}, u32[]{:S(2)}, u32[]{:S(2)}) collective-permute-start(bf16[32,2,1408]{2,1,0:T(2,128)(2,1)S(1)} %collective-permute-done.3.refs_4_), channel_id=1, source_target_pairs={{0,2},{2,4},{4,6},{6,0},{1,3},{3,5},{5,7},{7,1},{8,10},{10,12},{12... | collective-permute-start | bytes 540680 | tf_op jit(solution)/shard_map/ppermute | solution.py:243
  108.9 0.0 collective-permute-done.8.u1
  108.9 2.7 %collective-permute-start.5 = (bf16[32,2,1408]{2,1,0:T(2,128)(2,1)S(1)}, bf16[32,2,1408]{2,1,0:T(2,128)(2,1)S(1)}, u32[]{:S(2)}, u32[]{:S(2)}) collective-permute-start(bf16[32,2,1408]{2,1,0:T(2,128)(2,1)S(1)} %collective-permute-done.3.refs_4_), channel_id=1, source_target_pairs={{0,4},{2,6},{4,0},{6,2},{1,5},{3,7},{5,1},{7,3},{8,12},{10,14},{12... | collective-permute-start | bytes 540680 | tf_op jit(solution)/shard_map/ppermute | solution.py:243
  111.7 0.0 collective-permute-done.9.d1
  111.7 4.6 %collective-permute-start.6 = (bf16[32,2,1408]{2,1,0:T(2,128)(2,1)S(1)}, bf16[32,2,1408]{2,1,0:T(2,128)(2,1)S(1)}, u32[]{:S(2)}, u32[]{:S(2)}) collective-permute-start(bf16[32,2,1408]{2,1,0:T(2,128)(2,1)S(1)} %collective-permute-done.3.refs_4_), channel_id=1, source_target_pairs={{0,6},{2,0},{4,2},{6,4},{1,7},{3,1},{5,3},{7,5},{8,14},{10,8},{12,... | collective-permute-start | bytes 540680 | tf_op jit(solution)/shard_map/ppermute | solution.py:243
  116.2 3.8 %fetch.1 = (bf16[256,7168]{1,0:T(8,128)(2,1)S(1)}, bf16[256,7168]{1,0:T(8,128)(2,1)S(1)}, bf16[256,7168]{1,0:T(8,128)(2,1)S(1)}) custom-call(bf16[128,7168]{1,0:T(8,128)(2,1)} %bitcast.6, bf16[128,7168]{1,0:T(8,128)(2,1)} %bitcast.8, bf16[128,7168]{1,0:T(8,128)(2,1)} %bitcast.10, bf16[128,7168]{1,0:T(8,128)(2,1)S(1)} %collective-permute-done.7.g1, ...), custom_call_target="tpu_custom_call" | custom-call | flops 2818572288 | bytes 22020096 | tf_op jit(solution)/shard_map/fetch/pallas_call | solution.py:135
  120.1 4.1 %experts.1 = (bf16[4,64,1408]{2,1,0:T(8,128)(2,1)}, bf16[4,64,1408]{2,1,0:T(8,128)(2,1)S(1)}) custom-call(s32[1]{0:T(128)} %bitcast.refs_0_.here_ref, s32[1]{0:T(128)} %bitcast.1.odd_ref, bf16[32,2,1408]{2,1,0:T(2,128)(2,1)S(1)} %all_to_all.20.refs_0_, bf16[32,2,1408]{2,1,0:T(2,128)(2,1)S(1)} %collective-permute-done.refs_1_, ...), custom_call_target="tpu_custom_call" | custom-call | flops 1409286144 | bytes 11010048 | tf_op jit(solution)/shard_map/experts/pallas_call | solution.py:213
  124.2 14.2 %all_to_all.21 = bf16[4,64,1408]{2,1,0:T(8,128)(2,1)S(1)} all-to-all(bf16[4,64,1408]{2,1,0:T(8,128)(2,1)S(1)} %get-tuple-element.14), channel_id=1, replica_groups=mesh['group'=2,'expert'=32,'tensor'=4,'sub'=2] {'tensor'}, dimensions={0} | all-to-all | bytes 1441792 | tf_op jit(solution)/shard_map/all_to_all | solution.py:246
  138.4 3.6 %all-to-all-start.1 = ((bf16[4,64,1408]{2,1,0:T(8,128)(2,1)}), bf16[4,64,1408]{2,1,0:T(8,128)(2,1)S(1)}, u32[]{:S(2)}, u32[]{:S(2)}) async-start(bf16[4,64,1408]{2,1,0:T(8,128)(2,1)} %get-tuple-element.13), calls=%async_computation.1 | async-start | bytes 1441792 | tf_op jit(solution)/shard_map/all_to_all | solution.py:246
  142.0 0.0 copy-start.2
  142.0 0.0 copy-start.3
  142.0 0.1 reduce_sum.22
  142.1 2.0 %collective-permute-start.10 = (bf16[64,1408]{1,0:T(8,128)(2,1)S(1)}, bf16[64,1408]{1,0:T(8,128)(2,1)S(1)}, u32[]{:S(2)}, u32[]{:S(2)}) collective-permute-start(bf16[64,1408]{1,0:T(8,128)(2,1)S(1)} %reduce_sum.22), channel_id=1, source_target_pairs={{0,8},{8,0},{16,24},{24,16},{32,40},{40,32},{48,56},{56,48},{64,72... | collective-permute-start | bytes 540680 | tf_op jit(solution)/shard_map/ppermute | solution.py:266
  144.2 6.8 %all-to-all-done.1 = bf16[4,64,1408]{2,1,0:T(8,128)(2,1)S(1)} async-done(((bf16[4,64,1408]{2,1,0:T(8,128)(2,1)}), bf16[4,64,1408]{2,1,0:T(8,128)(2,1)S(1)}, u32[]{:S(2)}, u32[]{:S(2)}) %all-to-all-start.1) | async-done | bytes 720928 | tf_op jit(solution)/shard_map/all_to_all | solution.py:246
  151.0 0.1 convert_reduce_fusion
  151.2 0.1 reshape.18
  151.3 36.1 %all_to_all.22 = bf16[32,2,1408]{2,1,0:T(2,128)(2,1)S(1)} all-to-all(bf16[32,2,1408]{2,1,0:T(2,128)(2,1)S(1)} %reshape.18), channel_id=1, replica_groups=mesh['group'=2,'expert'=32,'tensor'=4,'sub'=2] {'expert'}, dimensions={0} | all-to-all | bytes 360448 | tf_op jit(solution)/shard_map/all_to_all | solution.py:249
  187.4 0.1 reshape.19.x_ref
  187.5 1.8 mix.1
  (13 shorter events, 0.1 us)
Async XLA Ops:
  0.0 105.9 %collective-permute-start.7 = (bf16[128,7168]{1,0:T(8,128)(2,1)}, bf16[128,7168]{1,0:T(8,128)(2,1)S(1)}, u32[]{:S(2)}, u32[]{:S(2)}) collective-permute-start(bf16[128,7168]{1,0:T(8,128)(2,1)} %bitcast.5), channel_id=1, source_target_pairs={{0,1},{1,0},{2,3},{3,2},{4,5},{5,4},{6,7},{7,6},{8,9},{9,8},{10,11... | collective-permute-start | bytes 5505032 | tf_op jit(solution)/shard_map/ppermute | solution.py:252
  1.9 107.0 %collective-permute-start.8 = (bf16[128,7168]{1,0:T(8,128)(2,1)}, bf16[128,7168]{1,0:T(8,128)(2,1)}, u32[]{:S(2)}, u32[]{:S(2)}) collective-permute-start(bf16[128,7168]{1,0:T(8,128)(2,1)} %bitcast.7), channel_id=1, source_target_pairs={{0,1},{1,0},{2,3},{3,2},{4,5},{5,4},{6,7},{7,6},{8,9},{9,8},{10,11... | collective-permute-start | bytes 5505032 | tf_op jit(solution)/shard_map/ppermute | solution.py:252
  4.4 107.3 %collective-permute-start.9 = (bf16[128,7168]{1,0:T(8,128)(2,1)}, bf16[128,7168]{1,0:T(8,128)(2,1)}, u32[]{:S(2)}, u32[]{:S(2)}) collective-permute-start(bf16[128,7168]{1,0:T(8,128)(2,1)} %bitcast.9), channel_id=1, source_target_pairs={{0,1},{1,0},{2,3},{3,2},{4,5},{5,4},{6,7},{7,6},{8,9},{9,8},{10,11... | collective-permute-start | bytes 5505032 | tf_op jit(solution)/shard_map/ppermute | solution.py:252
  6.4 0.8 copy-start
  7.2 0.7 copy-start.1
  90.1 7.6 %collective-permute-start.3 = (bf16[32,2,1408]{2,1,0:T(2,128)(2,1)S(1)}, bf16[32,2,1408]{2,1,0:T(2,128)(2,1)S(1)}, u32[]{:S(2)}, u32[]{:S(2)}) collective-permute-start(bf16[32,2,1408]{2,1,0:T(2,128)(2,1)S(1)} %all_to_all.20.refs_0_), channel_id=1, source_target_pairs={{0,8},{8,0},{16,24},{24,16},{32,40},{40,32},{48,56},{56,48},{64,72... | collective-permute-start | bytes 540680 | tf_op jit(solution)/shard_map/ppermute | solution.py:256
  92.3 10.6 %collective-permute-start = (bf16[32,2,1408]{2,1,0:T(2,128)(2,1)S(1)}, bf16[32,2,1408]{2,1,0:T(2,128)(2,1)S(1)}, u32[]{:S(2)}, u32[]{:S(2)}) collective-permute-start(bf16[32,2,1408]{2,1,0:T(2,128)(2,1)S(1)} %all_to_all.20.refs_0_), channel_id=1, source_target_pairs={{0,2},{2,4},{4,6},{6,0},{1,3},{3,5},{5,7},{7,1},{8,10},{10,12},{12... | collective-permute-start | bytes 540680 | tf_op jit(solution)/shard_map/ppermute | solution.py:243
  97.7 22.3 %collective-permute-start.1 = (bf16[32,2,1408]{2,1,0:T(2,128)(2,1)S(1)}, bf16[32,2,1408]{2,1,0:T(2,128)(2,1)S(1)}, u32[]{:S(2)}, u32[]{:S(2)}) collective-permute-start(bf16[32,2,1408]{2,1,0:T(2,128)(2,1)S(1)} %all_to_all.20.refs_0_), channel_id=1, source_target_pairs={{0,4},{2,6},{4,0},{6,2},{1,5},{3,7},{5,1},{7,3},{8,12},{10,14},{12... | collective-permute-start | bytes 540680 | tf_op jit(solution)/shard_map/ppermute | solution.py:243
  103.0 17.0 %collective-permute-start.2 = (bf16[32,2,1408]{2,1,0:T(2,128)(2,1)S(1)}, bf16[32,2,1408]{2,1,0:T(2,128)(2,1)S(1)}, u32[]{:S(2)}, u32[]{:S(2)}) collective-permute-start(bf16[32,2,1408]{2,1,0:T(2,128)(2,1)S(1)} %all_to_all.20.refs_0_), channel_id=1, source_target_pairs={{0,6},{2,0},{4,2},{6,4},{1,7},{3,1},{5,3},{7,5},{8,14},{10,8},{12,... | collective-permute-start | bytes 540680 | tf_op jit(solution)/shard_map/ppermute | solution.py:243
  106.0 14.1 %collective-permute-start.4 = (bf16[32,2,1408]{2,1,0:T(2,128)(2,1)S(1)}, bf16[32,2,1408]{2,1,0:T(2,128)(2,1)S(1)}, u32[]{:S(2)}, u32[]{:S(2)}) collective-permute-start(bf16[32,2,1408]{2,1,0:T(2,128)(2,1)S(1)} %collective-permute-done.3.refs_4_), channel_id=1, source_target_pairs={{0,2},{2,4},{4,6},{6,0},{1,3},{3,5},{5,7},{7,1},{8,10},{10,12},{12... | collective-permute-start | bytes 540680 | tf_op jit(solution)/shard_map/ppermute | solution.py:243
  108.9 11.1 %collective-permute-start.5 = (bf16[32,2,1408]{2,1,0:T(2,128)(2,1)S(1)}, bf16[32,2,1408]{2,1,0:T(2,128)(2,1)S(1)}, u32[]{:S(2)}, u32[]{:S(2)}) collective-permute-start(bf16[32,2,1408]{2,1,0:T(2,128)(2,1)S(1)} %collective-permute-done.3.refs_4_), channel_id=1, source_target_pairs={{0,4},{2,6},{4,0},{6,2},{1,5},{3,7},{5,1},{7,3},{8,12},{10,14},{12... | collective-permute-start | bytes 540680 | tf_op jit(solution)/shard_map/ppermute | solution.py:243
  111.7 8.4 %collective-permute-start.6 = (bf16[32,2,1408]{2,1,0:T(2,128)(2,1)S(1)}, bf16[32,2,1408]{2,1,0:T(2,128)(2,1)S(1)}, u32[]{:S(2)}, u32[]{:S(2)}) collective-permute-start(bf16[32,2,1408]{2,1,0:T(2,128)(2,1)S(1)} %collective-permute-done.3.refs_4_), channel_id=1, source_target_pairs={{0,6},{2,0},{4,2},{6,4},{1,7},{3,1},{5,3},{7,5},{8,14},{10,8},{12,... | collective-permute-start | bytes 540680 | tf_op jit(solution)/shard_map/ppermute | solution.py:243
  138.4 12.6 %all-to-all-start.1 = ((bf16[4,64,1408]{2,1,0:T(8,128)(2,1)}), bf16[4,64,1408]{2,1,0:T(8,128)(2,1)S(1)}, u32[]{:S(2)}, u32[]{:S(2)}) async-start(bf16[4,64,1408]{2,1,0:T(8,128)(2,1)} %get-tuple-element.13), calls=%async_computation.1 | async-start | bytes 1441792 | tf_op jit(solution)/shard_map/all_to_all | solution.py:246
  142.0 45.5 %copy-start.2 = (s32[4,8]{1,0:T(4,128)S(1)}, s32[4,8]{1,0:T(4,128)}, u32[]{:S(2)}) copy-start(s32[4,8]{1,0:T(4,128)} %ids_ref.1) | copy-start | bytes 388
  142.0 45.5 %copy-start.3 = (s32[4,8]{1,0:T(4,128)S(1)}, s32[4,8]{1,0:T(4,128)}, u32[]{:S(2)}) copy-start(s32[4,8]{1,0:T(4,128)} %code_ref.1) | copy-start | bytes 388
  142.1 9.0 %collective-permute-start.10 = (bf16[64,1408]{1,0:T(8,128)(2,1)S(1)}, bf16[64,1408]{1,0:T(8,128)(2,1)S(1)}, u32[]{:S(2)}, u32[]{:S(2)}) collective-permute-start(bf16[64,1408]{1,0:T(8,128)(2,1)S(1)} %reduce_sum.22), channel_id=1, source_target_pairs={{0,8},{8,0},{16,24},{24,16},{32,40},{40,32},{48,56},{56,48},{64,72... | collective-permute-start | bytes 540680 | tf_op jit(solution)/shard_map/ppermute | solution.py:266

commit v4 on v3

--- a/solution.py
+++ b/solution.py
@@ -149,9 +149,10 @@
 
 
 def expert_kernel(here_ref, odd_ref, *refs):
-    parts = (len(refs) - 5) // 2
-    pieces, (g_ref, u_ref, d_ref, keep_ref, give_ref) = refs[: 2 * parts], refs[2 * parts :]
-    owners, _, width = pieces[0].shape
+    own_ref = refs[0]
+    parts, owners, _, width = own_ref.shape
+    pals, (g_ref, u_ref, d_ref, give_ref) = refs[1 : 1 + parts], refs[1 + parts : 5 + parts]
+    keep_refs = refs[5 + parts :]
     rows = 2 * owners
     half = d_ref.shape[1] // (2 * parts)
     low = width - half
@@ -163,10 +164,12 @@
         return pl.multiple_of((2 * k + side) * half, 128)
 
     sums = [[jnp.zeros((2 * rows, units), F32) for _ in range(2)] for _ in range(2)]
-    for i, x_ref in enumerate(pieces):
-        k = lax.rem(here + parts - i % parts, parts)
-        x = x_ref[...].reshape(rows, width)
-        at = start(k, i >= parts)
+    for i in range(2 * parts):
+        if i < parts:
+            x, at = own_ref[i], start(i, False)
+        else:
+            x, at = pals[i - parts][...], start(lax.rem(here + 2 * parts - i, parts), True)
+        x = x.reshape(rows, width)
         lhs = (
             jnp.concatenate([x[:, :low], x[:, half:]], axis=0),
             jnp.concatenate([x[:, low:half], x[:, half : 2 * half - low]], axis=0),
@@ -192,29 +195,29 @@
         jnp.concatenate([hidden[:rows], lower], axis=0).astype(BF),
         jnp.concatenate([hidden[:rows], upper], axis=0).astype(BF),
     )
-    for other, o_ref in ((True, give_ref), (False, keep_ref)):
+    for other in (True, False):
         for k in range(parts):
-            at = start(k, other)
+            at = start(k if other else lax.rem(here + k, parts), other)
+            o_ref = give_ref.at[k] if other else keep_refs[k]
             a = jnp.dot(lhs[0], d_ref[:, pl.ds(at, low)], preferred_element_type=F32)
             cols = pl.ds(pl.multiple_of(at + low, 128), half - low)
             b = jnp.dot(lhs[1], d_ref[:, cols], preferred_element_type=F32)
-            o_ref[k, :, :low] = a[:rows].astype(BF)
-            o_ref[k, :, low:half] = b[:rows].astype(BF)
-            o_ref[k, :, half : 2 * half - low] = (a[rows:, : half - low] + b[rows:]).astype(BF)
+            o_ref[:, :low] = a[:rows].astype(BF)
+            o_ref[:, low:half] = b[:rows].astype(BF)
+            o_ref[:, half : 2 * half - low] = (a[rows:, : half - low] + b[rows:]).astype(BF)
             if 2 * low > half:
-                o_ref[k, :, 2 * half - low :] = a[rows:, half - low :].astype(BF)
-
-
-def experts_of(here, odd, pieces, weights):
-    parts = len(pieces) // 2
-    owners, _, width = pieces[0].shape
+                o_ref[:, 2 * half - low :] = a[rows:, half - low :].astype(BF)
+
+
+def experts_of(here, odd, own, pals, weights):
+    parts, owners, _, width = own.shape
     units, features = weights[0].shape
-    shape = jax.ShapeDtypeStruct((parts, 2 * owners, width), BF)
-    return pl.pallas_call(
+    one = jax.ShapeDtypeStruct((2 * owners, width), BF)
+    out = pl.pallas_call(
         expert_kernel,
-        out_shape=(shape, shape),
-        in_specs=[SM] * 2 + [VM] * (2 * parts + 3),
-        out_specs=(VM, VM),
+        out_shape=(jax.ShapeDtypeStruct((parts, *one.shape), BF), *(one,) * parts),
+        in_specs=[SM] * 2 + [VM] * (parts + 4),
+        out_specs=(VM,) * (parts + 1),
         cost_estimate=pl.CostEstimate(
             flops=24 * owners * units * features,
             bytes_accessed=6 * units * features,
@@ -222,7 +225,8 @@
         ),
         compiler_params=params(24),
         name="experts",
-    )(here, odd, *pieces, *weights)
+    )(here, odd, own, *pals, *weights)
+    return out[0], out[1:]
 
 
 def shards(tokens, expert_ids, gate_codes, w_gate, w_up, w_down):
@@ -254,21 +258,26 @@
     packed = packed_of(here, expert_ids, tokens, owners, block).reshape(owners, 2, width)
     arrived = along(packed)
     partner = lax.ppermute(arrived, "expert", swap_pair)
-    pieces = [arrived] + [None] * (parts - 1) + [partner] + [None] * (parts - 1)
-    steps = sorted(range(1, parts), key=lambda k: min(k, parts - k))
-    for k in steps:
-        pieces[k] = turned(arrived, k)
-    for k in steps:
-        pieces[parts + k] = turned(partner, k)
-    keep, give = experts_of(here, odd, pieces, weights)
+    spread = jnp.broadcast_to(arrived[None], (parts, *arrived.shape))
+    spread = across(spread)
+    pals = [partner] + [None] * (parts - 1)
+    for k in ring_steps(parts):
+        pals[k] = turned(partner, k)
+    give, keep = experts_of(here, odd, spread, pals, weights)
     give = across(give)
+    kept = [keep[0]]
+    for k in ring_steps(parts):
+        kept.append(turned(keep[k], k))
     give = jnp.sum(give.astype(F32), axis=0).astype(BF)
     taken = lax.ppermute(give, "expert", swap_pair)
-    keep = across(keep)
-    both = jnp.sum(keep.astype(F32), axis=0) + taken.astype(F32)
+    both = sum(x.astype(F32) for x in kept) + taken.astype(F32)
     both = both.astype(BF).reshape(owners, 2, width)
     back = along(both).reshape(2 * owners, width)
     return mixed_of(expert_ids, gate_codes, back, block)
+
+
+def ring_steps(parts):
+    return sorted(range(1, parts), key=lambda k: min(k, parts - k))
 
 
 def solution(mesh):

time: 190 us -> 195 us (1.026)
  blocking collectives: 132 us -> 114 us
  local copies, waits for them, and re-layouts: 1.72 us -> 14.6 us
  starting transfers between devices: 36.2 us -> 42.3 us
  waiting for transfers between devices: 8.71 us -> 11.5 us
    all_to_all x1 -> x0, blocking collectives: 14.2 us -> none  [across(): return lax.all_to_all(x, 'tensor', split_axis=0, concat_axis=0, tiled=True)]
    unnamed x8 -> x20, local copies, waits for them, and re-layouts: 1.51 us -> 13.2 us
    all_to_all x1 -> x2, waiting for transfers between devices: 6.85 us -> 0.87 us  [across(): return lax.all_to_all(x, 'tensor', split_axis=0, concat_axis=0, tiled=True)]
    all_to_all x1 -> x2, starting transfers between devices: 3.58 us -> 8.16 us  [across(): return lax.all_to_all(x, 'tensor', split_axis=0, concat_axis=0, tiled=True)]
    ppermute x1, waiting for transfers between devices: 1.84 us -> 5.17 us  [shards(): partner = lax.ppermute(arrived, 'expert', swap_pair)]
    ppermute x1, waiting for transfers between devices: 0.01 us -> 3.33 us  [shards(): taken = lax.ppermute(give, 'expert', swap_pair)]
    all_to_all x2, blocking collectives: 117 us -> 114 us  [along(): return lax.all_to_all(x, 'expert', split_axis=0, concat_axis=0, tiled=True)]
    ppermute x6, waiting for transfers between devices: 0.02 us -> 2.11 us  [turned(): lax.ppermute(x, 'tensor', [(i, (i + k) % parts) for i in range(parts)])]
  transfers between devices with their start and end apart: 12 -> 13, of which waited for: 2 -> 4; matrix products, arithmetic and copies ran while one was open for 0% -> 1% of each run, Pallas kernels for 3% -> 2%
where the time goes in v4:
time: 195 us; the launch traced here: 194 us
  blocking collectives  114 us (58%)
  starting transfers between devices  42.3 us (22%)
  local copies, waits for them, and re-layouts  14.6 us (7%)
  waiting for transfers between devices  11.5 us (6%)
  Pallas kernels  10.6 us (5%)
    all_to_all x2, blocking collectives, along(): return lax.all_to_all(x, 'expert', split_axis=0, concat_axis=0, tiled=True)  114 us
    ppermute x6, starting transfers between devices, turned(): lax.ppermute(x, 'tensor', [(i, (i + k) % parts) for i in range(parts)])  23.3 us
    unnamed x20, local copies, waits for them, and re-layouts  13.2 us
    all_to_all x2, starting transfers between devices, across(): return lax.all_to_all(x, 'tensor', split_axis=0, concat_axis=0, tiled=True)  8.16 us
    ppermute x3, starting transfers between devices, shards(): other = [lax.ppermute(w, 'sub', swap_sub) for w in own]  6.34 us
    ppermute x1, waiting for transfers between devices, shards(): partner = lax.ppermute(arrived, 'expert', swap_pair)  5.17 us
    pallas_call x1, Pallas kernels, experts_of(): pl.pallas_call(expert_kernel, out_shape=(jax.ShapeDtypeStruct((parts, *on...  4.03 us
  transfers between devices with their start and end apart: 13, of which 4 were waited for; matrix products, arithmetic and copies ran while one was open for 1% of the time, Pallas kernels for 2%

profile of v4, /device:TPU:40, one launch (start us, length us, event | category | flops | bytes accessed | tf_op | source)
XLA Modules:
  0.0 193.8 jit_solution(426432289532465859)
XLA Ops:
  0.0 1.9 %collective-permute-start.4 = (bf16[128,7168]{1,0:T(8,128)(2,1)}, bf16[128,7168]{1,0:T(8,128)(2,1)S(1)}, u32[]{:S(2)}, u32[]{:S(2)}) collective-permute-start(bf16[128,7168]{1,0:T(8,128)(2,1)} %bitcast.5), channel_id=1, source_target_pairs={{0,1},{1,0},{2,3},{3,2},{4,5},{5,4},{6,7},{7,6},{8,9},{9,8},{10,11... | collective-permute-start | bytes 5505032 | tf_op jit(solution)/shard_map/ppermute | solution.py:256
  1.9 2.4 %collective-permute-start.5 = (bf16[128,7168]{1,0:T(8,128)(2,1)}, bf16[128,7168]{1,0:T(8,128)(2,1)}, u32[]{:S(2)}, u32[]{:S(2)}) collective-permute-start(bf16[128,7168]{1,0:T(8,128)(2,1)} %bitcast.7), channel_id=1, source_target_pairs={{0,1},{1,0},{2,3},{3,2},{4,5},{5,4},{6,7},{7,6},{8,9},{9,8},{10,11... | collective-permute-start | bytes 5505032 | tf_op jit(solution)/shard_map/ppermute | solution.py:256
  4.4 2.0 %collective-permute-start.6 = (bf16[128,7168]{1,0:T(8,128)(2,1)}, bf16[128,7168]{1,0:T(8,128)(2,1)}, u32[]{:S(2)}, u32[]{:S(2)}) collective-permute-start(bf16[128,7168]{1,0:T(8,128)(2,1)} %bitcast.9), channel_id=1, source_target_pairs={{0,1},{1,0},{2,3},{3,2},{4,5},{5,4},{6,7},{7,6},{8,9},{9,8},{10,11... | collective-permute-start | bytes 5505032 | tf_op jit(solution)/shard_map/ppermute | solution.py:256
  6.4 0.8 copy-done.6
  7.2 0.7 copy-done.7
  7.9 1.0 pack.1
  9.0 81.1 %all_to_all.20 = bf16[32,2,1408]{2,1,0:T(2,128)(2,1)S(1)} all-to-all(bf16[32,2,1408]{2,1,0:T(2,128)(2,1)S(1)} %reshape.18), channel_id=1, replica_groups=mesh['group'=2,'expert'=32,'tensor'=4,'sub'=2] {'expert'}, dimensions={0} | all-to-all | bytes 360448 | tf_op jit(solution)/shard_map/all_to_all | solution.py:253
  90.1 1.2 broadcast_in_dim.2
  91.3 4.6 %all-to-all-start.1 = ((bf16[4,32,2,1408]{3,2,1,0:T(2,128)(2,1)}), bf16[4,32,2,1408]{3,2,1,0:T(2,128)(2,1)S(1)}, u32[]{:S(2)}, u32[]{:S(2)}) async-start(bf16[4,32,2,1408]{3,2,1,0:T(2,128)(2,1)} %broadcast_in_dim.2), calls=%async_computation.1 | async-start | bytes 1441792 | tf_op jit(solution)/shard_map/all_to_all | solution.py:250
  95.9 2.2 %collective-permute-start = (bf16[32,2,1408]{2,1,0:T(2,128)(2,1)S(1)}, bf16[32,2,1408]{2,1,0:T(2,128)(2,1)S(1)}, u32[]{:S(2)}, u32[]{:S(2)}) collective-permute-start(bf16[32,2,1408]{2,1,0:T(2,128)(2,1)S(1)} %all_to_all.20), channel_id=1, source_target_pairs={{0,8},{8,0},{16,24},{24,16},{32,40},{40,32},{48,56},{56,48},{64,72... | collective-permute-start | bytes 540680 | tf_op jit(solution)/shard_map/ppermute | solution.py:260
  98.1 5.2 %collective-permute-done.refs_1_ = bf16[32,2,1408]{2,1,0:T(2,128)(2,1)S(1)} collective-permute-done((bf16[32,2,1408]{2,1,0:T(2,128)(2,1)S(1)}, bf16[32,2,1408]{2,1,0:T(2,128)(2,1)S(1)}, u32[]{:S(2)}, u32[]{:S(2)}) %collective-permute-start) | collective-permute-done | bytes 180256 | tf_op jit(solution)/shard_map/ppermute | solution.py:260
  103.3 4.0 %collective-permute-start.1 = (bf16[32,2,1408]{2,1,0:T(2,128)(2,1)S(1)}, bf16[32,2,1408]{2,1,0:T(2,128)(2,1)S(1)}, u32[]{:S(2)}, u32[]{:S(2)}) collective-permute-start(bf16[32,2,1408]{2,1,0:T(2,128)(2,1)S(1)} %collective-permute-done.refs_1_), channel_id=1, source_target_pairs={{0,2},{2,4},{4,6},{6,0},{1,3},{3,5},{5,7},{7,1},{8,10},{10,12},{12... | collective-permute-start | bytes 540680 | tf_op jit(solution)/shard_map/ppermute | solution.py:247
  107.3 4.6 %collective-permute-start.2 = (bf16[32,2,1408]{2,1,0:T(2,128)(2,1)S(1)}, bf16[32,2,1408]{2,1,0:T(2,128)(2,1)S(1)}, u32[]{:S(2)}, u32[]{:S(2)}) collective-permute-start(bf16[32,2,1408]{2,1,0:T(2,128)(2,1)S(1)} %collective-permute-done.refs_1_), channel_id=1, source_target_pairs={{0,4},{2,6},{4,0},{6,2},{1,5},{3,7},{5,1},{7,3},{8,12},{10,14},{12... | collective-permute-start | bytes 540680 | tf_op jit(solution)/shard_map/ppermute | solution.py:247
  111.9 3.4 %collective-permute-start.3 = (bf16[32,2,1408]{2,1,0:T(2,128)(2,1)S(1)}, bf16[32,2,1408]{2,1,0:T(2,128)(2,1)S(1)}, u32[]{:S(2)}, u32[]{:S(2)}) collective-permute-start(bf16[32,2,1408]{2,1,0:T(2,128)(2,1)S(1)} %collective-permute-done.refs_1_), channel_id=1, source_target_pairs={{0,6},{2,0},{4,2},{6,4},{1,7},{3,1},{5,3},{7,5},{8,14},{10,8},{12,... | collective-permute-start | bytes 540680 | tf_op jit(solution)/shard_map/ppermute | solution.py:247
  115.3 3.8 %fetch.1 = (bf16[256,7168]{1,0:T(8,128)(2,1)S(1)}, bf16[256,7168]{1,0:T(8,128)(2,1)S(1)}, bf16[256,7168]{1,0:T(8,128)(2,1)S(1)}) custom-call(bf16[128,7168]{1,0:T(8,128)(2,1)} %bitcast.6, bf16[128,7168]{1,0:T(8,128)(2,1)} %bitcast.8, bf16[128,7168]{1,0:T(8,128)(2,1)} %bitcast.10, bf16[128,7168]{1,0:T(8,128)(2,1)S(1)} %collective-permute-done.4.g1, ...), custom_call_target="tpu_custom_call" | custom-call | flops 2818572288 | bytes 22020096 | tf_op jit(solution)/shard_map/fetch/pallas_call | solution.py:135
  119.1 1.8 copy-done
  120.9 1.8 copy-done.2
  122.7 1.9 copy-done.4
  124.7 2.0 %copy-done.1 = bf16[256,7168]{1,0:T(8,128)(2,1)S(1)} copy-done((bf16[256,7168]{1,0:T(8,128)(2,1)S(1)}, bf16[256,7168]{1,0:T(8,128)(2,1)}, u32[]{:S(2)}) %copy-start.1) | copy-done | bytes 3670040
  126.7 2.0 %copy-done.3 = bf16[256,7168]{1,0:T(8,128)(2,1)S(1)} copy-done((bf16[256,7168]{1,0:T(8,128)(2,1)S(1)}, bf16[256,7168]{1,0:T(8,128)(2,1)}, u32[]{:S(2)}) %copy-start.3) | copy-done | bytes 3670040
  128.8 2.0 %copy-done.5 = bf16[256,7168]{1,0:T(8,128)(2,1)S(1)} copy-done((bf16[256,7168]{1,0:T(8,128)(2,1)S(1)}, bf16[256,7168]{1,0:T(8,128)(2,1)}, u32[]{:S(2)}) %copy-start.5) | copy-done | bytes 3670040
  130.8 4.0 %experts.1 = (bf16[4,64,1408]{2,1,0:T(8,128)(2,1)}, bf16[64,1408]{1,0:T(8,128)(2,1)S(1)}, bf16[64,1408]{1,0:T(8,128)(2,1)S(1)}, bf16[64,1408]{1,0:T(8,128)(2,1)S(1)}, bf16[64,1408]{1,0:T(8,128)(2,1)S(1)}) custom-call(s32[1]{0:T(128)} %bitcast.refs_0_.here_ref, s32[1]{0:T(128)} %bitcast.1.odd_ref, bf16[4,32,2,1408]{3,2,1,0:T(2,128)(2,1)S(1)} %all-to-all-done.1.refs_0_, ...), custom_call_target="tpu_custom_call" | custom-call | flops 1409286144 | bytes 11010048 | tf_op jit(solution)/shard_map/experts/pallas_call | solution.py:216
  134.8 3.6 %all-to-all-start.2 = ((bf16[4,64,1408]{2,1,0:T(8,128)(2,1)}), bf16[4,64,1408]{2,1,0:T(8,128)(2,1)S(1)}, u32[]{:S(2)}, u32[]{:S(2)}) async-start(bf16[4,64,1408]{2,1,0:T(8,128)(2,1)} %get-tuple-element.20), calls=%async_computation.2 | async-start | bytes 1441792 | tf_op jit(solution)/shard_map/all_to_all | solution.py:250
  138.4 3.9 %collective-permute-start.7 = (bf16[64,1408]{1,0:T(8,128)(2,1)S(1)}, bf16[64,1408]{1,0:T(8,128)(2,1)S(1)}, u32[]{:S(2)}, u32[]{:S(2)}) collective-permute-start(bf16[64,1408]{1,0:T(8,128)(2,1)S(1)} %get-tuple-element.17), channel_id=1, source_target_pairs={{0,2},{2,4},{4,6},{6,0},{1,3},{3,5},{5,7},{7,1},{8,10},{10,12},{12... | collective-permute-start | bytes 540680 | tf_op jit(solution)/shard_map/ppermute | solution.py:247
  142.4 3.2 %collective-permute-start.8 = (bf16[64,1408]{1,0:T(8,128)(2,1)S(1)}, bf16[64,1408]{1,0:T(8,128)(2,1)S(1)}, u32[]{:S(2)}, u32[]{:S(2)}) collective-permute-start(bf16[64,1408]{1,0:T(8,128)(2,1)S(1)} %get-tuple-element.18), channel_id=1, source_target_pairs={{0,6},{2,0},{4,2},{6,4},{1,7},{3,1},{5,3},{7,5},{8,14},{10,8},{12,... | collective-permute-start | bytes 540680 | tf_op jit(solution)/shard_map/ppermute | solution.py:247
  145.6 4.2 %collective-permute-start.9 = (bf16[64,1408]{1,0:T(8,128)(2,1)S(1)}, bf16[64,1408]{1,0:T(8,128)(2,1)S(1)}, u32[]{:S(2)}, u32[]{:S(2)}) collective-permute-start(bf16[64,1408]{1,0:T(8,128)(2,1)S(1)} %get-tuple-element.19), channel_id=1, source_target_pairs={{0,4},{2,6},{4,0},{6,2},{1,5},{3,7},{5,1},{7,3},{8,12},{10,14},{12... | collective-permute-start | bytes 540680 | tf_op jit(solution)/shard_map/ppermute | solution.py:247
  149.8 0.9 all-to-all-done.2
  150.8 2.2 %collective-permute-start.10 = (bf16[64,1408]{1,0:T(8,128)(2,1)S(1)}, bf16[64,1408]{1,0:T(8,128)(2,1)S(1)}, u32[]{:S(2)}, u32[]{:S(2)}) collective-permute-start(bf16[64,1408]{1,0:T(8,128)(2,1)S(1)} %reduce_sum.12), channel_id=1, source_target_pairs={{0,8},{8,0},{16,24},{24,16},{32,40},{40,32},{48,56},{56,48},{64,72... | collective-permute-start | bytes 540680 | tf_op jit(solution)/shard_map/ppermute | solution.py:272
  153.1 2.1 %collective-permute-done.9 = bf16[64,1408]{1,0:T(8,128)(2,1)S(1)} collective-permute-done((bf16[64,1408]{1,0:T(8,128)(2,1)S(1)}, bf16[64,1408]{1,0:T(8,128)(2,1)S(1)}, u32[]{:S(2)}, u32[]{:S(2)}) %collective-permute-start.9) | collective-permute-done | bytes 180256 | tf_op jit(solution)/shard_map/ppermute | solution.py:247
  155.2 3.3 %collective-permute-done.10 = bf16[64,1408]{1,0:T(8,128)(2,1)S(1)} collective-permute-done((bf16[64,1408]{1,0:T(8,128)(2,1)S(1)}, bf16[64,1408]{1,0:T(8,128)(2,1)S(1)}, u32[]{:S(2)}, u32[]{:S(2)}) %collective-permute-start.10) | collective-permute-done | bytes 180256 | tf_op jit(solution)/shard_map/ppermute | solution.py:272
  158.7 33.2 %all_to_all.21 = bf16[32,2,1408]{2,1,0:T(2,128)(2,1)S(1)} all-to-all(bf16[32,2,1408]{2,1,0:T(2,128)(2,1)S(1)} %reshape.19), channel_id=1, replica_groups=mesh['group'=2,'expert'=32,'tensor'=4,'sub'=2] {'expert'}, dimensions={0} | all-to-all | bytes 360448 | tf_op jit(solution)/shard_map/all_to_all | solution.py:253
  192.0 1.8 mix.1
  (26 shorter events, 0.5 us)
Async XLA Ops:
  0.0 111.9 %collective-permute-start.4 = (bf16[128,7168]{1,0:T(8,128)(2,1)}, bf16[128,7168]{1,0:T(8,128)(2,1)S(1)}, u32[]{:S(2)}, u32[]{:S(2)}) collective-permute-start(bf16[128,7168]{1,0:T(8,128)(2,1)} %bitcast.5), channel_id=1, source_target_pairs={{0,1},{1,0},{2,3},{3,2},{4,5},{5,4},{6,7},{7,6},{8,9},{9,8},{10,11... | collective-permute-start | bytes 5505032 | tf_op jit(solution)/shard_map/ppermute | solution.py:256
  1.9 113.4 %collective-permute-start.5 = (bf16[128,7168]{1,0:T(8,128)(2,1)}, bf16[128,7168]{1,0:T(8,128)(2,1)}, u32[]{:S(2)}, u32[]{:S(2)}) collective-permute-start(bf16[128,7168]{1,0:T(8,128)(2,1)} %bitcast.7), channel_id=1, source_target_pairs={{0,1},{1,0},{2,3},{3,2},{4,5},{5,4},{6,7},{7,6},{8,9},{9,8},{10,11... | collective-permute-start | bytes 5505032 | tf_op jit(solution)/shard_map/ppermute | solution.py:256
  4.4 110.9 %collective-permute-start.6 = (bf16[128,7168]{1,0:T(8,128)(2,1)}, bf16[128,7168]{1,0:T(8,128)(2,1)}, u32[]{:S(2)}, u32[]{:S(2)}) collective-permute-start(bf16[128,7168]{1,0:T(8,128)(2,1)} %bitcast.9), channel_id=1, source_target_pairs={{0,1},{1,0},{2,3},{3,2},{4,5},{5,4},{6,7},{7,6},{8,9},{9,8},{10,11... | collective-permute-start | bytes 5505032 | tf_op jit(solution)/shard_map/ppermute | solution.py:256
  6.4 0.8 copy-start.6
  7.2 0.7 copy-start.7
  91.3 33.3 %all-to-all-start.1 = ((bf16[4,32,2,1408]{3,2,1,0:T(2,128)(2,1)}), bf16[4,32,2,1408]{3,2,1,0:T(2,128)(2,1)S(1)}, u32[]{:S(2)}, u32[]{:S(2)}) async-start(bf16[4,32,2,1408]{3,2,1,0:T(2,128)(2,1)} %broadcast_in_dim.2), calls=%async_computation.1 | async-start | bytes 1441792 | tf_op jit(solution)/shard_map/all_to_all | solution.py:250
  95.9 7.4 %collective-permute-start = (bf16[32,2,1408]{2,1,0:T(2,128)(2,1)S(1)}, bf16[32,2,1408]{2,1,0:T(2,128)(2,1)S(1)}, u32[]{:S(2)}, u32[]{:S(2)}) collective-permute-start(bf16[32,2,1408]{2,1,0:T(2,128)(2,1)S(1)} %all_to_all.20), channel_id=1, source_target_pairs={{0,8},{8,0},{16,24},{24,16},{32,40},{40,32},{48,56},{56,48},{64,72... | collective-permute-start | bytes 540680 | tf_op jit(solution)/shard_map/ppermute | solution.py:260
  103.3 21.3 %collective-permute-start.1 = (bf16[32,2,1408]{2,1,0:T(2,128)(2,1)S(1)}, bf16[32,2,1408]{2,1,0:T(2,128)(2,1)S(1)}, u32[]{:S(2)}, u32[]{:S(2)}) collective-permute-start(bf16[32,2,1408]{2,1,0:T(2,128)(2,1)S(1)} %collective-permute-done.refs_1_), channel_id=1, source_target_pairs={{0,2},{2,4},{4,6},{6,0},{1,3},{3,5},{5,7},{7,1},{8,10},{10,12},{12... | collective-permute-start | bytes 540680 | tf_op jit(solution)/shard_map/ppermute | solution.py:247
  107.3 17.4 %collective-permute-start.2 = (bf16[32,2,1408]{2,1,0:T(2,128)(2,1)S(1)}, bf16[32,2,1408]{2,1,0:T(2,128)(2,1)S(1)}, u32[]{:S(2)}, u32[]{:S(2)}) collective-permute-start(bf16[32,2,1408]{2,1,0:T(2,128)(2,1)S(1)} %collective-permute-done.refs_1_), channel_id=1, source_target_pairs={{0,4},{2,6},{4,0},{6,2},{1,5},{3,7},{5,1},{7,3},{8,12},{10,14},{12... | collective-permute-start | bytes 540680 | tf_op jit(solution)/shard_map/ppermute | solution.py:247
  111.9 12.8 %collective-permute-start.3 = (bf16[32,2,1408]{2,1,0:T(2,128)(2,1)S(1)}, bf16[32,2,1408]{2,1,0:T(2,128)(2,1)S(1)}, u32[]{:S(2)}, u32[]{:S(2)}) collective-permute-start(bf16[32,2,1408]{2,1,0:T(2,128)(2,1)S(1)} %collective-permute-done.refs_1_), channel_id=1, source_target_pairs={{0,6},{2,0},{4,2},{6,4},{1,7},{3,1},{5,3},{7,5},{8,14},{10,8},{12,... | collective-permute-start | bytes 540680 | tf_op jit(solution)/shard_map/ppermute | solution.py:247
  119.1 1.8 copy-start
  120.9 1.8 copy-start.2
  122.7 1.9 copy-start.4
  124.7 2.0 %copy-start.1 = (bf16[256,7168]{1,0:T(8,128)(2,1)S(1)}, bf16[256,7168]{1,0:T(8,128)(2,1)}, u32[]{:S(2)}) copy-start(bf16[256,7168]{1,0:T(8,128)(2,1)} %copy-done) | copy-start | bytes 11010052
  126.7 2.0 %copy-start.3 = (bf16[256,7168]{1,0:T(8,128)(2,1)S(1)}, bf16[256,7168]{1,0:T(8,128)(2,1)}, u32[]{:S(2)}) copy-start(bf16[256,7168]{1,0:T(8,128)(2,1)} %copy-done.2) | copy-start | bytes 11010052
  128.7 2.0 %copy-start.5 = (bf16[256,7168]{1,0:T(8,128)(2,1)S(1)}, bf16[256,7168]{1,0:T(8,128)(2,1)}, u32[]{:S(2)}) copy-start(bf16[256,7168]{1,0:T(8,128)(2,1)} %copy-done.4) | copy-start | bytes 11010052
  134.8 15.9 %all-to-all-start.2 = ((bf16[4,64,1408]{2,1,0:T(8,128)(2,1)}), bf16[4,64,1408]{2,1,0:T(8,128)(2,1)S(1)}, u32[]{:S(2)}, u32[]{:S(2)}) async-start(bf16[4,64,1408]{2,1,0:T(8,128)(2,1)} %get-tuple-element.20), calls=%async_computation.2 | async-start | bytes 1441792 | tf_op jit(solution)/shard_map/all_to_all | solution.py:250
  138.4 53.6 %copy-start.8 = (s32[4,8]{1,0:T(4,128)S(1)}, s32[4,8]{1,0:T(4,128)}, u32[]{:S(2)}) copy-start(s32[4,8]{1,0:T(4,128)} %ids_ref.1) | copy-start | bytes 388
  138.4 53.6 %copy-start.9 = (s32[4,8]{1,0:T(4,128)S(1)}, s32[4,8]{1,0:T(4,128)}, u32[]{:S(2)}) copy-start(s32[4,8]{1,0:T(4,128)} %code_ref.1) | copy-start | bytes 388
  138.4 14.6 %collective-permute-start.7 = (bf16[64,1408]{1,0:T(8,128)(2,1)S(1)}, bf16[64,1408]{1,0:T(8,128)(2,1)S(1)}, u32[]{:S(2)}, u32[]{:S(2)}) collective-permute-start(bf16[64,1408]{1,0:T(8,128)(2,1)S(1)} %get-tuple-element.17), channel_id=1, source_target_pairs={{0,2},{2,4},{4,6},{6,0},{1,3},{3,5},{5,7},{7,1},{8,10},{10,12},{12... | collective-permute-start | bytes 540680 | tf_op jit(solution)/shard_map/ppermute | solution.py:247
  142.4 10.7 %collective-permute-start.8 = (bf16[64,1408]{1,0:T(8,128)(2,1)S(1)}, bf16[64,1408]{1,0:T(8,128)(2,1)S(1)}, u32[]{:S(2)}, u32[]{:S(2)}) collective-permute-start(bf16[64,1408]{1,0:T(8,128)(2,1)S(1)} %get-tuple-element.18), channel_id=1, source_target_pairs={{0,6},{2,0},{4,2},{6,4},{1,7},{3,1},{5,3},{7,5},{8,14},{10,8},{12,... | collective-permute-start | bytes 540680 | tf_op jit(solution)/shard_map/ppermute | solution.py:247
  145.6 9.6 %collective-permute-start.9 = (bf16[64,1408]{1,0:T(8,128)(2,1)S(1)}, bf16[64,1408]{1,0:T(8,128)(2,1)S(1)}, u32[]{:S(2)}, u32[]{:S(2)}) collective-permute-start(bf16[64,1408]{1,0:T(8,128)(2,1)S(1)} %get-tuple-element.19), channel_id=1, source_target_pairs={{0,4},{2,6},{4,0},{6,2},{1,5},{3,7},{5,1},{7,3},{8,12},{10,14},{12... | collective-permute-start | bytes 540680 | tf_op jit(solution)/shard_map/ppermute | solution.py:247
  150.8 7.7 %collective-permute-start.10 = (bf16[64,1408]{1,0:T(8,128)(2,1)S(1)}, bf16[64,1408]{1,0:T(8,128)(2,1)S(1)}, u32[]{:S(2)}, u32[]{:S(2)}) collective-permute-start(bf16[64,1408]{1,0:T(8,128)(2,1)S(1)} %reduce_sum.12), channel_id=1, source_target_pairs={{0,8},{8,0},{16,24},{24,16},{32,40},{40,32},{48,56},{56,48},{64,72... | collective-permute-start | bytes 540680 | tf_op jit(solution)/shard_map/ppermute | solution.py:272

commit v5 on v4

v5 whole, which is shorter than its diff:
```python
import jax
import jax.numpy as jnp
from jax import lax
from jax.experimental import pallas as pl
from jax.experimental.pallas import tpu as pltpu
from jax.sharding import PartitionSpec as P

BF = jnp.bfloat16
F32 = jnp.float32
I32 = jnp.int32
VM = pl.BlockSpec(memory_space=pltpu.VMEM)
SM = pl.BlockSpec(memory_space=pltpu.SMEM)
ANY = pl.BlockSpec(memory_space=pl.ANY)
CONTRACT = (((1,), (1,)), ((), ()))
MIB = 1024 * 1024


def params(mib):
    return pltpu.CompilerParams(vmem_limit_bytes=mib * MIB)


def split_of(half):
    return -(-half // 256) * 128


def routing(ids_ref, rows, axis):
    shape = (rows, 1) if axis == 0 else (1, rows)
    row = lax.broadcasted_iota(I32, shape, axis)
    expert, side, part = row // 4, (row // 2) % 2, row % 2
    tokens, picks = ids_ref.shape
    count = jnp.zeros(shape, I32)
    out = []
    for t in range(tokens):
        hits = [(expert == ids_ref[t, j]).astype(I32) for j in range(picks)]
        named = sum(hits)
        first = named * (count == part).astype(I32)
        third = named * (count == 2).astype(I32)
        out.append((hits, first, third))
        count = count + named
    return out, side, part


def pack_kernel(here_ref, ids_hbm, tok_hbm, o_ref, ids_ref, tok_ref, sems):
    owners, _, width = o_ref.shape
    rows = 2 * owners
    block = tok_ref.shape[1]
    half = block // 2
    low = width - half
    start = pl.multiple_of(here_ref[0] * block, 128)
    take_ids = pltpu.make_async_copy(ids_hbm, ids_ref, sems.at[0])
    take_tok = pltpu.make_async_copy(tok_hbm.at[:, pl.ds(start, block)], tok_ref, sems.at[1])
    take_ids.start()
    take_tok.start()
    take_ids.wait()
    routes, side, part = routing(ids_ref, rows, 0)
    take_tok.wait()
    tok = tok_ref[...].astype(F32)
    main = jnp.zeros((rows, half), F32)
    tail = jnp.zeros((rows, low), F32)
    for t, (_, first, third) in enumerate(routes):
        for p in range(2):
            piece = tok[t : t + 1, p * half : (p + 1) * half]
            here = (side == p).astype(I32)
            main = main + (first * here).astype(F32) * piece
            rest = piece[:, low:]
            if 2 * low > half:
                rest = jnp.concatenate([rest, jnp.zeros((1, 2 * low - half), F32)], axis=1)
            third_here = third * here
            tail = tail + (third_here * (1 - part)).astype(F32) * piece[:, :low]
            tail = tail + (third_here * part).astype(F32) * rest
    o_ref[:, :, :half] = main.astype(BF).reshape(owners, 2, half)
    o_ref[:, :, half:] = tail.astype(BF).reshape(owners, 2, low)


def in_hbm(x):
    return pltpu.with_memory_space_constraint(x, pltpu.MemorySpace.HBM)


def packed_of(here, ids, tokens, owners, block):
    half = block // 2
    width = half + split_of(half)
    return pl.pallas_call(
        pack_kernel,
        out_shape=jax.ShapeDtypeStruct((owners, 2, width), BF),
        in_specs=[SM, ANY, ANY],
        out_specs=VM,
        scratch_shapes=[
            pltpu.SMEM(ids.shape, I32),
            pltpu.VMEM((tokens.shape[0], block), BF),
            pltpu.SemaphoreType.DMA((2,)),
        ],
        compiler_params=params(4),
        name="pack",
    )(here, in_hbm(ids), in_hbm(tokens))


def mix_kernel(ids_ref, code_ref, x_ref, o_ref):
    owners, _, width = x_ref.shape
    rows = 2 * owners
    tokens = o_ref.shape[0]
    half = o_ref.shape[1] // 2
    low = width - half
    routes, side, part = routing(ids_ref, rows, 1)
    mains, lowers, uppers = [], [], []
    for p in range(2):
        for t, (hits, first, third) in enumerate(routes):
            code = sum(hit * code_ref[t, j] for j, hit in enumerate(hits))
            code = code * (side == p).astype(I32)
            mains.append(first * code)
            lowers.append(third * (1 - part) * code)
            uppers.append(third * part * code)
    weights = (jnp.concatenate(mains + lowers + uppers, axis=0).astype(F32) / 64.0).astype(BF)
    x = x_ref[...].reshape(rows, width)
    r = jnp.dot(weights, x, preferred_element_type=F32)
    n = 2 * tokens
    for p in range(2):
        at, main = p * half, r[p * tokens : (p + 1) * tokens, :half]
        lower = r[n + p * tokens : n + (p + 1) * tokens, half:]
        upper = r[2 * n + p * tokens : 2 * n + (p + 1) * tokens, half : 2 * half - low]
        o_ref[:, at : at + low] = (main[:, :low] + lower).astype(BF)
        o_ref[:, at + low : at + half] = (main[:, low:] + upper).astype(BF)


def mixed_of(ids, codes, x, block):
    return pl.pallas_call(
        mix_kernel,
        out_shape=jax.ShapeDtypeStruct((ids.shape[0], block), BF),
        in_specs=[SM, SM, VM],
        out_specs=VM,
        compiler_params=params(4),
        name="mix",
    )(ids, codes, x)


def start_of(here, odd, parts, half, k, other, turned):
    side = 1 - odd if other else odd
    k = lax.rem(here + k, parts) if turned else k
    return pl.multiple_of((2 * k + side) * half, 128)


def halves_of(x, half):
    width = x.shape[-1]
    low = width - half
    x = x.reshape(-1, width)
    return (
        (0, low, jnp.concatenate([x[:, :low], x[:, half:]], axis=0)),
        (low, half - low, jnp.concatenate([x[:, low:half], x[:, half : 2 * half - low]], axis=0)),
    )


def add_in(sums, x, at, w_ref, half):
    return [
        total
        + lax.dot_general(
            lhs,
            w_ref[:, pl.ds(pl.multiple_of(at + lo, 128), size)],
            CONTRACT,
            preferred_element_type=F32,
        )
        for total, (lo, size, lhs) in zip(sums, halves_of(x, half))
    ]


def own_kernel(here_ref, odd_ref, own_ref, g0, u0, d0, g1, u1, d1, g_ref, u_ref, d_ref, s_ref, sems):
    parts, _, _, _ = own_ref.shape
    half = d_ref.shape[1] // (2 * parts)
    copies = []
    for i, (pair, dst) in enumerate((((g0, g1), g_ref), ((u0, u1), u_ref), ((d0, d1), d_ref))):
        for c, src in enumerate(pair):
            units = src.shape[0]
            rows = pl.ds(c * units, units)
            copies.append(pltpu.make_async_copy(src, dst.at[rows], sems.at[2 * i + c]))
    for copy in copies:
        copy.start()
    for i, w_ref in enumerate((g_ref, u_ref)):
        copies[2 * i].wait()
        copies[2 * i + 1].wait()
        sums = [jnp.zeros(s_ref.shape[1:], F32)] * 2
        for k in range(parts):
            at = start_of(here_ref[0], odd_ref[0], parts, half, k, False, False)
            sums = add_in(sums, own_ref[k], at, w_ref, half)
        s_ref[2 * i] = sums[0]
        s_ref[2 * i + 1] = sums[1]
    copies[4].wait()
    copies[5].wait()


def own_part(here, odd, own, mine, theirs):
    _, owners, _, _ = own.shape
    units, features = mine[0].shape
    shape = jax.ShapeDtypeStruct((2 * units, features), BF)
    return pl.pallas_call(
        own_kernel,
        out_shape=(shape,) * 3 + (jax.ShapeDtypeStruct((4, 4 * owners, 2 * units), F32),),
        in_specs=[SM, SM, VM] + [ANY] * 6,
        out_specs=(VM,) * 4,
        scratch_shapes=[pltpu.SemaphoreType.DMA((6,))],
        cost_estimate=pl.CostEstimate(
            flops=16 * owners * units * features,
            bytes_accessed=24 * units * features,
            transcendentals=0,
        ),
        compiler_params=params(16),
        name="ownpart",
    )(here, odd, own, *(in_hbm(w) for w in mine), *theirs)


def expert_kernel(here_ref, odd_ref, s_ref, *refs):
    parts = (len(refs) - 4) // 2
    pals, (g_ref, u_ref, d_ref, give_ref) = refs[:parts], refs[parts : parts + 4]
    keep_refs = refs[parts + 4 :]
    owners, _, width = pals[0].shape
    rows = 2 * owners
    half = d_ref.shape[1] // (2 * parts)
    low = width - half
    odd, here = odd_ref[0], here_ref[0]

    gates, ups = [s_ref[0], s_ref[1]], [s_ref[2], s_ref[3]]
    for i, x_ref in enumerate(pals):
        at = start_of(here, odd, parts, half, parts - i, True, True)
        gates = add_in(gates, x_ref[...], at, g_ref, half)
        ups = add_in(ups, x_ref[...], at, u_ref, half)

    def joined(a, b):
        third = a[rows:] + pltpu.roll(b[rows:], rows - 1, 0)
        return jnp.concatenate([a[:rows] + b[:rows], third], axis=0)

    gate, up = joined(*gates), joined(*ups)
    hidden = gate / (1.0 + jnp.exp(-gate)) * up
    third = hidden[rows:]
    even = lax.broadcasted_iota(I32, third.shape, 0) % 2 == 0
    lower = jnp.where(even, third, 0.0)
    upper = jnp.where(even, 0.0, pltpu.roll(third, 1, 0))
    lhs = (
        jnp.concatenate([hidden[:rows], lower], axis=0).astype(BF),
        jnp.concatenate([hidden[:rows], upper], axis=0).astype(BF),
    )
    for other in (True, False):
        for k in range(parts):
            at = start_of(here, odd, parts, half, k, other, not other)
            o_ref = give_ref.at[k] if other else keep_refs[k]
            a = jnp.dot(lhs[0], d_ref[:, pl.ds(at, low)], preferred_element_type=F32)
            cols = pl.ds(pl.multiple_of(at + low, 128), half - low)
            b = jnp.dot(lhs[1], d_ref[:, cols], preferred_element_type=F32)
            o_ref[:, :low] = a[:rows].astype(BF)
            o_ref[:, low:half] = b[:rows].astype(BF)
            o_ref[:, half : 2 * half - low] = (a[rows:, : half - low] + b[rows:]).astype(BF)
            if 2 * low > half:
                o_ref[:, 2 * half - low :] = a[rows:, half - low :].astype(BF)


def experts_of(here, odd, sums, pals, weights):
    parts = len(pals)
    owners, _, width = pals[0].shape
    units, features = weights[0].shape
    one = jax.ShapeDtypeStruct((2 * owners, width), BF)
    out = pl.pallas_call(
        expert_kernel,
        out_shape=(jax.ShapeDtypeStruct((parts, *one.shape), BF), *(one,) * parts),
        in_specs=[SM] * 2 + [VM] * (parts + 4),
        out_specs=(VM,) * (parts + 1),
        cost_estimate=pl.CostEstimate(
            flops=16 * owners * units * features,
            bytes_accessed=6 * units * features,
            transcendentals=4 * owners * units,
        ),
        compiler_params=params(24),
        name="experts",
    )(here, odd, sums, *pals, *weights)
    return out[0], out[1:]


def shards(tokens, expert_ids, gate_codes, w_gate, w_up, w_down):
    rows, features = tokens.shape
    owners = lax.axis_size("expert")
    subs = lax.axis_size("sub")
    parts = lax.axis_size("tensor")
    experts = owners // 2
    assert min(rows, rows * expert_ids.shape[1] // experts + 1) == 3
    block = features // parts
    here = lax.axis_index("tensor").reshape(1)
    odd = (lax.axis_index("expert") & 1).reshape(1)
    swap_sub = [(i, subs - 1 - i) for i in range(subs)]
    swap_pair = [(i, i ^ 1) for i in range(owners)]

    def turned(x, k):
        return lax.ppermute(x, "tensor", [(i, (i + k) % parts) for i in range(parts)])

    def across(x):
        return lax.all_to_all(x, "tensor", split_axis=0, concat_axis=0, tiled=True)

    def along(x):
        return lax.all_to_all(x, "expert", split_axis=0, concat_axis=0, tiled=True)

    own = (w_gate[0], w_up[0], w_down[0])
    other = [lax.ppermute(w, "sub", swap_sub) for w in own]
    packed = packed_of(here, expert_ids, tokens, owners, block)
    arrived = along(packed)
    partner = lax.ppermute(arrived, "expert", swap_pair)
    spread = jnp.broadcast_to(arrived[None], (parts, *arrived.shape))
    spread = across(spread)
    pals = [partner] + [None] * (parts - 1)
    for k in ring_steps(parts):
        pals[k] = turned(partner, k)
    *weights, sums = own_part(here, odd, spread, own, other)
    give, keep = experts_of(here, odd, sums, pals, weights)
    give = across(give)
    kept = [keep[0]]
    for k in ring_steps(parts):
        kept.append(turned(keep[k], k))
    give = jnp.sum(give.astype(F32), axis=0).astype(BF)
    taken = lax.ppermute(give, "expert", swap_pair)
    both = sum(x.astype(F32) for x in kept) + taken.astype(F32)
    both = both.astype(BF).reshape(arrived.shape)
    back = along(both)
    return mixed_of(expert_ids, gate_codes, back, block)


def ring_steps(parts):
    return sorted(range(1, parts), key=lambda k: min(k, parts - k))


def solution(mesh):
    spread = P(("group", "expert", "sub"), None)
    weights = P("expert", ("tensor", "sub"), None)
    return jax.shard_map(
        shards,
        mesh=mesh,
        in_specs=(spread, spread, spread, weights, weights, weights),
        out_specs=P(("group", "expert", "sub"), "tensor"),
        check_vma=False,
    )
```

time: 195 us -> 177 us (0.908)
  blocking collectives: 114 us -> 32.8 us
  starting transfers between devices: 42.3 us -> 88.5 us
  waiting for transfers between devices: 11.5 us -> 43.3 us
  local copies, waits for them, and re-layouts: 14.6 us -> 1.32 us
    all_to_all x2 -> x1, blocking collectives: 114 us -> 32.8 us  [along(): return lax.all_to_all(x, 'expert', split_axis=0, concat_axis=0, tiled=True)]
    all_to_all x0 -> x1, starting transfers between devices: none -> 45.8 us  [along(): return lax.all_to_all(x, 'expert', split_axis=0, concat_axis=0, tiled=True)]
    all_to_all x0 -> x1, waiting for transfers between devices: none -> 31.2 us  [along(): return lax.all_to_all(x, 'expert', split_axis=0, concat_axis=0, tiled=True)]
    unnamed x20 -> x4, local copies, waits for them, and re-layouts: 13.2 us -> 0.01 us
  transfers between devices with their start and end apart: 13 -> 14, of which waited for: 4 -> 6; matrix products, arithmetic and copies ran while one was open for 1% -> 1% of each run, Pallas kernels for 2% -> 3%
where the time goes in v5:
time: 177 us; the launch traced here: 176 us
  starting transfers between devices  88.5 us (50%)
  waiting for transfers between devices  43.3 us (24%)
  blocking collectives  32.8 us (19%)
  Pallas kernels  9.94 us (6%)
    all_to_all x1, starting transfers between devices, along(): return lax.all_to_all(x, 'expert', split_axis=0, concat_axis=0, tiled=True)  45.8 us
    all_to_all x1, blocking collectives, along(): return lax.all_to_all(x, 'expert', split_axis=0, concat_axis=0, tiled=True)  32.8 us
    all_to_all x1, waiting for transfers between devices, along(): return lax.all_to_all(x, 'expert', split_axis=0, concat_axis=0, tiled=True)  31.2 us
    ppermute x6, starting transfers between devices, turned(): lax.ppermute(x, 'tensor', [(i, (i + k) % parts) for i in range(parts)])  23.3 us
    all_to_all x2, starting transfers between devices, across(): return lax.all_to_all(x, 'tensor', split_axis=0, concat_axis=0, tiled=True)  8.64 us
    ppermute x3, starting transfers between devices, shards(): other = [lax.ppermute(w, 'sub', swap_sub) for w in own]  6.34 us
    ppermute x1, waiting for transfers between devices, shards(): partner = lax.ppermute(arrived, 'expert', swap_pair)  5.18 us
    pallas_call x1, Pallas kernels, own_part(): pl.pallas_call(own_kernel, out_shape=(shape,) * 3 + (jax.ShapeDtypeStruct...  3.76 us
  transfers between devices with their start and end apart: 14, of which 6 were waited for; matrix products, arithmetic and copies ran while one was open for 1% of the time, Pallas kernels for 3%

profile of v5, /device:TPU:40, one launch (start us, length us, event | category | flops | bytes accessed | tf_op | source)
XLA Modules:
  0.0 176.2 jit_solution(14719082492852051075)
XLA Ops:
  0.0 1.9 %collective-permute-start = (bf16[128,7168]{1,0:T(8,128)(2,1)}, bf16[128,7168]{1,0:T(8,128)(2,1)S(1)}, u32[]{:S(2)}, u32[]{:S(2)}) collective-permute-start(bf16[128,7168]{1,0:T(8,128)(2,1)} %bitcast.5), channel_id=1, source_target_pairs={{0,1},{1,0},{2,3},{3,2},{4,5},{5,4},{6,7},{7,6},{8,9},{9,8},{10,11... | collective-permute-start | bytes 5505032 | tf_op jit(solution)/shard_map/ppermute | solution.py:296
  2.0 1.9 %pack.1 = bf16[32,2,1408]{2,1,0:T(2,128)(2,1)} custom-call(s32[1]{0:T(128)} %bitcast.here_ref, s32[4,8]{1,0:T(4,128)} %ids_ref.1, bf16[4,7168]{1,0:T(4,128)(2,1)} %tok_hbm.1), custom_call_target="tpu_custom_call" | custom-call | tf_op jit(solution)/shard_map/pack/pallas_call | solution.py:82
  3.8 45.8 %all-to-all-start = ((bf16[32,2,1408]{2,1,0:T(2,128)(2,1)}), bf16[32,2,1408]{2,1,0:T(2,128)(2,1)S(1)}, u32[]{:S(2)}, u32[]{:S(2)}) async-start(bf16[32,2,1408]{2,1,0:T(2,128)(2,1)} %pack.1), calls=%async_computation | async-start | bytes 360448 | tf_op jit(solution)/shard_map/all_to_all | solution.py:293
  49.6 2.2 %collective-permute-start.1 = (bf16[128,7168]{1,0:T(8,128)(2,1)}, bf16[128,7168]{1,0:T(8,128)(2,1)}, u32[]{:S(2)}, u32[]{:S(2)}) collective-permute-start(bf16[128,7168]{1,0:T(8,128)(2,1)} %bitcast.7), channel_id=1, source_target_pairs={{0,1},{1,0},{2,3},{3,2},{4,5},{5,4},{6,7},{7,6},{8,9},{9,8},{10,11... | collective-permute-start | bytes 5505032 | tf_op jit(solution)/shard_map/ppermute | solution.py:296
  51.8 2.2 %collective-permute-start.2 = (bf16[128,7168]{1,0:T(8,128)(2,1)}, bf16[128,7168]{1,0:T(8,128)(2,1)}, u32[]{:S(2)}, u32[]{:S(2)}) collective-permute-start(bf16[128,7168]{1,0:T(8,128)(2,1)} %bitcast.9), channel_id=1, source_target_pairs={{0,1},{1,0},{2,3},{3,2},{4,5},{5,4},{6,7},{7,6},{8,9},{9,8},{10,11... | collective-permute-start | bytes 5505032 | tf_op jit(solution)/shard_map/ppermute | solution.py:296
  54.0 31.2 %all-to-all-done = bf16[32,2,1408]{2,1,0:T(2,128)(2,1)S(1)} async-done(((bf16[32,2,1408]{2,1,0:T(2,128)(2,1)}), bf16[32,2,1408]{2,1,0:T(2,128)(2,1)S(1)}, u32[]{:S(2)}, u32[]{:S(2)}) %all-to-all-start) | async-done | bytes 180256 | tf_op jit(solution)/shard_map/all_to_all | solution.py:293
  85.2 1.2 broadcast_in_dim.2
  86.4 4.6 %all-to-all-start.1 = ((bf16[4,32,2,1408]{3,2,1,0:T(2,128)(2,1)}), bf16[4,32,2,1408]{3,2,1,0:T(2,128)(2,1)S(1)}, u32[]{:S(2)}, u32[]{:S(2)}) async-start(bf16[4,32,2,1408]{3,2,1,0:T(2,128)(2,1)} %broadcast_in_dim.2), calls=%async_computation.1 | async-start | bytes 1441792 | tf_op jit(solution)/shard_map/all_to_all | solution.py:290
  91.0 2.2 %collective-permute-start.3 = (bf16[32,2,1408]{2,1,0:T(2,128)(2,1)S(1)}, bf16[32,2,1408]{2,1,0:T(2,128)(2,1)S(1)}, u32[]{:S(2)}, u32[]{:S(2)}) collective-permute-start(bf16[32,2,1408]{2,1,0:T(2,128)(2,1)S(1)} %all-to-all-done), channel_id=1, source_target_pairs={{0,8},{8,0},{16,24},{24,16},{32,40},{40,32},{48,56},{56,48},{64,72... | collective-permute-start | bytes 540680 | tf_op jit(solution)/shard_map/ppermute | solution.py:299
  93.2 5.2 %collective-permute-done.3.refs_0_ = bf16[32,2,1408]{2,1,0:T(2,128)(2,1)S(1)} collective-permute-done((bf16[32,2,1408]{2,1,0:T(2,128)(2,1)S(1)}, bf16[32,2,1408]{2,1,0:T(2,128)(2,1)S(1)}, u32[]{:S(2)}, u32[]{:S(2)}) %collective-permute-start.3) | collective-permute-done | bytes 180256 | tf_op jit(solution)/shard_map/ppermute | solution.py:299
  98.4 4.0 %collective-permute-start.4 = (bf16[32,2,1408]{2,1,0:T(2,128)(2,1)S(1)}, bf16[32,2,1408]{2,1,0:T(2,128)(2,1)S(1)}, u32[]{:S(2)}, u32[]{:S(2)}) collective-permute-start(bf16[32,2,1408]{2,1,0:T(2,128)(2,1)S(1)} %collective-permute-done.3.refs_0_), channel_id=1, source_target_pairs={{0,2},{2,4},{4,6},{6,0},{1,3},{3,5},{5,7},{7,1},{8,10},{10,12},{12... | collective-permute-start | bytes 540680 | tf_op jit(solution)/shard_map/ppermute | solution.py:287
  102.4 4.6 %collective-permute-start.5 = (bf16[32,2,1408]{2,1,0:T(2,128)(2,1)S(1)}, bf16[32,2,1408]{2,1,0:T(2,128)(2,1)S(1)}, u32[]{:S(2)}, u32[]{:S(2)}) collective-permute-start(bf16[32,2,1408]{2,1,0:T(2,128)(2,1)S(1)} %collective-permute-done.3.refs_0_), channel_id=1, source_target_pairs={{0,4},{2,6},{4,0},{6,2},{1,5},{3,7},{5,1},{7,3},{8,12},{10,14},{12... | collective-permute-start | bytes 540680 | tf_op jit(solution)/shard_map/ppermute | solution.py:287
  107.0 0.0 collective-permute-done.g1
  107.0 3.4 %collective-permute-start.6 = (bf16[32,2,1408]{2,1,0:T(2,128)(2,1)S(1)}, bf16[32,2,1408]{2,1,0:T(2,128)(2,1)S(1)}, u32[]{:S(2)}, u32[]{:S(2)}) collective-permute-start(bf16[32,2,1408]{2,1,0:T(2,128)(2,1)S(1)} %collective-permute-done.3.refs_0_), channel_id=1, source_target_pairs={{0,6},{2,0},{4,2},{6,4},{1,7},{3,1},{5,3},{7,5},{8,14},{10,8},{12,... | collective-permute-start | bytes 540680 | tf_op jit(solution)/shard_map/ppermute | solution.py:287
  110.4 0.0 collective-permute-done.2.d1
  110.4 0.0 all-to-all-done.1.own_ref
  110.5 3.8 %ownpart.1 = (bf16[256,7168]{1,0:T(8,128)(2,1)S(1)}, bf16[256,7168]{1,0:T(8,128)(2,1)S(1)}, bf16[256,7168]{1,0:T(8,128)(2,1)S(1)}, f32[4,128,256]{2,1,0:T(8,128)S(1)}) custom-call(s32[1]{0:T(128)} %bitcast.here_ref, s32[1]{0:T(128)} %bitcast.1.odd_ref, bf16[4,32,2,1408]{3,2,1,0:T(2,128)(2,1)S(1)} %all-to-all-done.1.own_ref, bf16[128,7168]{1,0:T(8,128)(2,1)} %bitcast.6, ...), custom_call_target="tpu_custom_call" | custom-call | flops 469762048 | bytes 22020096 | tf_op jit(solution)/shard_map/ownpart/pallas_call | solution.py:192
  114.2 0.2 collective-permute-done.6.refs_3_
  114.4 2.9 %experts.1 = (bf16[4,64,1408]{2,1,0:T(8,128)(2,1)}, bf16[64,1408]{1,0:T(8,128)(2,1)S(1)}, bf16[64,1408]{1,0:T(8,128)(2,1)S(1)}, bf16[64,1408]{1,0:T(8,128)(2,1)S(1)}, bf16[64,1408]{1,0:T(8,128)(2,1)S(1)}) custom-call(s32[1]{0:T(128)} %bitcast.here_ref, s32[1]{0:T(128)} %bitcast.1.odd_ref, f32[4,128,256]{2,1,0:T(8,128)S(1)} %get-tuple-element.14.s_ref, ...), custom_call_target="tpu_custom_call" | custom-call | flops 939524096 | bytes 11010048 | tf_op jit(solution)/shard_map/experts/pallas_call | solution.py:257
  117.3 4.1 %all-to-all-start.2 = ((bf16[4,64,1408]{2,1,0:T(8,128)(2,1)}), bf16[4,64,1408]{2,1,0:T(8,128)(2,1)S(1)}, u32[]{:S(2)}, u32[]{:S(2)}) async-start(bf16[4,64,1408]{2,1,0:T(8,128)(2,1)} %get-tuple-element.22), calls=%async_computation.2 | async-start | bytes 1441792 | tf_op jit(solution)/shard_map/all_to_all | solution.py:290
  121.4 4.0 %collective-permute-start.7 = (bf16[64,1408]{1,0:T(8,128)(2,1)S(1)}, bf16[64,1408]{1,0:T(8,128)(2,1)S(1)}, u32[]{:S(2)}, u32[]{:S(2)}) collective-permute-start(bf16[64,1408]{1,0:T(8,128)(2,1)S(1)} %get-tuple-element.19), channel_id=1, source_target_pairs={{0,2},{2,4},{4,6},{6,0},{1,3},{3,5},{5,7},{7,1},{8,10},{10,12},{12... | collective-permute-start | bytes 540680 | tf_op jit(solution)/shard_map/ppermute | solution.py:287
  125.4 3.2 %collective-permute-start.8 = (bf16[64,1408]{1,0:T(8,128)(2,1)S(1)}, bf16[64,1408]{1,0:T(8,128)(2,1)S(1)}, u32[]{:S(2)}, u32[]{:S(2)}) collective-permute-start(bf16[64,1408]{1,0:T(8,128)(2,1)S(1)} %get-tuple-element.20), channel_id=1, source_target_pairs={{0,6},{2,0},{4,2},{6,4},{1,7},{3,1},{5,3},{7,5},{8,14},{10,8},{12,... | collective-permute-start | bytes 540680 | tf_op jit(solution)/shard_map/ppermute | solution.py:287
  128.5 4.2 %collective-permute-start.9 = (bf16[64,1408]{1,0:T(8,128)(2,1)S(1)}, bf16[64,1408]{1,0:T(8,128)(2,1)S(1)}, u32[]{:S(2)}, u32[]{:S(2)}) collective-permute-start(bf16[64,1408]{1,0:T(8,128)(2,1)S(1)} %get-tuple-element.21), channel_id=1, source_target_pairs={{0,4},{2,6},{4,0},{6,2},{1,5},{3,7},{5,1},{7,3},{8,12},{10,14},{12... | collective-permute-start | bytes 540680 | tf_op jit(solution)/shard_map/ppermute | solution.py:287
  132.8 1.1 all-to-all-done.2
  133.8 0.1 reduce_sum.12
  134.0 2.2 %collective-permute-start.10 = (bf16[64,1408]{1,0:T(8,128)(2,1)S(1)}, bf16[64,1408]{1,0:T(8,128)(2,1)S(1)}, u32[]{:S(2)}, u32[]{:S(2)}) collective-permute-start(bf16[64,1408]{1,0:T(8,128)(2,1)S(1)} %reduce_sum.12), channel_id=1, source_target_pairs={{0,8},{8,0},{16,24},{24,16},{32,40},{40,32},{48,56},{56,48},{64,72... | collective-permute-start | bytes 540680 | tf_op jit(solution)/shard_map/ppermute | solution.py:312
  136.2 2.1 %collective-permute-done.9 = bf16[64,1408]{1,0:T(8,128)(2,1)S(1)} collective-permute-done((bf16[64,1408]{1,0:T(8,128)(2,1)S(1)}, bf16[64,1408]{1,0:T(8,128)(2,1)S(1)}, u32[]{:S(2)}, u32[]{:S(2)}) %collective-permute-start.9) | collective-permute-done | bytes 180256 | tf_op jit(solution)/shard_map/ppermute | solution.py:287
  138.3 3.6 %collective-permute-done.10 = bf16[64,1408]{1,0:T(8,128)(2,1)S(1)} collective-permute-done((bf16[64,1408]{1,0:T(8,128)(2,1)S(1)}, bf16[64,1408]{1,0:T(8,128)(2,1)S(1)}, u32[]{:S(2)}, u32[]{:S(2)}) %collective-permute-start.10) | collective-permute-done | bytes 180256 | tf_op jit(solution)/shard_map/ppermute | solution.py:312
  141.9 0.1 add_convert_fusion
  142.0 0.1 reshape.12
  142.1 32.8 %all_to_all.20.x_ref = bf16[32,2,1408]{2,1,0:T(2,128)(2,1)S(1)} all-to-all(bf16[32,2,1408]{2,1,0:T(2,128)(2,1)S(1)} %reshape.12), channel_id=1, replica_groups=mesh['group'=2,'expert'=32,'tensor'=4,'sub'=2] {'expert'}, dimensions={0} | all-to-all | bytes 360448 | tf_op jit(solution)/shard_map/all_to_all | solution.py:293
  174.8 1.4 mix.1
  (9 shorter events, 0.0 us)
Async XLA Ops:
  0.0 107.0 %collective-permute-start = (bf16[128,7168]{1,0:T(8,128)(2,1)}, bf16[128,7168]{1,0:T(8,128)(2,1)S(1)}, u32[]{:S(2)}, u32[]{:S(2)}) collective-permute-start(bf16[128,7168]{1,0:T(8,128)(2,1)} %bitcast.5), channel_id=1, source_target_pairs={{0,1},{1,0},{2,3},{3,2},{4,5},{5,4},{6,7},{7,6},{8,9},{9,8},{10,11... | collective-permute-start | bytes 5505032 | tf_op jit(solution)/shard_map/ppermute | solution.py:296
  3.8 81.4 %all-to-all-start = ((bf16[32,2,1408]{2,1,0:T(2,128)(2,1)}), bf16[32,2,1408]{2,1,0:T(2,128)(2,1)S(1)}, u32[]{:S(2)}, u32[]{:S(2)}) async-start(bf16[32,2,1408]{2,1,0:T(2,128)(2,1)} %pack.1), calls=%async_computation | async-start | bytes 360448 | tf_op jit(solution)/shard_map/all_to_all | solution.py:293
  49.6 60.8 %collective-permute-start.1 = (bf16[128,7168]{1,0:T(8,128)(2,1)}, bf16[128,7168]{1,0:T(8,128)(2,1)}, u32[]{:S(2)}, u32[]{:S(2)}) collective-permute-start(bf16[128,7168]{1,0:T(8,128)(2,1)} %bitcast.7), channel_id=1, source_target_pairs={{0,1},{1,0},{2,3},{3,2},{4,5},{5,4},{6,7},{7,6},{8,9},{9,8},{10,11... | collective-permute-start | bytes 5505032 | tf_op jit(solution)/shard_map/ppermute | solution.py:296
  51.8 58.7 %collective-permute-start.2 = (bf16[128,7168]{1,0:T(8,128)(2,1)}, bf16[128,7168]{1,0:T(8,128)(2,1)}, u32[]{:S(2)}, u32[]{:S(2)}) collective-permute-start(bf16[128,7168]{1,0:T(8,128)(2,1)} %bitcast.9), channel_id=1, source_target_pairs={{0,1},{1,0},{2,3},{3,2},{4,5},{5,4},{6,7},{7,6},{8,9},{9,8},{10,11... | collective-permute-start | bytes 5505032 | tf_op jit(solution)/shard_map/ppermute | solution.py:296
  86.4 24.0 %all-to-all-start.1 = ((bf16[4,32,2,1408]{3,2,1,0:T(2,128)(2,1)}), bf16[4,32,2,1408]{3,2,1,0:T(2,128)(2,1)S(1)}, u32[]{:S(2)}, u32[]{:S(2)}) async-start(bf16[4,32,2,1408]{3,2,1,0:T(2,128)(2,1)} %broadcast_in_dim.2), calls=%async_computation.1 | async-start | bytes 1441792 | tf_op jit(solution)/shard_map/all_to_all | solution.py:290
  91.0 7.4 %collective-permute-start.3 = (bf16[32,2,1408]{2,1,0:T(2,128)(2,1)S(1)}, bf16[32,2,1408]{2,1,0:T(2,128)(2,1)S(1)}, u32[]{:S(2)}, u32[]{:S(2)}) collective-permute-start(bf16[32,2,1408]{2,1,0:T(2,128)(2,1)S(1)} %all-to-all-done), channel_id=1, source_target_pairs={{0,8},{8,0},{16,24},{24,16},{32,40},{40,32},{48,56},{56,48},{64,72... | collective-permute-start | bytes 540680 | tf_op jit(solution)/shard_map/ppermute | solution.py:299
  98.4 15.8 %collective-permute-start.4 = (bf16[32,2,1408]{2,1,0:T(2,128)(2,1)S(1)}, bf16[32,2,1408]{2,1,0:T(2,128)(2,1)S(1)}, u32[]{:S(2)}, u32[]{:S(2)}) collective-permute-start(bf16[32,2,1408]{2,1,0:T(2,128)(2,1)S(1)} %collective-permute-done.3.refs_0_), channel_id=1, source_target_pairs={{0,2},{2,4},{4,6},{6,0},{1,3},{3,5},{5,7},{7,1},{8,10},{10,12},{12... | collective-permute-start | bytes 540680 | tf_op jit(solution)/shard_map/ppermute | solution.py:287
  102.4 11.9 %collective-permute-start.5 = (bf16[32,2,1408]{2,1,0:T(2,128)(2,1)S(1)}, bf16[32,2,1408]{2,1,0:T(2,128)(2,1)S(1)}, u32[]{:S(2)}, u32[]{:S(2)}) collective-permute-start(bf16[32,2,1408]{2,1,0:T(2,128)(2,1)S(1)} %collective-permute-done.3.refs_0_), channel_id=1, source_target_pairs={{0,4},{2,6},{4,0},{6,2},{1,5},{3,7},{5,1},{7,3},{8,12},{10,14},{12... | collective-permute-start | bytes 540680 | tf_op jit(solution)/shard_map/ppermute | solution.py:287
  107.0 7.4 %collective-permute-start.6 = (bf16[32,2,1408]{2,1,0:T(2,128)(2,1)S(1)}, bf16[32,2,1408]{2,1,0:T(2,128)(2,1)S(1)}, u32[]{:S(2)}, u32[]{:S(2)}) collective-permute-start(bf16[32,2,1408]{2,1,0:T(2,128)(2,1)S(1)} %collective-permute-done.3.refs_0_), channel_id=1, source_target_pairs={{0,6},{2,0},{4,2},{6,4},{1,7},{3,1},{5,3},{7,5},{8,14},{10,8},{12,... | collective-permute-start | bytes 540680 | tf_op jit(solution)/shard_map/ppermute | solution.py:287
  117.3 57.5 %copy-start = (s32[4,8]{1,0:T(4,128)S(1)}, s32[4,8]{1,0:T(4,128)}, u32[]{:S(2)}) copy-start(s32[4,8]{1,0:T(4,128)} %ids_ref.1) | copy-start | bytes 388
  117.3 57.5 %copy-start.1 = (s32[4,8]{1,0:T(4,128)S(1)}, s32[4,8]{1,0:T(4,128)}, u32[]{:S(2)}) copy-start(s32[4,8]{1,0:T(4,128)} %code_ref.1) | copy-start | bytes 388
  117.3 16.5 %all-to-all-start.2 = ((bf16[4,64,1408]{2,1,0:T(8,128)(2,1)}), bf16[4,64,1408]{2,1,0:T(8,128)(2,1)S(1)}, u32[]{:S(2)}, u32[]{:S(2)}) async-start(bf16[4,64,1408]{2,1,0:T(8,128)(2,1)} %get-tuple-element.22), calls=%async_computation.2 | async-start | bytes 1441792 | tf_op jit(solution)/shard_map/all_to_all | solution.py:290
  121.4 14.8 %collective-permute-start.7 = (bf16[64,1408]{1,0:T(8,128)(2,1)S(1)}, bf16[64,1408]{1,0:T(8,128)(2,1)S(1)}, u32[]{:S(2)}, u32[]{:S(2)}) collective-permute-start(bf16[64,1408]{1,0:T(8,128)(2,1)S(1)} %get-tuple-element.19), channel_id=1, source_target_pairs={{0,2},{2,4},{4,6},{6,0},{1,3},{3,5},{5,7},{7,1},{8,10},{10,12},{12... | collective-permute-start | bytes 540680 | tf_op jit(solution)/shard_map/ppermute | solution.py:287
  125.4 10.8 %collective-permute-start.8 = (bf16[64,1408]{1,0:T(8,128)(2,1)S(1)}, bf16[64,1408]{1,0:T(8,128)(2,1)S(1)}, u32[]{:S(2)}, u32[]{:S(2)}) collective-permute-start(bf16[64,1408]{1,0:T(8,128)(2,1)S(1)} %get-tuple-element.20), channel_id=1, source_target_pairs={{0,6},{2,0},{4,2},{6,4},{1,7},{3,1},{5,3},{7,5},{8,14},{10,8},{12,... | collective-permute-start | bytes 540680 | tf_op jit(solution)/shard_map/ppermute | solution.py:287
  128.5 9.7 %collective-permute-start.9 = (bf16[64,1408]{1,0:T(8,128)(2,1)S(1)}, bf16[64,1408]{1,0:T(8,128)(2,1)S(1)}, u32[]{:S(2)}, u32[]{:S(2)}) collective-permute-start(bf16[64,1408]{1,0:T(8,128)(2,1)S(1)} %get-tuple-element.21), channel_id=1, source_target_pairs={{0,4},{2,6},{4,0},{6,2},{1,5},{3,7},{5,1},{7,3},{8,12},{10,14},{12... | collective-permute-start | bytes 540680 | tf_op jit(solution)/shard_map/ppermute | solution.py:287
  134.0 7.9 %collective-permute-start.10 = (bf16[64,1408]{1,0:T(8,128)(2,1)S(1)}, bf16[64,1408]{1,0:T(8,128)(2,1)S(1)}, u32[]{:S(2)}, u32[]{:S(2)}) collective-permute-start(bf16[64,1408]{1,0:T(8,128)(2,1)S(1)} %reduce_sum.12), channel_id=1, source_target_pairs={{0,8},{8,0},{16,24},{24,16},{32,40},{40,32},{48,56},{56,48},{64,72... | collective-permute-start | bytes 540680 | tf_op jit(solution)/shard_map/ppermute | solution.py:312

commit v6 on v5

--- a/solution.py
+++ b/solution.py
@@ -132,9 +132,9 @@
     )(ids, codes, x)
 
 
-def start_of(here, odd, parts, half, k, other, turned):
+def start_of(here, odd, half, k, other, turned):
     side = 1 - odd if other else odd
-    k = lax.rem(here + k, parts) if turned else k
+    k = lax.bitwise_xor(here, jnp.int32(k)) if turned else k
     return pl.multiple_of((2 * k + side) * half, 128)
 
 
@@ -161,8 +161,9 @@
     ]
 
 
-def own_kernel(here_ref, odd_ref, own_ref, g0, u0, d0, g1, u1, d1, g_ref, u_ref, d_ref, s_ref, sems):
-    parts, _, _, _ = own_ref.shape
+def own_kernel(here_ref, odd_ref, *refs):
+    parts = len(refs) - 11
+    owns, (g0, u0, d0, g1, u1, d1, g_ref, u_ref, d_ref, s_ref, sems) = refs[:parts], refs[parts:]
     half = d_ref.shape[1] // (2 * parts)
     copies = []
     for i, (pair, dst) in enumerate((((g0, g1), g_ref), ((u0, u1), u_ref), ((d0, d1), d_ref))):
@@ -177,22 +178,23 @@
         copies[2 * i + 1].wait()
         sums = [jnp.zeros(s_ref.shape[1:], F32)] * 2
         for k in range(parts):
-            at = start_of(here_ref[0], odd_ref[0], parts, half, k, False, False)
-            sums = add_in(sums, own_ref[k], at, w_ref, half)
+            at = start_of(here_ref[0], odd_ref[0], half, k, False, True)
+            sums = add_in(sums, owns[k][...], at, w_ref, half)
         s_ref[2 * i] = sums[0]
         s_ref[2 * i + 1] = sums[1]
     copies[4].wait()
     copies[5].wait()
 
 
-def own_part(here, odd, own, mine, theirs):
-    _, owners, _, _ = own.shape
+def own_part(here, odd, owns, mine, theirs):
+    parts = len(owns)
+    owners, _, _ = owns[0].shape
     units, features = mine[0].shape
     shape = jax.ShapeDtypeStruct((2 * units, features), BF)
     return pl.pallas_call(
         own_kernel,
         out_shape=(shape,) * 3 + (jax.ShapeDtypeStruct((4, 4 * owners, 2 * units), F32),),
-        in_specs=[SM, SM, VM] + [ANY] * 6,
+        in_specs=[SM] * 2 + [VM] * parts + [ANY] * 6,
         out_specs=(VM,) * 4,
         scratch_shapes=[pltpu.SemaphoreType.DMA((6,))],
         cost_estimate=pl.CostEstimate(
@@ -202,7 +204,7 @@
         ),
         compiler_params=params(16),
         name="ownpart",
-    )(here, odd, own, *(in_hbm(w) for w in mine), *theirs)
+    )(here, odd, *owns, *(in_hbm(w) for w in mine), *theirs)
 
 
 def expert_kernel(here_ref, odd_ref, s_ref, *refs):
@@ -217,7 +219,7 @@
 
     gates, ups = [s_ref[0], s_ref[1]], [s_ref[2], s_ref[3]]
     for i, x_ref in enumerate(pals):
-        at = start_of(here, odd, parts, half, parts - i, True, True)
+        at = start_of(here, odd, half, i, True, True)
         gates = add_in(gates, x_ref[...], at, g_ref, half)
         ups = add_in(ups, x_ref[...], at, u_ref, half)
 
@@ -237,7 +239,7 @@
     )
     for other in (True, False):
         for k in range(parts):
-            at = start_of(here, odd, parts, half, k, other, not other)
+            at = start_of(here, odd, half, k, other, not other)
             o_ref = give_ref.at[k] if other else keep_refs[k]
             a = jnp.dot(lhs[0], d_ref[:, pl.ds(at, low)], preferred_element_type=F32)
             cols = pl.ds(pl.multiple_of(at + low, 128), half - low)
@@ -283,8 +285,8 @@
     swap_sub = [(i, subs - 1 - i) for i in range(subs)]
     swap_pair = [(i, i ^ 1) for i in range(owners)]
 
-    def turned(x, k):
-        return lax.ppermute(x, "tensor", [(i, (i + k) % parts) for i in range(parts)])
+    def swapped(x, k):
+        return lax.ppermute(x, "tensor", [(i, i ^ k) for i in range(parts)])
 
     def across(x):
         return lax.all_to_all(x, "tensor", split_axis=0, concat_axis=0, tiled=True)
@@ -297,17 +299,20 @@
     packed = packed_of(here, expert_ids, tokens, owners, block)
     arrived = along(packed)
     partner = lax.ppermute(arrived, "expert", swap_pair)
-    spread = jnp.broadcast_to(arrived[None], (parts, *arrived.shape))
-    spread = across(spread)
-    pals = [partner] + [None] * (parts - 1)
-    for k in ring_steps(parts):
-        pals[k] = turned(partner, k)
-    *weights, sums = own_part(here, odd, spread, own, other)
+    far, *near = swaps(parts)
+    owns, pals = {0: arrived}, {0: partner}
+    for k in (far, *near):
+        owns[k] = swapped(arrived, k)
+    for k in near:
+        pals[k] = swapped(partner, k)
+    pals[far] = lax.ppermute(owns[far], "expert", swap_pair)
+    owns, pals = ([x[k] for k in range(parts)] for x in (owns, pals))
+    *weights, sums = own_part(here, odd, owns, own, other)
     give, keep = experts_of(here, odd, sums, pals, weights)
     give = across(give)
     kept = [keep[0]]
-    for k in ring_steps(parts):
-        kept.append(turned(keep[k], k))
+    for k in (far, *near):
+        kept.append(swapped(keep[k], k))
     give = jnp.sum(give.astype(F32), axis=0).astype(BF)
     taken = lax.ppermute(give, "expert", swap_pair)
     both = sum(x.astype(F32) for x in kept) + taken.astype(F32)
@@ -316,8 +321,8 @@
     return mixed_of(expert_ids, gate_codes, back, block)
 
 
-def ring_steps(parts):
-    return sorted(range(1, parts), key=lambda k: min(k, parts - k))
+def swaps(parts):
+    return [parts // 2, *(k for k in range(1, parts) if k != parts // 2)]
 
 
 def solution(mesh):

time: 177 us -> 181 us (1.023)
  starting transfers between devices: 88.5 us -> 95.1 us
  waiting for transfers between devices: 43.3 us -> 40.4 us
    ppermute x6 -> x9, starting transfers between devices: 23.3 us -> 34.1 us  [the longest x8 30.4 us: swapped(): return lax.ppermute(x, 'tensor', [(i, i ^ k) for i in range(parts)])]
    ppermute x1, waiting for transfers between devices: 5.18 us -> 0.02 us  [shards(): partner = lax.ppermute(arrived, 'expert', swap_pair)]
    all_to_all x2 -> x1, starting transfers between devices: 8.64 us -> 3.71 us  [across(): return lax.all_to_all(x, 'tensor', split_axis=0, concat_axis=0, tiled=True)]
    ppermute x6 -> x9, waiting for transfers between devices: 2.24 us -> 5.75 us  [the longest x8 5.75 us: swapped(): return lax.ppermute(x, 'tensor', [(i, i ^ k) for i in range(parts)])]
  transfers between devices with their start and end apart: 14 -> 16, of which waited for: 6 -> 7; matrix products, arithmetic and copies ran while one was open for 1% -> 0% of each run, Pallas kernels for 3% -> 3%
where the time goes in v6:
time: 181 us; the launch traced here: 180 us
  starting transfers between devices  95.1 us (53%)
  waiting for transfers between devices  40.4 us (22%)
  blocking collectives  34.2 us (19%)
  Pallas kernels  9.96 us (6%)
    all_to_all x1, starting transfers between devices, along(): return lax.all_to_all(x, 'expert', split_axis=0, concat_axis=0, tiled=True)  45.8 us
    all_to_all x1, blocking collectives, along(): return lax.all_to_all(x, 'expert', split_axis=0, concat_axis=0, tiled=True)  34.2 us
    all_to_all x1, waiting for transfers between devices, along(): return lax.all_to_all(x, 'expert', split_axis=0, concat_axis=0, tiled=True)  31.2 us
    ppermute x8, starting transfers between devices, swapped(): return lax.ppermute(x, 'tensor', [(i, i ^ k) for i in range(parts)])  30.4 us
    ppermute x3, starting transfers between devices, shards(): other = [lax.ppermute(w, 'sub', swap_sub) for w in own]  6.34 us
    ppermute x8, waiting for transfers between devices, swapped(): return lax.ppermute(x, 'tensor', [(i, i ^ k) for i in range(parts)])  5.75 us
    pallas_call x1, Pallas kernels, own_part(): pl.pallas_call(own_kernel, out_shape=(shape,) * 3 + (jax.ShapeDtypeStruct...  3.76 us
    ppermute x1, starting transfers between devices, shards(): pals[far] = lax.ppermute(owns[far], 'expert', swap_pair)  3.75 us
  transfers between devices with their start and end apart: 16, of which 7 were waited for; matrix products, arithmetic and copies ran while one was open for 0% of the time, Pallas kernels for 3%

profile of v6, /device:TPU:40, one launch (start us, length us, event | category | flops | bytes accessed | tf_op | source)
XLA Modules:
  0.0 180.2 jit_solution(1284568256491664017)
XLA Ops:
  0.0 1.9 %collective-permute-start.3 = (bf16[128,7168]{1,0:T(8,128)(2,1)}, bf16[128,7168]{1,0:T(8,128)(2,1)S(1)}, u32[]{:S(2)}, u32[]{:S(2)}) collective-permute-start(bf16[128,7168]{1,0:T(8,128)(2,1)} %bitcast.5), channel_id=1, source_target_pairs={{0,1},{1,0},{2,3},{3,2},{4,5},{5,4},{6,7},{7,6},{8,9},{9,8},{10,11... | collective-permute-start | bytes 5505032 | tf_op jit(solution)/shard_map/ppermute | solution.py:298
  2.0 1.9 %pack.1 = bf16[32,2,1408]{2,1,0:T(2,128)(2,1)} custom-call(s32[1]{0:T(128)} %bitcast.here_ref, s32[4,8]{1,0:T(4,128)} %ids_ref.1, bf16[4,7168]{1,0:T(4,128)(2,1)} %tok_hbm.1), custom_call_target="tpu_custom_call" | custom-call | tf_op jit(solution)/shard_map/pack/pallas_call | solution.py:82
  3.8 45.8 %all-to-all-start = ((bf16[32,2,1408]{2,1,0:T(2,128)(2,1)}), bf16[32,2,1408]{2,1,0:T(2,128)(2,1)S(1)}, u32[]{:S(2)}, u32[]{:S(2)}) async-start(bf16[32,2,1408]{2,1,0:T(2,128)(2,1)} %pack.1), calls=%async_computation | async-start | bytes 360448 | tf_op jit(solution)/shard_map/all_to_all | solution.py:295
  49.6 2.2 %collective-permute-start.4 = (bf16[128,7168]{1,0:T(8,128)(2,1)}, bf16[128,7168]{1,0:T(8,128)(2,1)}, u32[]{:S(2)}, u32[]{:S(2)}) collective-permute-start(bf16[128,7168]{1,0:T(8,128)(2,1)} %bitcast.7), channel_id=1, source_target_pairs={{0,1},{1,0},{2,3},{3,2},{4,5},{5,4},{6,7},{7,6},{8,9},{9,8},{10,11... | collective-permute-start | bytes 5505032 | tf_op jit(solution)/shard_map/ppermute | solution.py:298
  51.8 2.2 %collective-permute-start.5 = (bf16[128,7168]{1,0:T(8,128)(2,1)}, bf16[128,7168]{1,0:T(8,128)(2,1)}, u32[]{:S(2)}, u32[]{:S(2)}) collective-permute-start(bf16[128,7168]{1,0:T(8,128)(2,1)} %bitcast.9), channel_id=1, source_target_pairs={{0,1},{1,0},{2,3},{3,2},{4,5},{5,4},{6,7},{7,6},{8,9},{9,8},{10,11... | collective-permute-start | bytes 5505032 | tf_op jit(solution)/shard_map/ppermute | solution.py:298
  54.0 31.2 %all-to-all-done.refs_0_ = bf16[32,2,1408]{2,1,0:T(2,128)(2,1)S(1)} async-done(((bf16[32,2,1408]{2,1,0:T(2,128)(2,1)}), bf16[32,2,1408]{2,1,0:T(2,128)(2,1)S(1)}, u32[]{:S(2)}, u32[]{:S(2)}) %all-to-all-start) | async-done | bytes 180256 | tf_op jit(solution)/shard_map/all_to_all | solution.py:295
  85.2 5.2 %collective-permute-start.1 = (bf16[32,2,1408]{2,1,0:T(2,128)(2,1)S(1)}, bf16[32,2,1408]{2,1,0:T(2,128)(2,1)S(1)}, u32[]{:S(2)}, u32[]{:S(2)}) collective-permute-start(bf16[32,2,1408]{2,1,0:T(2,128)(2,1)S(1)} %all-to-all-done.refs_0_), channel_id=1, source_target_pairs={{0,4},{2,6},{4,0},{6,2},{1,5},{3,7},{5,1},{7,3},{8,12},{10,14},{12... | collective-permute-start | bytes 540680 | tf_op jit(solution)/shard_map/ppermute | solution.py:289
  90.4 2.7 %collective-permute-start = (bf16[32,2,1408]{2,1,0:T(2,128)(2,1)S(1)}, bf16[32,2,1408]{2,1,0:T(2,128)(2,1)S(1)}, u32[]{:S(2)}, u32[]{:S(2)}) collective-permute-start(bf16[32,2,1408]{2,1,0:T(2,128)(2,1)S(1)} %all-to-all-done.refs_0_), channel_id=1, source_target_pairs={{0,2},{2,0},{4,6},{6,4},{1,3},{3,1},{5,7},{7,5},{8,10},{10,8},{12,... | collective-permute-start | bytes 540680 | tf_op jit(solution)/shard_map/ppermute | solution.py:289
  93.1 2.0 %collective-permute-done.1.refs_2_ = bf16[32,2,1408]{2,1,0:T(2,128)(2,1)S(1)} collective-permute-done((bf16[32,2,1408]{2,1,0:T(2,128)(2,1)S(1)}, bf16[32,2,1408]{2,1,0:T(2,128)(2,1)S(1)}, u32[]{:S(2)}, u32[]{:S(2)}) %collective-permute-start.1) | collective-permute-done | bytes 180256 | tf_op jit(solution)/shard_map/ppermute | solution.py:289
  95.1 2.1 %collective-permute-start.6 = (bf16[32,2,1408]{2,1,0:T(2,128)(2,1)S(1)}, bf16[32,2,1408]{2,1,0:T(2,128)(2,1)S(1)}, u32[]{:S(2)}, u32[]{:S(2)}) collective-permute-start(bf16[32,2,1408]{2,1,0:T(2,128)(2,1)S(1)} %all-to-all-done.refs_0_), channel_id=1, source_target_pairs={{0,8},{8,0},{16,24},{24,16},{32,40},{40,32},{48,56},{56,48},{64,72... | collective-permute-start | bytes 540680 | tf_op jit(solution)/shard_map/ppermute | solution.py:301
  97.3 1.4 collective-permute-done.refs_1_
  98.7 3.8 %collective-permute-start.2 = (bf16[32,2,1408]{2,1,0:T(2,128)(2,1)S(1)}, bf16[32,2,1408]{2,1,0:T(2,128)(2,1)S(1)}, u32[]{:S(2)}, u32[]{:S(2)}) collective-permute-start(bf16[32,2,1408]{2,1,0:T(2,128)(2,1)S(1)} %all-to-all-done.refs_0_), channel_id=1, source_target_pairs={{0,6},{2,4},{4,2},{6,0},{1,7},{3,5},{5,3},{7,1},{8,14},{10,12},{12... | collective-permute-start | bytes 540680 | tf_op jit(solution)/shard_map/ppermute | solution.py:289
  102.5 0.0 collective-permute-done.6.refs_0_
  102.5 4.5 %collective-permute-start.7 = (bf16[32,2,1408]{2,1,0:T(2,128)(2,1)S(1)}, bf16[32,2,1408]{2,1,0:T(2,128)(2,1)S(1)}, u32[]{:S(2)}, u32[]{:S(2)}) collective-permute-start(bf16[32,2,1408]{2,1,0:T(2,128)(2,1)S(1)} %collective-permute-done.6.refs_0_), channel_id=1, source_target_pairs={{0,2},{2,0},{4,6},{6,4},{1,3},{3,1},{5,7},{7,5},{8,10},{10,8},{12,... | collective-permute-start | bytes 540680 | tf_op jit(solution)/shard_map/ppermute | solution.py:289
  107.0 0.3 collective-permute-done.2.refs_3_
  107.3 3.8 %collective-permute-start.9 = (bf16[32,2,1408]{2,1,0:T(2,128)(2,1)S(1)}, bf16[32,2,1408]{2,1,0:T(2,128)(2,1)S(1)}, u32[]{:S(2)}, u32[]{:S(2)}) collective-permute-start(bf16[32,2,1408]{2,1,0:T(2,128)(2,1)S(1)} %collective-permute-done.6.refs_0_), channel_id=1, source_target_pairs={{0,6},{2,4},{4,2},{6,0},{1,7},{3,5},{5,3},{7,1},{8,14},{10,12},{12... | collective-permute-start | bytes 540680 | tf_op jit(solution)/shard_map/ppermute | solution.py:289
  111.1 3.8 %collective-permute-start.8 = (bf16[32,2,1408]{2,1,0:T(2,128)(2,1)S(1)}, bf16[32,2,1408]{2,1,0:T(2,128)(2,1)S(1)}, u32[]{:S(2)}, u32[]{:S(2)}) collective-permute-start(bf16[32,2,1408]{2,1,0:T(2,128)(2,1)S(1)} %collective-permute-done.1.refs_2_), channel_id=1, source_target_pairs={{0,8},{8,0},{16,24},{24,16},{32,40},{40,32},{48,56},{56,48},{64,72... | collective-permute-start | bytes 540680 | tf_op jit(solution)/shard_map/ppermute | solution.py:308
  114.9 3.8 %ownpart.1 = (bf16[256,7168]{1,0:T(8,128)(2,1)S(1)}, bf16[256,7168]{1,0:T(8,128)(2,1)S(1)}, bf16[256,7168]{1,0:T(8,128)(2,1)S(1)}, f32[4,128,256]{2,1,0:T(8,128)S(1)}) custom-call(s32[1]{0:T(128)} %bitcast.here_ref, s32[1]{0:T(128)} %bitcast.1.odd_ref, bf16[32,2,1408]{2,1,0:T(2,128)(2,1)S(1)} %all-to-all-done.refs_0_, ...), custom_call_target="tpu_custom_call" | custom-call | flops 469762048 | bytes 22020096 | tf_op jit(solution)/shard_map/ownpart/pallas_call | solution.py:194
  118.7 2.9 %experts.1 = (bf16[4,64,1408]{2,1,0:T(8,128)(2,1)}, bf16[64,1408]{1,0:T(8,128)(2,1)S(1)}, bf16[64,1408]{1,0:T(8,128)(2,1)S(1)}, bf16[64,1408]{1,0:T(8,128)(2,1)S(1)}, bf16[64,1408]{1,0:T(8,128)(2,1)S(1)}) custom-call(s32[1]{0:T(128)} %bitcast.here_ref, s32[1]{0:T(128)} %bitcast.1.odd_ref, f32[4,128,256]{2,1,0:T(8,128)S(1)} %get-tuple-element.14.s_ref, ...), custom_call_target="tpu_custom_call" | custom-call | flops 939524096 | bytes 11010048 | tf_op jit(solution)/shard_map/experts/pallas_call | solution.py:259
  121.7 3.7 %all-to-all-start.1 = ((bf16[4,64,1408]{2,1,0:T(8,128)(2,1)}), bf16[4,64,1408]{2,1,0:T(8,128)(2,1)S(1)}, u32[]{:S(2)}, u32[]{:S(2)}) async-start(bf16[4,64,1408]{2,1,0:T(8,128)(2,1)} %get-tuple-element.22), calls=%async_computation.1 | async-start | bytes 1441792 | tf_op jit(solution)/shard_map/all_to_all | solution.py:292
  125.4 5.4 %collective-permute-start.10 = (bf16[64,1408]{1,0:T(8,128)(2,1)S(1)}, bf16[64,1408]{1,0:T(8,128)(2,1)S(1)}, u32[]{:S(2)}, u32[]{:S(2)}) collective-permute-start(bf16[64,1408]{1,0:T(8,128)(2,1)S(1)} %get-tuple-element.19), channel_id=1, source_target_pairs={{0,4},{2,6},{4,0},{6,2},{1,5},{3,7},{5,1},{7,3},{8,12},{10,14},{12... | collective-permute-start | bytes 540680 | tf_op jit(solution)/shard_map/ppermute | solution.py:289
  130.7 2.5 %collective-permute-start.11 = (bf16[64,1408]{1,0:T(8,128)(2,1)S(1)}, bf16[64,1408]{1,0:T(8,128)(2,1)S(1)}, u32[]{:S(2)}, u32[]{:S(2)}) collective-permute-start(bf16[64,1408]{1,0:T(8,128)(2,1)S(1)} %get-tuple-element.20), channel_id=1, source_target_pairs={{0,2},{2,0},{4,6},{6,4},{1,3},{3,1},{5,7},{7,5},{8,10},{10,8},{12,... | collective-permute-start | bytes 540680 | tf_op jit(solution)/shard_map/ppermute | solution.py:289
  133.3 2.5 %collective-permute-start.12 = (bf16[64,1408]{1,0:T(8,128)(2,1)S(1)}, bf16[64,1408]{1,0:T(8,128)(2,1)S(1)}, u32[]{:S(2)}, u32[]{:S(2)}) collective-permute-start(bf16[64,1408]{1,0:T(8,128)(2,1)S(1)} %get-tuple-element.21), channel_id=1, source_target_pairs={{0,6},{2,4},{4,2},{6,0},{1,7},{3,5},{5,3},{7,1},{8,14},{10,12},{12... | collective-permute-start | bytes 540680 | tf_op jit(solution)/shard_map/ppermute | solution.py:289
  135.8 1.0 all-to-all-done.1
  136.8 0.1 reduce_sum.12
  136.9 3.0 %collective-permute-start.13 = (bf16[64,1408]{1,0:T(8,128)(2,1)S(1)}, bf16[64,1408]{1,0:T(8,128)(2,1)S(1)}, u32[]{:S(2)}, u32[]{:S(2)}) collective-permute-start(bf16[64,1408]{1,0:T(8,128)(2,1)S(1)} %reduce_sum.12), channel_id=1, source_target_pairs={{0,8},{8,0},{16,24},{24,16},{32,40},{40,32},{48,56},{56,48},{64,72... | collective-permute-start | bytes 540680 | tf_op jit(solution)/shard_map/ppermute | solution.py:317
  139.9 2.0 %collective-permute-done.12 = bf16[64,1408]{1,0:T(8,128)(2,1)S(1)} collective-permute-done((bf16[64,1408]{1,0:T(8,128)(2,1)S(1)}, bf16[64,1408]{1,0:T(8,128)(2,1)S(1)}, u32[]{:S(2)}, u32[]{:S(2)}) %collective-permute-start.12) | collective-permute-done | bytes 180256 | tf_op jit(solution)/shard_map/ppermute | solution.py:289
  141.9 2.4 %collective-permute-done.13 = bf16[64,1408]{1,0:T(8,128)(2,1)S(1)} collective-permute-done((bf16[64,1408]{1,0:T(8,128)(2,1)S(1)}, bf16[64,1408]{1,0:T(8,128)(2,1)S(1)}, u32[]{:S(2)}, u32[]{:S(2)}) %collective-permute-start.13) | collective-permute-done | bytes 180256 | tf_op jit(solution)/shard_map/ppermute | solution.py:317
  144.3 0.1 add_convert_fusion
  144.5 0.1 reshape.11
  144.5 34.2 %all_to_all.15.x_ref = bf16[32,2,1408]{2,1,0:T(2,128)(2,1)S(1)} all-to-all(bf16[32,2,1408]{2,1,0:T(2,128)(2,1)S(1)} %reshape.11), channel_id=1, replica_groups=mesh['group'=2,'expert'=32,'tensor'=4,'sub'=2] {'expert'}, dimensions={0} | all-to-all | bytes 360448 | tf_op jit(solution)/shard_map/all_to_all | solution.py:295
  178.8 1.4 mix.1
  (12 shorter events, 0.0 us)
Async XLA Ops:
  0.0 111.1 %collective-permute-start.3 = (bf16[128,7168]{1,0:T(8,128)(2,1)}, bf16[128,7168]{1,0:T(8,128)(2,1)S(1)}, u32[]{:S(2)}, u32[]{:S(2)}) collective-permute-start(bf16[128,7168]{1,0:T(8,128)(2,1)} %bitcast.5), channel_id=1, source_target_pairs={{0,1},{1,0},{2,3},{3,2},{4,5},{5,4},{6,7},{7,6},{8,9},{9,8},{10,11... | collective-permute-start | bytes 5505032 | tf_op jit(solution)/shard_map/ppermute | solution.py:298
  3.8 81.4 %all-to-all-start = ((bf16[32,2,1408]{2,1,0:T(2,128)(2,1)}), bf16[32,2,1408]{2,1,0:T(2,128)(2,1)S(1)}, u32[]{:S(2)}, u32[]{:S(2)}) async-start(bf16[32,2,1408]{2,1,0:T(2,128)(2,1)} %pack.1), calls=%async_computation | async-start | bytes 360448 | tf_op jit(solution)/shard_map/all_to_all | solution.py:295
  49.6 65.3 %collective-permute-start.4 = (bf16[128,7168]{1,0:T(8,128)(2,1)}, bf16[128,7168]{1,0:T(8,128)(2,1)}, u32[]{:S(2)}, u32[]{:S(2)}) collective-permute-start(bf16[128,7168]{1,0:T(8,128)(2,1)} %bitcast.7), channel_id=1, source_target_pairs={{0,1},{1,0},{2,3},{3,2},{4,5},{5,4},{6,7},{7,6},{8,9},{9,8},{10,11... | collective-permute-start | bytes 5505032 | tf_op jit(solution)/shard_map/ppermute | solution.py:298
  51.8 63.1 %collective-permute-start.5 = (bf16[128,7168]{1,0:T(8,128)(2,1)}, bf16[128,7168]{1,0:T(8,128)(2,1)}, u32[]{:S(2)}, u32[]{:S(2)}) collective-permute-start(bf16[128,7168]{1,0:T(8,128)(2,1)} %bitcast.9), channel_id=1, source_target_pairs={{0,1},{1,0},{2,3},{3,2},{4,5},{5,4},{6,7},{7,6},{8,9},{9,8},{10,11... | collective-permute-start | bytes 5505032 | tf_op jit(solution)/shard_map/ppermute | solution.py:298
  85.2 9.9 %collective-permute-start.1 = (bf16[32,2,1408]{2,1,0:T(2,128)(2,1)S(1)}, bf16[32,2,1408]{2,1,0:T(2,128)(2,1)S(1)}, u32[]{:S(2)}, u32[]{:S(2)}) collective-permute-start(bf16[32,2,1408]{2,1,0:T(2,128)(2,1)S(1)} %all-to-all-done.refs_0_), channel_id=1, source_target_pairs={{0,4},{2,6},{4,0},{6,2},{1,5},{3,7},{5,1},{7,3},{8,12},{10,14},{12... | collective-permute-start | bytes 540680 | tf_op jit(solution)/shard_map/ppermute | solution.py:289
  90.4 8.3 %collective-permute-start = (bf16[32,2,1408]{2,1,0:T(2,128)(2,1)S(1)}, bf16[32,2,1408]{2,1,0:T(2,128)(2,1)S(1)}, u32[]{:S(2)}, u32[]{:S(2)}) collective-permute-start(bf16[32,2,1408]{2,1,0:T(2,128)(2,1)S(1)} %all-to-all-done.refs_0_), channel_id=1, source_target_pairs={{0,2},{2,0},{4,6},{6,4},{1,3},{3,1},{5,7},{7,5},{8,10},{10,8},{12,... | collective-permute-start | bytes 540680 | tf_op jit(solution)/shard_map/ppermute | solution.py:289
  95.1 7.4 %collective-permute-start.6 = (bf16[32,2,1408]{2,1,0:T(2,128)(2,1)S(1)}, bf16[32,2,1408]{2,1,0:T(2,128)(2,1)S(1)}, u32[]{:S(2)}, u32[]{:S(2)}) collective-permute-start(bf16[32,2,1408]{2,1,0:T(2,128)(2,1)S(1)} %all-to-all-done.refs_0_), channel_id=1, source_target_pairs={{0,8},{8,0},{16,24},{24,16},{32,40},{40,32},{48,56},{56,48},{64,72... | collective-permute-start | bytes 540680 | tf_op jit(solution)/shard_map/ppermute | solution.py:301
  98.7 8.6 %collective-permute-start.2 = (bf16[32,2,1408]{2,1,0:T(2,128)(2,1)S(1)}, bf16[32,2,1408]{2,1,0:T(2,128)(2,1)S(1)}, u32[]{:S(2)}, u32[]{:S(2)}) collective-permute-start(bf16[32,2,1408]{2,1,0:T(2,128)(2,1)S(1)} %all-to-all-done.refs_0_), channel_id=1, source_target_pairs={{0,6},{2,4},{4,2},{6,0},{1,7},{3,5},{5,3},{7,1},{8,14},{10,12},{12... | collective-permute-start | bytes 540680 | tf_op jit(solution)/shard_map/ppermute | solution.py:289
  102.5 16.2 %collective-permute-start.7 = (bf16[32,2,1408]{2,1,0:T(2,128)(2,1)S(1)}, bf16[32,2,1408]{2,1,0:T(2,128)(2,1)S(1)}, u32[]{:S(2)}, u32[]{:S(2)}) collective-permute-start(bf16[32,2,1408]{2,1,0:T(2,128)(2,1)S(1)} %collective-permute-done.6.refs_0_), channel_id=1, source_target_pairs={{0,2},{2,0},{4,6},{6,4},{1,3},{3,1},{5,7},{7,5},{8,10},{10,8},{12,... | collective-permute-start | bytes 540680 | tf_op jit(solution)/shard_map/ppermute | solution.py:289
  107.3 11.4 %collective-permute-start.9 = (bf16[32,2,1408]{2,1,0:T(2,128)(2,1)S(1)}, bf16[32,2,1408]{2,1,0:T(2,128)(2,1)S(1)}, u32[]{:S(2)}, u32[]{:S(2)}) collective-permute-start(bf16[32,2,1408]{2,1,0:T(2,128)(2,1)S(1)} %collective-permute-done.6.refs_0_), channel_id=1, source_target_pairs={{0,6},{2,4},{4,2},{6,0},{1,7},{3,5},{5,3},{7,1},{8,14},{10,12},{12... | collective-permute-start | bytes 540680 | tf_op jit(solution)/shard_map/ppermute | solution.py:289
  111.1 7.6 %collective-permute-start.8 = (bf16[32,2,1408]{2,1,0:T(2,128)(2,1)S(1)}, bf16[32,2,1408]{2,1,0:T(2,128)(2,1)S(1)}, u32[]{:S(2)}, u32[]{:S(2)}) collective-permute-start(bf16[32,2,1408]{2,1,0:T(2,128)(2,1)S(1)} %collective-permute-done.1.refs_2_), channel_id=1, source_target_pairs={{0,8},{8,0},{16,24},{24,16},{32,40},{40,32},{48,56},{56,48},{64,72... | collective-permute-start | bytes 540680 | tf_op jit(solution)/shard_map/ppermute | solution.py:308
  121.7 57.1 %copy-start = (s32[4,8]{1,0:T(4,128)S(1)}, s32[4,8]{1,0:T(4,128)}, u32[]{:S(2)}) copy-start(s32[4,8]{1,0:T(4,128)} %ids_ref.1) | copy-start | bytes 388
  121.7 57.1 %copy-start.1 = (s32[4,8]{1,0:T(4,128)S(1)}, s32[4,8]{1,0:T(4,128)}, u32[]{:S(2)}) copy-start(s32[4,8]{1,0:T(4,128)} %code_ref.1) | copy-start | bytes 388
  121.7 15.1 %all-to-all-start.1 = ((bf16[4,64,1408]{2,1,0:T(8,128)(2,1)}), bf16[4,64,1408]{2,1,0:T(8,128)(2,1)S(1)}, u32[]{:S(2)}, u32[]{:S(2)}) async-start(bf16[4,64,1408]{2,1,0:T(8,128)(2,1)} %get-tuple-element.22), calls=%async_computation.1 | async-start | bytes 1441792 | tf_op jit(solution)/shard_map/all_to_all | solution.py:292
  125.4 14.5 %collective-permute-start.10 = (bf16[64,1408]{1,0:T(8,128)(2,1)S(1)}, bf16[64,1408]{1,0:T(8,128)(2,1)S(1)}, u32[]{:S(2)}, u32[]{:S(2)}) collective-permute-start(bf16[64,1408]{1,0:T(8,128)(2,1)S(1)} %get-tuple-element.19), channel_id=1, source_target_pairs={{0,4},{2,6},{4,0},{6,2},{1,5},{3,7},{5,1},{7,3},{8,12},{10,14},{12... | collective-permute-start | bytes 540680 | tf_op jit(solution)/shard_map/ppermute | solution.py:289
  130.7 9.2 %collective-permute-start.11 = (bf16[64,1408]{1,0:T(8,128)(2,1)S(1)}, bf16[64,1408]{1,0:T(8,128)(2,1)S(1)}, u32[]{:S(2)}, u32[]{:S(2)}) collective-permute-start(bf16[64,1408]{1,0:T(8,128)(2,1)S(1)} %get-tuple-element.20), channel_id=1, source_target_pairs={{0,2},{2,0},{4,6},{6,4},{1,3},{3,1},{5,7},{7,5},{8,10},{10,8},{12,... | collective-permute-start | bytes 540680 | tf_op jit(solution)/shard_map/ppermute | solution.py:289
  133.3 8.6 %collective-permute-start.12 = (bf16[64,1408]{1,0:T(8,128)(2,1)S(1)}, bf16[64,1408]{1,0:T(8,128)(2,1)S(1)}, u32[]{:S(2)}, u32[]{:S(2)}) collective-permute-start(bf16[64,1408]{1,0:T(8,128)(2,1)S(1)} %get-tuple-element.21), channel_id=1, source_target_pairs={{0,6},{2,4},{4,2},{6,0},{1,7},{3,5},{5,3},{7,1},{8,14},{10,12},{12... | collective-permute-start | bytes 540680 | tf_op jit(solution)/shard_map/ppermute | solution.py:289
  136.9 7.4 %collective-permute-start.13 = (bf16[64,1408]{1,0:T(8,128)(2,1)S(1)}, bf16[64,1408]{1,0:T(8,128)(2,1)S(1)}, u32[]{:S(2)}, u32[]{:S(2)}) collective-permute-start(bf16[64,1408]{1,0:T(8,128)(2,1)S(1)} %reduce_sum.12), channel_id=1, source_target_pairs={{0,8},{8,0},{16,24},{24,16},{32,40},{40,32},{48,56},{56,48},{64,72... | collective-permute-start | bytes 540680 | tf_op jit(solution)/shard_map/ppermute | solution.py:317

commit v7 on v5

--- a/solution.py
+++ b/solution.py
@@ -132,9 +132,9 @@
     )(ids, codes, x)
 
 
-def start_of(here, odd, parts, half, k, other, turned):
+def start_of(here, odd, half, k, other, turned):
     side = 1 - odd if other else odd
-    k = lax.rem(here + k, parts) if turned else k
+    k = lax.bitwise_xor(here, jnp.int32(k)) if turned else k
     return pl.multiple_of((2 * k + side) * half, 128)
 
 
@@ -161,8 +161,9 @@
     ]
 
 
-def own_kernel(here_ref, odd_ref, own_ref, g0, u0, d0, g1, u1, d1, g_ref, u_ref, d_ref, s_ref, sems):
-    parts, _, _, _ = own_ref.shape
+def own_kernel(here_ref, odd_ref, *refs):
+    own_ref, g0, u0, d0, g1, u1, d1, g_ref, u_ref, d_ref, s_ref, sems = refs
+    parts = own_ref.shape[0]
     half = d_ref.shape[1] // (2 * parts)
     copies = []
     for i, (pair, dst) in enumerate((((g0, g1), g_ref), ((u0, u1), u_ref), ((d0, d1), d_ref))):
@@ -177,7 +178,7 @@
         copies[2 * i + 1].wait()
         sums = [jnp.zeros(s_ref.shape[1:], F32)] * 2
         for k in range(parts):
-            at = start_of(here_ref[0], odd_ref[0], parts, half, k, False, False)
+            at = start_of(here_ref[0], odd_ref[0], half, k, False, False)
             sums = add_in(sums, own_ref[k], at, w_ref, half)
         s_ref[2 * i] = sums[0]
         s_ref[2 * i + 1] = sums[1]
@@ -207,8 +208,8 @@
 
 def expert_kernel(here_ref, odd_ref, s_ref, *refs):
     parts = (len(refs) - 4) // 2
-    pals, (g_ref, u_ref, d_ref, give_ref) = refs[:parts], refs[parts : parts + 4]
-    keep_refs = refs[parts + 4 :]
+    pals, (g_ref, u_ref, d_ref, keep_ref) = refs[:parts], refs[parts : parts + 4]
+    give_refs = refs[parts + 4 :]
     owners, _, width = pals[0].shape
     rows = 2 * owners
     half = d_ref.shape[1] // (2 * parts)
@@ -217,7 +218,7 @@
 
     gates, ups = [s_ref[0], s_ref[1]], [s_ref[2], s_ref[3]]
     for i, x_ref in enumerate(pals):
-        at = start_of(here, odd, parts, half, parts - i, True, True)
+        at = start_of(here, odd, half, i, True, True)
         gates = add_in(gates, x_ref[...], at, g_ref, half)
         ups = add_in(ups, x_ref[...], at, u_ref, half)
 
@@ -237,8 +238,8 @@
     )
     for other in (True, False):
         for k in range(parts):
-            at = start_of(here, odd, parts, half, k, other, not other)
-            o_ref = give_ref.at[k] if other else keep_refs[k]
+            at = start_of(here, odd, half, k, other, other)
+            o_ref = give_refs[k] if other else keep_ref.at[k]
             a = jnp.dot(lhs[0], d_ref[:, pl.ds(at, low)], preferred_element_type=F32)
             cols = pl.ds(pl.multiple_of(at + low, 128), half - low)
             b = jnp.dot(lhs[1], d_ref[:, cols], preferred_element_type=F32)
@@ -283,8 +284,8 @@
     swap_sub = [(i, subs - 1 - i) for i in range(subs)]
     swap_pair = [(i, i ^ 1) for i in range(owners)]
 
-    def turned(x, k):
-        return lax.ppermute(x, "tensor", [(i, (i + k) % parts) for i in range(parts)])
+    def swapped(x, k):
+        return lax.ppermute(x, "tensor", [(i, i ^ k) for i in range(parts)])
 
     def across(x):
         return lax.all_to_all(x, "tensor", split_axis=0, concat_axis=0, tiled=True)
@@ -300,24 +301,24 @@
     spread = jnp.broadcast_to(arrived[None], (parts, *arrived.shape))
     spread = across(spread)
     pals = [partner] + [None] * (parts - 1)
-    for k in ring_steps(parts):
-        pals[k] = turned(partner, k)
+    for k in swaps(parts):
+        pals[k] = swapped(partner, k)
     *weights, sums = own_part(here, odd, spread, own, other)
-    give, keep = experts_of(here, odd, sums, pals, weights)
-    give = across(give)
-    kept = [keep[0]]
-    for k in ring_steps(parts):
-        kept.append(turned(keep[k], k))
-    give = jnp.sum(give.astype(F32), axis=0).astype(BF)
+    keep, give = experts_of(here, odd, sums, pals, weights)
+    given = [give[0]]
+    for k in swaps(parts):
+        given.append(swapped(give[k], k))
+    keep = across(keep)
+    give = sum(x.astype(F32) for x in given).astype(BF)
     taken = lax.ppermute(give, "expert", swap_pair)
-    both = sum(x.astype(F32) for x in kept) + taken.astype(F32)
+    both = jnp.sum(keep.astype(F32), axis=0) + taken.astype(F32)
     both = both.astype(BF).reshape(arrived.shape)
     back = along(both)
     return mixed_of(expert_ids, gate_codes, back, block)
 
 
-def ring_steps(parts):
-    return sorted(range(1, parts), key=lambda k: min(k, parts - k))
+def swaps(parts):
+    return sorted(range(1, parts), key=lambda k: k == parts // 2)
 
 
 def solution(mesh):

time: 177 us -> 180 us (1.017)
  starting transfers between devices: 88.5 us -> 85.1 us
  blocking collectives: 32.8 us -> 35.9 us
  waiting for transfers between devices: 43.3 us -> 45.9 us
    all_to_all x2, waiting for transfers between devices: 1.06 us -> 5.54 us  [across(): return lax.all_to_all(x, 'tensor', split_axis=0, concat_axis=0, tiled=True)]
    ppermute x1, waiting for transfers between devices: 3.6 us -> 0.01 us  [shards(): taken = lax.ppermute(give, 'expert', swap_pair)]
    all_to_all x1, blocking collectives: 32.8 us -> 35.9 us  [along(): return lax.all_to_all(x, 'expert', split_axis=0, concat_axis=0, tiled=True)]
    ppermute x6, starting transfers between devices: 23.3 us -> 20.4 us  [swapped(): return lax.ppermute(x, 'tensor', [(i, i ^ k) for i in range(parts)])]
  transfers between devices with their start and end apart: 14 -> 14, of which waited for: 6 -> 5; matrix products, arithmetic and copies ran while one was open for 1% -> 1% of each run, Pallas kernels for 3% -> 3%
where the time goes in v7:
time: 180 us; the launch traced here: 179 us
  starting transfers between devices  85.1 us (47%)
  waiting for transfers between devices  45.9 us (26%)
  blocking collectives  35.9 us (20%)
  Pallas kernels  10 us (6%)
    all_to_all x1, starting transfers between devices, along(): return lax.all_to_all(x, 'expert', split_axis=0, concat_axis=0, tiled=True)  45.8 us
    all_to_all x1, blocking collectives, along(): return lax.all_to_all(x, 'expert', split_axis=0, concat_axis=0, tiled=True)  35.9 us
    all_to_all x1, waiting for transfers between devices, along(): return lax.all_to_all(x, 'expert', split_axis=0, concat_axis=0, tiled=True)  31.2 us
    ppermute x6, starting transfers between devices, swapped(): return lax.ppermute(x, 'tensor', [(i, i ^ k) for i in range(parts)])  20.4 us
    all_to_all x2, starting transfers between devices, across(): return lax.all_to_all(x, 'tensor', split_axis=0, concat_axis=0, tiled=True)  8.17 us
    ppermute x3, starting transfers between devices, shards(): other = [lax.ppermute(w, 'sub', swap_sub) for w in own]  6.34 us
    all_to_all x2, waiting for transfers between devices, across(): return lax.all_to_all(x, 'tensor', split_axis=0, concat_axis=0, tiled=True)  5.54 us
    ppermute x1, waiting for transfers between devices, shards(): partner = lax.ppermute(arrived, 'expert', swap_pair)  5.18 us
  transfers between devices with their start and end apart: 14, of which 5 were waited for; matrix products, arithmetic and copies ran while one was open for 1% of the time, Pallas kernels for 3%

profile of v7, /device:TPU:40, one launch (start us, length us, event | category | flops | bytes accessed | tf_op | source)
XLA Modules:
  0.0 178.7 jit_solution(17376389662401274541)
XLA Ops:
  0.0 1.9 %collective-permute-start = (bf16[128,7168]{1,0:T(8,128)(2,1)}, bf16[128,7168]{1,0:T(8,128)(2,1)S(1)}, u32[]{:S(2)}, u32[]{:S(2)}) collective-permute-start(bf16[128,7168]{1,0:T(8,128)(2,1)} %bitcast.5), channel_id=1, source_target_pairs={{0,1},{1,0},{2,3},{3,2},{4,5},{5,4},{6,7},{7,6},{8,9},{9,8},{10,11... | collective-permute-start | bytes 5505032 | tf_op jit(solution)/shard_map/ppermute | solution.py:297
  2.0 1.9 %pack.1 = bf16[32,2,1408]{2,1,0:T(2,128)(2,1)} custom-call(s32[1]{0:T(128)} %bitcast.here_ref, s32[4,8]{1,0:T(4,128)} %ids_ref.1, bf16[4,7168]{1,0:T(4,128)(2,1)} %tok_hbm.1), custom_call_target="tpu_custom_call" | custom-call | tf_op jit(solution)/shard_map/pack/pallas_call | solution.py:82
  3.8 45.8 %all-to-all-start = ((bf16[32,2,1408]{2,1,0:T(2,128)(2,1)}), bf16[32,2,1408]{2,1,0:T(2,128)(2,1)S(1)}, u32[]{:S(2)}, u32[]{:S(2)}) async-start(bf16[32,2,1408]{2,1,0:T(2,128)(2,1)} %pack.1), calls=%async_computation | async-start | bytes 360448 | tf_op jit(solution)/shard_map/all_to_all | solution.py:294
  49.6 2.2 %collective-permute-start.1 = (bf16[128,7168]{1,0:T(8,128)(2,1)}, bf16[128,7168]{1,0:T(8,128)(2,1)}, u32[]{:S(2)}, u32[]{:S(2)}) collective-permute-start(bf16[128,7168]{1,0:T(8,128)(2,1)} %bitcast.7), channel_id=1, source_target_pairs={{0,1},{1,0},{2,3},{3,2},{4,5},{5,4},{6,7},{7,6},{8,9},{9,8},{10,11... | collective-permute-start | bytes 5505032 | tf_op jit(solution)/shard_map/ppermute | solution.py:297
  51.8 2.2 %collective-permute-start.2 = (bf16[128,7168]{1,0:T(8,128)(2,1)}, bf16[128,7168]{1,0:T(8,128)(2,1)}, u32[]{:S(2)}, u32[]{:S(2)}) collective-permute-start(bf16[128,7168]{1,0:T(8,128)(2,1)} %bitcast.9), channel_id=1, source_target_pairs={{0,1},{1,0},{2,3},{3,2},{4,5},{5,4},{6,7},{7,6},{8,9},{9,8},{10,11... | collective-permute-start | bytes 5505032 | tf_op jit(solution)/shard_map/ppermute | solution.py:297
  54.0 31.2 %all-to-all-done = bf16[32,2,1408]{2,1,0:T(2,128)(2,1)S(1)} async-done(((bf16[32,2,1408]{2,1,0:T(2,128)(2,1)}), bf16[32,2,1408]{2,1,0:T(2,128)(2,1)S(1)}, u32[]{:S(2)}, u32[]{:S(2)}) %all-to-all-start) | async-done | bytes 180256 | tf_op jit(solution)/shard_map/all_to_all | solution.py:294
  85.2 1.2 broadcast_in_dim.2
  86.4 4.6 %all-to-all-start.1 = ((bf16[4,32,2,1408]{3,2,1,0:T(2,128)(2,1)}), bf16[4,32,2,1408]{3,2,1,0:T(2,128)(2,1)S(1)}, u32[]{:S(2)}, u32[]{:S(2)}) async-start(bf16[4,32,2,1408]{3,2,1,0:T(2,128)(2,1)} %broadcast_in_dim.2), calls=%async_computation.1 | async-start | bytes 1441792 | tf_op jit(solution)/shard_map/all_to_all | solution.py:291
  91.0 2.2 %collective-permute-start.3 = (bf16[32,2,1408]{2,1,0:T(2,128)(2,1)S(1)}, bf16[32,2,1408]{2,1,0:T(2,128)(2,1)S(1)}, u32[]{:S(2)}, u32[]{:S(2)}) collective-permute-start(bf16[32,2,1408]{2,1,0:T(2,128)(2,1)S(1)} %all-to-all-done), channel_id=1, source_target_pairs={{0,8},{8,0},{16,24},{24,16},{32,40},{40,32},{48,56},{56,48},{64,72... | collective-permute-start | bytes 540680 | tf_op jit(solution)/shard_map/ppermute | solution.py:300
  93.2 5.2 %collective-permute-done.3.refs_0_ = bf16[32,2,1408]{2,1,0:T(2,128)(2,1)S(1)} collective-permute-done((bf16[32,2,1408]{2,1,0:T(2,128)(2,1)S(1)}, bf16[32,2,1408]{2,1,0:T(2,128)(2,1)S(1)}, u32[]{:S(2)}, u32[]{:S(2)}) %collective-permute-start.3) | collective-permute-done | bytes 180256 | tf_op jit(solution)/shard_map/ppermute | solution.py:300
  98.4 4.0 %collective-permute-start.4 = (bf16[32,2,1408]{2,1,0:T(2,128)(2,1)S(1)}, bf16[32,2,1408]{2,1,0:T(2,128)(2,1)S(1)}, u32[]{:S(2)}, u32[]{:S(2)}) collective-permute-start(bf16[32,2,1408]{2,1,0:T(2,128)(2,1)S(1)} %collective-permute-done.3.refs_0_), channel_id=1, source_target_pairs={{0,2},{2,0},{4,6},{6,4},{1,3},{3,1},{5,7},{7,5},{8,10},{10,8},{12,... | collective-permute-start | bytes 540680 | tf_op jit(solution)/shard_map/ppermute | solution.py:288
  102.4 4.6 %collective-permute-start.5 = (bf16[32,2,1408]{2,1,0:T(2,128)(2,1)S(1)}, bf16[32,2,1408]{2,1,0:T(2,128)(2,1)S(1)}, u32[]{:S(2)}, u32[]{:S(2)}) collective-permute-start(bf16[32,2,1408]{2,1,0:T(2,128)(2,1)S(1)} %collective-permute-done.3.refs_0_), channel_id=1, source_target_pairs={{0,4},{2,6},{4,0},{6,2},{1,5},{3,7},{5,1},{7,3},{8,12},{10,14},{12... | collective-permute-start | bytes 540680 | tf_op jit(solution)/shard_map/ppermute | solution.py:288
  107.0 0.0 collective-permute-done.refs_4_
  107.0 2.0 %collective-permute-start.6 = (bf16[32,2,1408]{2,1,0:T(2,128)(2,1)S(1)}, bf16[32,2,1408]{2,1,0:T(2,128)(2,1)S(1)}, u32[]{:S(2)}, u32[]{:S(2)}) collective-permute-start(bf16[32,2,1408]{2,1,0:T(2,128)(2,1)S(1)} %collective-permute-done.3.refs_0_), channel_id=1, source_target_pairs={{0,6},{2,4},{4,2},{6,0},{1,7},{3,5},{5,3},{7,1},{8,14},{10,12},{12... | collective-permute-start | bytes 540680 | tf_op jit(solution)/shard_map/ppermute | solution.py:288
  109.0 0.0 collective-permute-done.1.refs_5_
  109.0 3.8 %ownpart.1 = (bf16[256,7168]{1,0:T(8,128)(2,1)S(1)}, bf16[256,7168]{1,0:T(8,128)(2,1)S(1)}, bf16[256,7168]{1,0:T(8,128)(2,1)S(1)}, f32[4,128,256]{2,1,0:T(8,128)S(1)}) custom-call(s32[1]{0:T(128)} %bitcast.here_ref, s32[1]{0:T(128)} %bitcast.1.odd_ref, bf16[4,32,2,1408]{3,2,1,0:T(2,128)(2,1)S(1)} %all-to-all-done.1.refs_0_, bf16[128,7168]{1,0:T(8,128)(2,1)} %bitcast.6, ...), custom_call_target="tpu_custom_call" | custom-call | flops 469762048 | bytes 22020096 | tf_op jit(solution)/shard_map/ownpart/pallas_call | solution.py:193
  112.8 2.8 %collective-permute-done.6.refs_3_ = bf16[32,2,1408]{2,1,0:T(2,128)(2,1)S(1)} collective-permute-done((bf16[32,2,1408]{2,1,0:T(2,128)(2,1)S(1)}, bf16[32,2,1408]{2,1,0:T(2,128)(2,1)S(1)}, u32[]{:S(2)}, u32[]{:S(2)}) %collective-permute-start.6) | collective-permute-done | bytes 180256 | tf_op jit(solution)/shard_map/ppermute | solution.py:288
  115.6 3.0 %experts.1 = (bf16[4,64,1408]{2,1,0:T(8,128)(2,1)}, bf16[64,1408]{1,0:T(8,128)(2,1)S(1)}, bf16[64,1408]{1,0:T(8,128)(2,1)S(1)}, bf16[64,1408]{1,0:T(8,128)(2,1)S(1)}, bf16[64,1408]{1,0:T(8,128)(2,1)S(1)}) custom-call(s32[1]{0:T(128)} %bitcast.here_ref, s32[1]{0:T(128)} %bitcast.1.odd_ref, f32[4,128,256]{2,1,0:T(8,128)S(1)} %get-tuple-element.14.s_ref, ...), custom_call_target="tpu_custom_call" | custom-call | flops 939524096 | bytes 11010048 | tf_op jit(solution)/shard_map/experts/pallas_call | solution.py:258
  118.6 1.9 %collective-permute-start.7 = (bf16[64,1408]{1,0:T(8,128)(2,1)S(1)}, bf16[64,1408]{1,0:T(8,128)(2,1)S(1)}, u32[]{:S(2)}, u32[]{:S(2)}) collective-permute-start(bf16[64,1408]{1,0:T(8,128)(2,1)S(1)} %get-tuple-element.20), channel_id=1, source_target_pairs={{0,2},{2,0},{4,6},{6,4},{1,3},{3,1},{5,7},{7,5},{8,10},{10,8},{12,... | collective-permute-start | bytes 540680 | tf_op jit(solution)/shard_map/ppermute | solution.py:288
  120.6 3.7 %collective-permute-start.8 = (bf16[64,1408]{1,0:T(8,128)(2,1)S(1)}, bf16[64,1408]{1,0:T(8,128)(2,1)S(1)}, u32[]{:S(2)}, u32[]{:S(2)}) collective-permute-start(bf16[64,1408]{1,0:T(8,128)(2,1)S(1)} %get-tuple-element.21), channel_id=1, source_target_pairs={{0,6},{2,4},{4,2},{6,0},{1,7},{3,5},{5,3},{7,1},{8,14},{10,12},{12... | collective-permute-start | bytes 540680 | tf_op jit(solution)/shard_map/ppermute | solution.py:288
  124.3 4.2 %collective-permute-start.9 = (bf16[64,1408]{1,0:T(8,128)(2,1)S(1)}, bf16[64,1408]{1,0:T(8,128)(2,1)S(1)}, u32[]{:S(2)}, u32[]{:S(2)}) collective-permute-start(bf16[64,1408]{1,0:T(8,128)(2,1)S(1)} %get-tuple-element.22), channel_id=1, source_target_pairs={{0,4},{2,6},{4,0},{6,2},{1,5},{3,7},{5,1},{7,3},{8,12},{10,14},{12... | collective-permute-start | bytes 540680 | tf_op jit(solution)/shard_map/ppermute | solution.py:288
  128.6 3.6 %all-to-all-start.2 = ((bf16[4,64,1408]{2,1,0:T(8,128)(2,1)}), bf16[4,64,1408]{2,1,0:T(8,128)(2,1)S(1)}, u32[]{:S(2)}, u32[]{:S(2)}) async-start(bf16[4,64,1408]{2,1,0:T(8,128)(2,1)} %get-tuple-element.18), calls=%async_computation.2 | async-start | bytes 1441792 | tf_op jit(solution)/shard_map/all_to_all | solution.py:291
  132.2 0.0 copy-start
  132.2 0.0 copy-start.1
  132.2 1.1 collective-permute-done.9
  133.3 0.1 add_convert_fusion.1
  133.4 2.2 %collective-permute-start.10 = (bf16[64,1408]{1,0:T(8,128)(2,1)S(1)}, bf16[64,1408]{1,0:T(8,128)(2,1)S(1)}, u32[]{:S(2)}, u32[]{:S(2)}) collective-permute-start(bf16[64,1408]{1,0:T(8,128)(2,1)S(1)} %add_convert_fusion.1), channel_id=1, source_target_pairs={{0,8},{8,0},{16,24},{24,16},{32,40},{40,32},{48,56},{56,48},{64,72... | collective-permute-start | bytes 540680 | tf_op jit(solution)/shard_map/ppermute | solution.py:313
  135.7 5.5 %all-to-all-done.2 = bf16[4,64,1408]{2,1,0:T(8,128)(2,1)S(1)} async-done(((bf16[4,64,1408]{2,1,0:T(8,128)(2,1)}), bf16[4,64,1408]{2,1,0:T(8,128)(2,1)S(1)}, u32[]{:S(2)}, u32[]{:S(2)}) %all-to-all-start.2) | async-done | bytes 720928 | tf_op jit(solution)/shard_map/all_to_all | solution.py:291
  141.2 0.1 convert_reduce_fusion
  141.4 0.1 reshape.12
  141.4 35.9 %all_to_all.20.x_ref = bf16[32,2,1408]{2,1,0:T(2,128)(2,1)S(1)} all-to-all(bf16[32,2,1408]{2,1,0:T(2,128)(2,1)S(1)} %reshape.12), channel_id=1, replica_groups=mesh['group'=2,'expert'=32,'tensor'=4,'sub'=2] {'expert'}, dimensions={0} | all-to-all | bytes 360448 | tf_op jit(solution)/shard_map/all_to_all | solution.py:294
  177.3 1.4 mix.1
  (10 shorter events, 0.1 us)
Async XLA Ops:
  0.0 107.0 %collective-permute-start = (bf16[128,7168]{1,0:T(8,128)(2,1)}, bf16[128,7168]{1,0:T(8,128)(2,1)S(1)}, u32[]{:S(2)}, u32[]{:S(2)}) collective-permute-start(bf16[128,7168]{1,0:T(8,128)(2,1)} %bitcast.5), channel_id=1, source_target_pairs={{0,1},{1,0},{2,3},{3,2},{4,5},{5,4},{6,7},{7,6},{8,9},{9,8},{10,11... | collective-permute-start | bytes 5505032 | tf_op jit(solution)/shard_map/ppermute | solution.py:297
  3.8 81.4 %all-to-all-start = ((bf16[32,2,1408]{2,1,0:T(2,128)(2,1)}), bf16[32,2,1408]{2,1,0:T(2,128)(2,1)S(1)}, u32[]{:S(2)}, u32[]{:S(2)}) async-start(bf16[32,2,1408]{2,1,0:T(2,128)(2,1)} %pack.1), calls=%async_computation | async-start | bytes 360448 | tf_op jit(solution)/shard_map/all_to_all | solution.py:294
  49.6 59.4 %collective-permute-start.1 = (bf16[128,7168]{1,0:T(8,128)(2,1)}, bf16[128,7168]{1,0:T(8,128)(2,1)}, u32[]{:S(2)}, u32[]{:S(2)}) collective-permute-start(bf16[128,7168]{1,0:T(8,128)(2,1)} %bitcast.7), channel_id=1, source_target_pairs={{0,1},{1,0},{2,3},{3,2},{4,5},{5,4},{6,7},{7,6},{8,9},{9,8},{10,11... | collective-permute-start | bytes 5505032 | tf_op jit(solution)/shard_map/ppermute | solution.py:297
  51.8 57.2 %collective-permute-start.2 = (bf16[128,7168]{1,0:T(8,128)(2,1)}, bf16[128,7168]{1,0:T(8,128)(2,1)}, u32[]{:S(2)}, u32[]{:S(2)}) collective-permute-start(bf16[128,7168]{1,0:T(8,128)(2,1)} %bitcast.9), channel_id=1, source_target_pairs={{0,1},{1,0},{2,3},{3,2},{4,5},{5,4},{6,7},{7,6},{8,9},{9,8},{10,11... | collective-permute-start | bytes 5505032 | tf_op jit(solution)/shard_map/ppermute | solution.py:297
  86.4 22.6 %all-to-all-start.1 = ((bf16[4,32,2,1408]{3,2,1,0:T(2,128)(2,1)}), bf16[4,32,2,1408]{3,2,1,0:T(2,128)(2,1)S(1)}, u32[]{:S(2)}, u32[]{:S(2)}) async-start(bf16[4,32,2,1408]{3,2,1,0:T(2,128)(2,1)} %broadcast_in_dim.2), calls=%async_computation.1 | async-start | bytes 1441792 | tf_op jit(solution)/shard_map/all_to_all | solution.py:291
  91.0 7.4 %collective-permute-start.3 = (bf16[32,2,1408]{2,1,0:T(2,128)(2,1)S(1)}, bf16[32,2,1408]{2,1,0:T(2,128)(2,1)S(1)}, u32[]{:S(2)}, u32[]{:S(2)}) collective-permute-start(bf16[32,2,1408]{2,1,0:T(2,128)(2,1)S(1)} %all-to-all-done), channel_id=1, source_target_pairs={{0,8},{8,0},{16,24},{24,16},{32,40},{40,32},{48,56},{56,48},{64,72... | collective-permute-start | bytes 540680 | tf_op jit(solution)/shard_map/ppermute | solution.py:300
  98.4 14.4 %collective-permute-start.4 = (bf16[32,2,1408]{2,1,0:T(2,128)(2,1)S(1)}, bf16[32,2,1408]{2,1,0:T(2,128)(2,1)S(1)}, u32[]{:S(2)}, u32[]{:S(2)}) collective-permute-start(bf16[32,2,1408]{2,1,0:T(2,128)(2,1)S(1)} %collective-permute-done.3.refs_0_), channel_id=1, source_target_pairs={{0,2},{2,0},{4,6},{6,4},{1,3},{3,1},{5,7},{7,5},{8,10},{10,8},{12,... | collective-permute-start | bytes 540680 | tf_op jit(solution)/shard_map/ppermute | solution.py:288
  102.4 10.4 %collective-permute-start.5 = (bf16[32,2,1408]{2,1,0:T(2,128)(2,1)S(1)}, bf16[32,2,1408]{2,1,0:T(2,128)(2,1)S(1)}, u32[]{:S(2)}, u32[]{:S(2)}) collective-permute-start(bf16[32,2,1408]{2,1,0:T(2,128)(2,1)S(1)} %collective-permute-done.3.refs_0_), channel_id=1, source_target_pairs={{0,4},{2,6},{4,0},{6,2},{1,5},{3,7},{5,1},{7,3},{8,12},{10,14},{12... | collective-permute-start | bytes 540680 | tf_op jit(solution)/shard_map/ppermute | solution.py:288
  107.0 8.6 %collective-permute-start.6 = (bf16[32,2,1408]{2,1,0:T(2,128)(2,1)S(1)}, bf16[32,2,1408]{2,1,0:T(2,128)(2,1)S(1)}, u32[]{:S(2)}, u32[]{:S(2)}) collective-permute-start(bf16[32,2,1408]{2,1,0:T(2,128)(2,1)S(1)} %collective-permute-done.3.refs_0_), channel_id=1, source_target_pairs={{0,6},{2,4},{4,2},{6,0},{1,7},{3,5},{5,3},{7,1},{8,14},{10,12},{12... | collective-permute-start | bytes 540680 | tf_op jit(solution)/shard_map/ppermute | solution.py:288
  118.6 13.5 %collective-permute-start.7 = (bf16[64,1408]{1,0:T(8,128)(2,1)S(1)}, bf16[64,1408]{1,0:T(8,128)(2,1)S(1)}, u32[]{:S(2)}, u32[]{:S(2)}) collective-permute-start(bf16[64,1408]{1,0:T(8,128)(2,1)S(1)} %get-tuple-element.20), channel_id=1, source_target_pairs={{0,2},{2,0},{4,6},{6,4},{1,3},{3,1},{5,7},{7,5},{8,10},{10,8},{12,... | collective-permute-start | bytes 540680 | tf_op jit(solution)/shard_map/ppermute | solution.py:288
  120.6 11.6 %collective-permute-start.8 = (bf16[64,1408]{1,0:T(8,128)(2,1)S(1)}, bf16[64,1408]{1,0:T(8,128)(2,1)S(1)}, u32[]{:S(2)}, u32[]{:S(2)}) collective-permute-start(bf16[64,1408]{1,0:T(8,128)(2,1)S(1)} %get-tuple-element.21), channel_id=1, source_target_pairs={{0,6},{2,4},{4,2},{6,0},{1,7},{3,5},{5,3},{7,1},{8,14},{10,12},{12... | collective-permute-start | bytes 540680 | tf_op jit(solution)/shard_map/ppermute | solution.py:288
  124.3 9.0 %collective-permute-start.9 = (bf16[64,1408]{1,0:T(8,128)(2,1)S(1)}, bf16[64,1408]{1,0:T(8,128)(2,1)S(1)}, u32[]{:S(2)}, u32[]{:S(2)}) collective-permute-start(bf16[64,1408]{1,0:T(8,128)(2,1)S(1)} %get-tuple-element.22), channel_id=1, source_target_pairs={{0,4},{2,6},{4,0},{6,2},{1,5},{3,7},{5,1},{7,3},{8,12},{10,14},{12... | collective-permute-start | bytes 540680 | tf_op jit(solution)/shard_map/ppermute | solution.py:288
  128.6 12.6 %all-to-all-start.2 = ((bf16[4,64,1408]{2,1,0:T(8,128)(2,1)}), bf16[4,64,1408]{2,1,0:T(8,128)(2,1)S(1)}, u32[]{:S(2)}, u32[]{:S(2)}) async-start(bf16[4,64,1408]{2,1,0:T(8,128)(2,1)} %get-tuple-element.18), calls=%async_computation.2 | async-start | bytes 1441792 | tf_op jit(solution)/shard_map/all_to_all | solution.py:291
  132.2 45.1 %copy-start = (s32[4,8]{1,0:T(4,128)S(1)}, s32[4,8]{1,0:T(4,128)}, u32[]{:S(2)}) copy-start(s32[4,8]{1,0:T(4,128)} %ids_ref.1) | copy-start | bytes 388
  132.2 45.1 %copy-start.1 = (s32[4,8]{1,0:T(4,128)S(1)}, s32[4,8]{1,0:T(4,128)}, u32[]{:S(2)}) copy-start(s32[4,8]{1,0:T(4,128)} %code_ref.1) | copy-start | bytes 388
  133.4 7.9 %collective-permute-start.10 = (bf16[64,1408]{1,0:T(8,128)(2,1)S(1)}, bf16[64,1408]{1,0:T(8,128)(2,1)S(1)}, u32[]{:S(2)}, u32[]{:S(2)}) collective-permute-start(bf16[64,1408]{1,0:T(8,128)(2,1)S(1)} %add_convert_fusion.1), channel_id=1, source_target_pairs={{0,8},{8,0},{16,24},{24,16},{32,40},{40,32},{48,56},{56,48},{64,72... | collective-permute-start | bytes 540680 | tf_op jit(solution)/shard_map/ppermute | solution.py:313

commit v8 on v7

--- a/solution.py
+++ b/solution.py
@@ -94,13 +94,8 @@
     )(here, in_hbm(ids), in_hbm(tokens))
 
 
-def mix_kernel(ids_ref, code_ref, x_ref, o_ref):
-    owners, _, width = x_ref.shape
-    rows = 2 * owners
-    tokens = o_ref.shape[0]
-    half = o_ref.shape[1] // 2
-    low = width - half
-    routes, side, part = routing(ids_ref, rows, 1)
+def route_kernel(ids_ref, code_ref, w_ref):
+    routes, side, part = routing(ids_ref, w_ref.shape[1], 1)
     mains, lowers, uppers = [], [], []
     for p in range(2):
         for t, (hits, first, third) in enumerate(routes):
@@ -109,9 +104,28 @@
             mains.append(first * code)
             lowers.append(third * (1 - part) * code)
             uppers.append(third * part * code)
-    weights = (jnp.concatenate(mains + lowers + uppers, axis=0).astype(F32) / 64.0).astype(BF)
-    x = x_ref[...].reshape(rows, width)
-    r = jnp.dot(weights, x, preferred_element_type=F32)
+    weights = jnp.concatenate(mains + lowers + uppers, axis=0).astype(F32) / 64.0
+    w_ref[...] = weights.astype(BF)
+
+
+def route_of(ids, codes, owners):
+    return pl.pallas_call(
+        route_kernel,
+        out_shape=jax.ShapeDtypeStruct((6 * ids.shape[0], 2 * owners), BF),
+        in_specs=[SM, SM],
+        out_specs=VM,
+        compiler_params=params(4),
+        name="route",
+    )(ids, codes)
+
+
+def mix_kernel(w_ref, x_ref, o_ref):
+    owners, _, width = x_ref.shape
+    tokens = o_ref.shape[0]
+    half = o_ref.shape[1] // 2
+    low = width - half
+    x = x_ref[...].reshape(2 * owners, width)
+    r = jnp.dot(w_ref[...], x, preferred_element_type=F32)
     n = 2 * tokens
     for p in range(2):
         at, main = p * half, r[p * tokens : (p + 1) * tokens, :half]
@@ -121,15 +135,15 @@
         o_ref[:, at + low : at + half] = (main[:, low:] + upper).astype(BF)
 
 
-def mixed_of(ids, codes, x, block):
+def mixed_of(weights, x, tokens, block):
     return pl.pallas_call(
         mix_kernel,
-        out_shape=jax.ShapeDtypeStruct((ids.shape[0], block), BF),
-        in_specs=[SM, SM, VM],
+        out_shape=jax.ShapeDtypeStruct((tokens, block), BF),
+        in_specs=[VM, VM],
         out_specs=VM,
         compiler_params=params(4),
         name="mix",
-    )(ids, codes, x)
+    )(weights, x)
 
 
 def start_of(here, odd, half, k, other, turned):
@@ -207,13 +221,12 @@
 
 
 def expert_kernel(here_ref, odd_ref, s_ref, *refs):
-    parts = (len(refs) - 4) // 2
-    pals, (g_ref, u_ref, d_ref, keep_ref) = refs[:parts], refs[parts : parts + 4]
-    give_refs = refs[parts + 4 :]
-    owners, _, width = pals[0].shape
+    parts = (len(refs) - 5) // 2
+    pals, (g_ref, u_ref, d_ref, a_ref, b_ref) = refs[:parts], refs[parts : parts + 5]
+    give_refs = refs[parts + 5 :]
+    owners = pals[0].shape[0]
     rows = 2 * owners
     half = d_ref.shape[1] // (2 * parts)
-    low = width - half
     odd, here = odd_ref[0], here_ref[0]
 
     gates, ups = [s_ref[0], s_ref[1]], [s_ref[2], s_ref[3]]
@@ -232,43 +245,70 @@
     even = lax.broadcasted_iota(I32, third.shape, 0) % 2 == 0
     lower = jnp.where(even, third, 0.0)
     upper = jnp.where(even, 0.0, pltpu.roll(third, 1, 0))
-    lhs = (
-        jnp.concatenate([hidden[:rows], lower], axis=0).astype(BF),
-        jnp.concatenate([hidden[:rows], upper], axis=0).astype(BF),
-    )
-    for other in (True, False):
-        for k in range(parts):
-            at = start_of(here, odd, half, k, other, other)
-            o_ref = give_refs[k] if other else keep_ref.at[k]
-            a = jnp.dot(lhs[0], d_ref[:, pl.ds(at, low)], preferred_element_type=F32)
-            cols = pl.ds(pl.multiple_of(at + low, 128), half - low)
-            b = jnp.dot(lhs[1], d_ref[:, cols], preferred_element_type=F32)
-            o_ref[:, :low] = a[:rows].astype(BF)
-            o_ref[:, low:half] = b[:rows].astype(BF)
-            o_ref[:, half : 2 * half - low] = (a[rows:, : half - low] + b[rows:]).astype(BF)
-            if 2 * low > half:
-                o_ref[:, 2 * half - low :] = a[rows:, half - low :].astype(BF)
+    a_ref[...] = jnp.concatenate([hidden[:rows], lower], axis=0).astype(BF)
+    b_ref[...] = jnp.concatenate([hidden[:rows], upper], axis=0).astype(BF)
+    for k in range(parts):
+        at = start_of(here, odd, half, k, True, True)
+        down_into(give_refs[k], a_ref[...], b_ref[...], d_ref, at, half)
+
+
+def down_into(o_ref, first, second, d_ref, at, half):
+    rows, width = o_ref.shape
+    low = width - half
+    a = jnp.dot(first, d_ref[:, pl.ds(at, low)], preferred_element_type=F32)
+    cols = pl.ds(pl.multiple_of(at + low, 128), half - low)
+    b = jnp.dot(second, d_ref[:, cols], preferred_element_type=F32)
+    o_ref[:, :low] = a[:rows].astype(BF)
+    o_ref[:, low:half] = b[:rows].astype(BF)
+    o_ref[:, half : 2 * half - low] = (a[rows:, : half - low] + b[rows:]).astype(BF)
+    if 2 * low > half:
+        o_ref[:, 2 * half - low :] = a[rows:, half - low :].astype(BF)
+
+
+def keep_kernel(odd_ref, a_ref, b_ref, d_ref, o_ref):
+    parts = o_ref.shape[0]
+    half = d_ref.shape[1] // (2 * parts)
+    for k in range(parts):
+        at = start_of(0, odd_ref[0], half, k, False, False)
+        down_into(o_ref.at[k], a_ref[...], b_ref[...], d_ref, at, half)
 
 
 def experts_of(here, odd, sums, pals, weights):
     parts = len(pals)
     owners, _, width = pals[0].shape
     units, features = weights[0].shape
+    lhs = jax.ShapeDtypeStruct((4 * owners, units), BF)
     one = jax.ShapeDtypeStruct((2 * owners, width), BF)
-    out = pl.pallas_call(
+    a, b, *give = pl.pallas_call(
         expert_kernel,
-        out_shape=(jax.ShapeDtypeStruct((parts, *one.shape), BF), *(one,) * parts),
+        out_shape=(lhs, lhs, *(one,) * parts),
         in_specs=[SM] * 2 + [VM] * (parts + 4),
-        out_specs=(VM,) * (parts + 1),
+        out_specs=(VM,) * (parts + 2),
         cost_estimate=pl.CostEstimate(
-            flops=16 * owners * units * features,
+            flops=12 * owners * units * features,
             bytes_accessed=6 * units * features,
             transcendentals=4 * owners * units,
         ),
         compiler_params=params(24),
         name="experts",
     )(here, odd, sums, *pals, *weights)
-    return out[0], out[1:]
+    return a, b, give
+
+
+def keep_of(odd, a, b, down, parts, shape):
+    return pl.pallas_call(
+        keep_kernel,
+        out_shape=jax.ShapeDtypeStruct((parts, *shape), BF),
+        in_specs=[SM, VM, VM, VM],
+        out_specs=VM,
+        cost_estimate=pl.CostEstimate(
+            flops=a.size * down.shape[1],
+            bytes_accessed=2 * down.size,
+            transcendentals=0,
+        ),
+        compiler_params=params(24),
+        name="keepdown",
+    )(odd, a, b, down)
 
 
 def shards(tokens, expert_ids, gate_codes, w_gate, w_up, w_down):
@@ -297,6 +337,7 @@
     other = [lax.ppermute(w, "sub", swap_sub) for w in own]
     packed = packed_of(here, expert_ids, tokens, owners, block)
     arrived = along(packed)
+    route = route_of(expert_ids, gate_codes, owners)
     partner = lax.ppermute(arrived, "expert", swap_pair)
     spread = jnp.broadcast_to(arrived[None], (parts, *arrived.shape))
     spread = across(spread)
@@ -304,17 +345,18 @@
     for k in swaps(parts):
         pals[k] = swapped(partner, k)
     *weights, sums = own_part(here, odd, spread, own, other)
-    keep, give = experts_of(here, odd, sums, pals, weights)
+    first, second, give = experts_of(here, odd, sums, pals, weights)
     given = [give[0]]
     for k in swaps(parts):
         given.append(swapped(give[k], k))
+    keep = keep_of(odd, first, second, weights[2], parts, give[0].shape)
     keep = across(keep)
     give = sum(x.astype(F32) for x in given).astype(BF)
     taken = lax.ppermute(give, "expert", swap_pair)
     both = jnp.sum(keep.astype(F32), axis=0) + taken.astype(F32)
     both = both.astype(BF).reshape(arrived.shape)
     back = along(both)
-    return mixed_of(expert_ids, gate_codes, back, block)
+    return mixed_of(route, back, rows, block)
 
 
 def swaps(parts):

time: 180 us -> 180 us (level)
  blocking collectives: 35.9 us -> 0 us
  waiting for transfers between devices: 45.9 us -> 76.5 us
  starting transfers between devices: 85.1 us -> 89.9 us
    all_to_all x1 -> x0, blocking collectives: 35.9 us -> none  [along(): return lax.all_to_all(x, 'expert', split_axis=0, concat_axis=0, tiled=True)]
    all_to_all x1 -> x2, waiting for transfers between devices: 31.2 us -> 61.8 us  [along(): return lax.all_to_all(x, 'expert', split_axis=0, concat_axis=0, tiled=True)]
    all_to_all x1 -> x2, starting transfers between devices: 45.8 us -> 50.6 us  [along(): return lax.all_to_all(x, 'expert', split_axis=0, concat_axis=0, tiled=True)]
    pallas_call x2 -> x4, Pallas kernels: 4.41 us -> 4.57 us  [the longest x1 1.8 us: experts_of(): pl.pallas_call(expert_kernel, out_shape=(lhs, lhs, *(one,) * parts), in_s...]
  transfers between devices with their start and end apart: 14 -> 15, of which waited for: 5 -> 5; matrix products, arithmetic and copies ran while one was open for 1% -> 1% of each run, Pallas kernels for 3% -> 4%
where the time goes in v8:
time: 180 us; the launch traced here: 179 us
  starting transfers between devices  89.9 us (50%)
  waiting for transfers between devices  76.5 us (42%)
  Pallas kernels  10.2 us (6%)
  local copies, waits for them, and re-layouts  1.99 us (1%)
    all_to_all x2, waiting for transfers between devices, along(): return lax.all_to_all(x, 'expert', split_axis=0, concat_axis=0, tiled=True)  61.8 us
    all_to_all x2, starting transfers between devices, along(): return lax.all_to_all(x, 'expert', split_axis=0, concat_axis=0, tiled=True)  50.6 us
    ppermute x6, starting transfers between devices, swapped(): return lax.ppermute(x, 'tensor', [(i, i ^ k) for i in range(parts)])  20.4 us
    all_to_all x2, starting transfers between devices, across(): return lax.all_to_all(x, 'tensor', split_axis=0, concat_axis=0, tiled=True)  8.16 us
    all_to_all x2, waiting for transfers between devices, across(): return lax.all_to_all(x, 'tensor', split_axis=0, concat_axis=0, tiled=True)  6.64 us
    ppermute x3, starting transfers between devices, shards(): other = [lax.ppermute(w, 'sub', swap_sub) for w in own]  6.34 us
    ppermute x1, waiting for transfers between devices, shards(): partner = lax.ppermute(arrived, 'expert', swap_pair)  5.18 us
    pallas_call x1, Pallas kernels, own_part(): pl.pallas_call(own_kernel, out_shape=(shape,) * 3 + (jax.ShapeDtypeStruct...  3.76 us
  transfers between devices with their start and end apart: 15, of which 5 were waited for; matrix products, arithmetic and copies ran while one was open for 1% of the time, Pallas kernels for 4%

profile of v8, /device:TPU:40, one launch (start us, length us, event | category | flops | bytes accessed | tf_op | source)
XLA Modules:
  0.0 179.1 jit_solution(16757250716962494310)
XLA Ops:
  0.0 1.9 %collective-permute-start = (bf16[128,7168]{1,0:T(8,128)(2,1)}, bf16[128,7168]{1,0:T(8,128)(2,1)S(1)}, u32[]{:S(2)}, u32[]{:S(2)}) collective-permute-start(bf16[128,7168]{1,0:T(8,128)(2,1)} %bitcast.5), channel_id=1, source_target_pairs={{0,1},{1,0},{2,3},{3,2},{4,5},{5,4},{6,7},{7,6},{8,9},{9,8},{10,11... | collective-permute-start | bytes 5505032 | tf_op jit(solution)/shard_map/ppermute | solution.py:337
  2.0 1.9 %pack.1 = bf16[32,2,1408]{2,1,0:T(2,128)(2,1)} custom-call(s32[1]{0:T(128)} %bitcast.1.here_ref, s32[4,8]{1,0:T(4,128)} %ids_hbm.1, bf16[4,7168]{1,0:T(4,128)(2,1)} %tok_hbm.1), custom_call_target="tpu_custom_call" | custom-call | tf_op jit(solution)/shard_map/pack/pallas_call | solution.py:82
  3.8 45.8 %all-to-all-start = ((bf16[32,2,1408]{2,1,0:T(2,128)(2,1)}), bf16[32,2,1408]{2,1,0:T(2,128)(2,1)S(1)}, u32[]{:S(2)}, u32[]{:S(2)}) async-start(bf16[32,2,1408]{2,1,0:T(2,128)(2,1)} %pack.1), calls=%async_computation | async-start | bytes 360448 | tf_op jit(solution)/shard_map/all_to_all | solution.py:334
  49.6 2.2 %collective-permute-start.1 = (bf16[128,7168]{1,0:T(8,128)(2,1)}, bf16[128,7168]{1,0:T(8,128)(2,1)}, u32[]{:S(2)}, u32[]{:S(2)}) collective-permute-start(bf16[128,7168]{1,0:T(8,128)(2,1)} %bitcast.7), channel_id=1, source_target_pairs={{0,1},{1,0},{2,3},{3,2},{4,5},{5,4},{6,7},{7,6},{8,9},{9,8},{10,11... | collective-permute-start | bytes 5505032 | tf_op jit(solution)/shard_map/ppermute | solution.py:337
  51.8 2.2 %collective-permute-start.2 = (bf16[128,7168]{1,0:T(8,128)(2,1)}, bf16[128,7168]{1,0:T(8,128)(2,1)}, u32[]{:S(2)}, u32[]{:S(2)}) collective-permute-start(bf16[128,7168]{1,0:T(8,128)(2,1)} %bitcast.9), channel_id=1, source_target_pairs={{0,1},{1,0},{2,3},{3,2},{4,5},{5,4},{6,7},{7,6},{8,9},{9,8},{10,11... | collective-permute-start | bytes 5505032 | tf_op jit(solution)/shard_map/ppermute | solution.py:337
  54.0 31.2 %all-to-all-done = bf16[32,2,1408]{2,1,0:T(2,128)(2,1)S(1)} async-done(((bf16[32,2,1408]{2,1,0:T(2,128)(2,1)}), bf16[32,2,1408]{2,1,0:T(2,128)(2,1)S(1)}, u32[]{:S(2)}, u32[]{:S(2)}) %all-to-all-start) | async-done | bytes 180256 | tf_op jit(solution)/shard_map/all_to_all | solution.py:334
  85.2 1.2 broadcast_in_dim.2
  86.4 4.6 %all-to-all-start.1 = ((bf16[4,32,2,1408]{3,2,1,0:T(2,128)(2,1)}), bf16[4,32,2,1408]{3,2,1,0:T(2,128)(2,1)S(1)}, u32[]{:S(2)}, u32[]{:S(2)}) async-start(bf16[4,32,2,1408]{3,2,1,0:T(2,128)(2,1)} %broadcast_in_dim.2), calls=%async_computation.1 | async-start | bytes 1441792 | tf_op jit(solution)/shard_map/all_to_all | solution.py:331
  91.0 2.2 %collective-permute-start.3 = (bf16[32,2,1408]{2,1,0:T(2,128)(2,1)S(1)}, bf16[32,2,1408]{2,1,0:T(2,128)(2,1)S(1)}, u32[]{:S(2)}, u32[]{:S(2)}) collective-permute-start(bf16[32,2,1408]{2,1,0:T(2,128)(2,1)S(1)} %all-to-all-done), channel_id=1, source_target_pairs={{0,8},{8,0},{16,24},{24,16},{32,40},{40,32},{48,56},{56,48},{64,72... | collective-permute-start | bytes 540680 | tf_op jit(solution)/shard_map/ppermute | solution.py:341
  93.2 5.2 %collective-permute-done.3.refs_0_ = bf16[32,2,1408]{2,1,0:T(2,128)(2,1)S(1)} collective-permute-done((bf16[32,2,1408]{2,1,0:T(2,128)(2,1)S(1)}, bf16[32,2,1408]{2,1,0:T(2,128)(2,1)S(1)}, u32[]{:S(2)}, u32[]{:S(2)}) %collective-permute-start.3) | collective-permute-done | bytes 180256 | tf_op jit(solution)/shard_map/ppermute | solution.py:341
  98.4 4.0 %collective-permute-start.4 = (bf16[32,2,1408]{2,1,0:T(2,128)(2,1)S(1)}, bf16[32,2,1408]{2,1,0:T(2,128)(2,1)S(1)}, u32[]{:S(2)}, u32[]{:S(2)}) collective-permute-start(bf16[32,2,1408]{2,1,0:T(2,128)(2,1)S(1)} %collective-permute-done.3.refs_0_), channel_id=1, source_target_pairs={{0,2},{2,0},{4,6},{6,4},{1,3},{3,1},{5,7},{7,5},{8,10},{10,8},{12,... | collective-permute-start | bytes 540680 | tf_op jit(solution)/shard_map/ppermute | solution.py:328
  102.4 4.6 %collective-permute-start.5 = (bf16[32,2,1408]{2,1,0:T(2,128)(2,1)S(1)}, bf16[32,2,1408]{2,1,0:T(2,128)(2,1)S(1)}, u32[]{:S(2)}, u32[]{:S(2)}) collective-permute-start(bf16[32,2,1408]{2,1,0:T(2,128)(2,1)S(1)} %collective-permute-done.3.refs_0_), channel_id=1, source_target_pairs={{0,4},{2,6},{4,0},{6,2},{1,5},{3,7},{5,1},{7,3},{8,12},{10,14},{12... | collective-permute-start | bytes 540680 | tf_op jit(solution)/shard_map/ppermute | solution.py:328
  107.0 2.0 %collective-permute-start.6 = (bf16[32,2,1408]{2,1,0:T(2,128)(2,1)S(1)}, bf16[32,2,1408]{2,1,0:T(2,128)(2,1)S(1)}, u32[]{:S(2)}, u32[]{:S(2)}) collective-permute-start(bf16[32,2,1408]{2,1,0:T(2,128)(2,1)S(1)} %collective-permute-done.3.refs_0_), channel_id=1, source_target_pairs={{0,6},{2,4},{4,2},{6,0},{1,7},{3,5},{5,3},{7,1},{8,14},{10,12},{12... | collective-permute-start | bytes 540680 | tf_op jit(solution)/shard_map/ppermute | solution.py:328
  109.0 3.8 %ownpart.1 = (bf16[256,7168]{1,0:T(8,128)(2,1)S(1)}, bf16[256,7168]{1,0:T(8,128)(2,1)S(1)}, bf16[256,7168]{1,0:T(8,128)(2,1)S(1)}, f32[4,128,256]{2,1,0:T(8,128)S(1)}) custom-call(s32[1]{0:T(128)} %bitcast.1.here_ref, s32[1]{0:T(128)} %bitcast.odd_ref, bf16[4,32,2,1408]{3,2,1,0:T(2,128)(2,1)S(1)} %all-to-all-done.1.refs_0_, bf16[128,7168]{1,0:T(8,128)(2,1)} %bitcast.6, ...), custom_call_target="tpu_custom_call" | custom-call | flops 469762048 | bytes 22020096 | tf_op jit(solution)/shard_map/ownpart/pallas_call | solution.py:207
  112.8 2.8 %collective-permute-done.6.refs_3_ = bf16[32,2,1408]{2,1,0:T(2,128)(2,1)S(1)} collective-permute-done((bf16[32,2,1408]{2,1,0:T(2,128)(2,1)S(1)}, bf16[32,2,1408]{2,1,0:T(2,128)(2,1)S(1)}, u32[]{:S(2)}, u32[]{:S(2)}) %collective-permute-start.6) | collective-permute-done | bytes 180256 | tf_op jit(solution)/shard_map/ppermute | solution.py:328
  115.6 1.8 %experts.1 = (bf16[128,256]{1,0:T(8,128)(2,1)S(1)}, bf16[128,256]{1,0:T(8,128)(2,1)S(1)}, bf16[64,1408]{1,0:T(8,128)(2,1)S(1)}, bf16[64,1408]{1,0:T(8,128)(2,1)S...) custom-call(s32[1]{0:T(128)} %bitcast.1.here_ref, s32[1]{0:T(128)} %bitcast.odd_ref, ...), custom_call_target="tpu_custom_call" | custom-call | flops 704643072 | bytes 11010048 | tf_op jit(solution)/shard_map/experts/pallas_call | solution.py:282
  117.5 2.0 %collective-permute-start.7 = (bf16[64,1408]{1,0:T(8,128)(2,1)S(1)}, bf16[64,1408]{1,0:T(8,128)(2,1)S(1)}, u32[]{:S(2)}, u32[]{:S(2)}) collective-permute-start(bf16[64,1408]{1,0:T(8,128)(2,1)S(1)} %get-tuple-element.22), channel_id=1, source_target_pairs={{0,2},{2,0},{4,6},{6,4},{1,3},{3,1},{5,7},{7,5},{8,10},{10,8},{12,... | collective-permute-start | bytes 540680 | tf_op jit(solution)/shard_map/ppermute | solution.py:328
  119.4 3.7 %collective-permute-start.8 = (bf16[64,1408]{1,0:T(8,128)(2,1)S(1)}, bf16[64,1408]{1,0:T(8,128)(2,1)S(1)}, u32[]{:S(2)}, u32[]{:S(2)}) collective-permute-start(bf16[64,1408]{1,0:T(8,128)(2,1)S(1)} %get-tuple-element.23), channel_id=1, source_target_pairs={{0,6},{2,4},{4,2},{6,0},{1,7},{3,5},{5,3},{7,1},{8,14},{10,12},{12... | collective-permute-start | bytes 540680 | tf_op jit(solution)/shard_map/ppermute | solution.py:328
  123.2 4.2 %collective-permute-start.9 = (bf16[64,1408]{1,0:T(8,128)(2,1)S(1)}, bf16[64,1408]{1,0:T(8,128)(2,1)S(1)}, u32[]{:S(2)}, u32[]{:S(2)}) collective-permute-start(bf16[64,1408]{1,0:T(8,128)(2,1)S(1)} %get-tuple-element.24), channel_id=1, source_target_pairs={{0,4},{2,6},{4,0},{6,2},{1,5},{3,7},{5,1},{7,3},{8,12},{10,14},{12... | collective-permute-start | bytes 540680 | tf_op jit(solution)/shard_map/ppermute | solution.py:328
  127.4 1.3 keepdown.1
  128.7 3.6 %all-to-all-start.2 = ((bf16[4,64,1408]{2,1,0:T(8,128)(2,1)}), bf16[4,64,1408]{2,1,0:T(8,128)(2,1)S(1)}, u32[]{:S(2)}, u32[]{:S(2)}) async-start(bf16[4,64,1408]{2,1,0:T(8,128)(2,1)} %keepdown.1), calls=%async_computation.2 | async-start | bytes 1441792 | tf_op jit(solution)/shard_map/all_to_all | solution.py:331
  132.3 0.0 copy-start
  132.3 0.0 copy-start.1
  132.4 0.1 add_convert_fusion.1
  132.5 2.2 %collective-permute-start.10 = (bf16[64,1408]{1,0:T(8,128)(2,1)S(1)}, bf16[64,1408]{1,0:T(8,128)(2,1)S(1)}, u32[]{:S(2)}, u32[]{:S(2)}) collective-permute-start(bf16[64,1408]{1,0:T(8,128)(2,1)S(1)} %add_convert_fusion.1), channel_id=1, source_target_pairs={{0,8},{8,0},{16,24},{24,16},{32,40},{40,32},{48,56},{56,48},{64,72... | collective-permute-start | bytes 540680 | tf_op jit(solution)/shard_map/ppermute | solution.py:355
  134.7 6.6 %all-to-all-done.2 = bf16[4,64,1408]{2,1,0:T(8,128)(2,1)S(1)} async-done(((bf16[4,64,1408]{2,1,0:T(8,128)(2,1)}), bf16[4,64,1408]{2,1,0:T(8,128)(2,1)S(1)}, u32[]{:S(2)}, u32[]{:S(2)}) %all-to-all-start.2) | async-done | bytes 720928 | tf_op jit(solution)/shard_map/all_to_all | solution.py:331
  141.4 0.1 convert_reduce_fusion
  141.5 0.7 reshape.12
  142.3 4.8 %all-to-all-start.3 = ((bf16[32,2,1408]{2,1,0:T(2,128)(2,1)}), bf16[32,2,1408]{2,1,0:T(2,128)(2,1)S(1)}, u32[]{:S(2)}, u32[]{:S(2)}) async-start(bf16[32,2,1408]{2,1,0:T(2,128)(2,1)} %reshape.12), calls=%async_computation.3 | async-start | bytes 360448 | tf_op jit(solution)/shard_map/all_to_all | solution.py:334
  147.1 0.6 route.1.w_ref
  147.7 30.7 %all-to-all-done.3.x_ref = bf16[32,2,1408]{2,1,0:T(2,128)(2,1)S(1)} async-done(((bf16[32,2,1408]{2,1,0:T(2,128)(2,1)}), bf16[32,2,1408]{2,1,0:T(2,128)(2,1)S(1)}, u32[]{:S(2)}, u32[]{:S(2)}) %all-to-all-start.3) | async-done | bytes 180256 | tf_op jit(solution)/shard_map/all_to_all | solution.py:334
  178.4 0.8 mix.1
  (13 shorter events, 0.1 us)
Async XLA Ops:
  0.0 107.0 %collective-permute-start = (bf16[128,7168]{1,0:T(8,128)(2,1)}, bf16[128,7168]{1,0:T(8,128)(2,1)S(1)}, u32[]{:S(2)}, u32[]{:S(2)}) collective-permute-start(bf16[128,7168]{1,0:T(8,128)(2,1)} %bitcast.5), channel_id=1, source_target_pairs={{0,1},{1,0},{2,3},{3,2},{4,5},{5,4},{6,7},{7,6},{8,9},{9,8},{10,11... | collective-permute-start | bytes 5505032 | tf_op jit(solution)/shard_map/ppermute | solution.py:337
  3.8 81.4 %all-to-all-start = ((bf16[32,2,1408]{2,1,0:T(2,128)(2,1)}), bf16[32,2,1408]{2,1,0:T(2,128)(2,1)S(1)}, u32[]{:S(2)}, u32[]{:S(2)}) async-start(bf16[32,2,1408]{2,1,0:T(2,128)(2,1)} %pack.1), calls=%async_computation | async-start | bytes 360448 | tf_op jit(solution)/shard_map/all_to_all | solution.py:334
  49.6 59.4 %collective-permute-start.1 = (bf16[128,7168]{1,0:T(8,128)(2,1)}, bf16[128,7168]{1,0:T(8,128)(2,1)}, u32[]{:S(2)}, u32[]{:S(2)}) collective-permute-start(bf16[128,7168]{1,0:T(8,128)(2,1)} %bitcast.7), channel_id=1, source_target_pairs={{0,1},{1,0},{2,3},{3,2},{4,5},{5,4},{6,7},{7,6},{8,9},{9,8},{10,11... | collective-permute-start | bytes 5505032 | tf_op jit(solution)/shard_map/ppermute | solution.py:337
  51.8 57.2 %collective-permute-start.2 = (bf16[128,7168]{1,0:T(8,128)(2,1)}, bf16[128,7168]{1,0:T(8,128)(2,1)}, u32[]{:S(2)}, u32[]{:S(2)}) collective-permute-start(bf16[128,7168]{1,0:T(8,128)(2,1)} %bitcast.9), channel_id=1, source_target_pairs={{0,1},{1,0},{2,3},{3,2},{4,5},{5,4},{6,7},{7,6},{8,9},{9,8},{10,11... | collective-permute-start | bytes 5505032 | tf_op jit(solution)/shard_map/ppermute | solution.py:337
  86.4 22.6 %all-to-all-start.1 = ((bf16[4,32,2,1408]{3,2,1,0:T(2,128)(2,1)}), bf16[4,32,2,1408]{3,2,1,0:T(2,128)(2,1)S(1)}, u32[]{:S(2)}, u32[]{:S(2)}) async-start(bf16[4,32,2,1408]{3,2,1,0:T(2,128)(2,1)} %broadcast_in_dim.2), calls=%async_computation.1 | async-start | bytes 1441792 | tf_op jit(solution)/shard_map/all_to_all | solution.py:331
  91.0 7.4 %collective-permute-start.3 = (bf16[32,2,1408]{2,1,0:T(2,128)(2,1)S(1)}, bf16[32,2,1408]{2,1,0:T(2,128)(2,1)S(1)}, u32[]{:S(2)}, u32[]{:S(2)}) collective-permute-start(bf16[32,2,1408]{2,1,0:T(2,128)(2,1)S(1)} %all-to-all-done), channel_id=1, source_target_pairs={{0,8},{8,0},{16,24},{24,16},{32,40},{40,32},{48,56},{56,48},{64,72... | collective-permute-start | bytes 540680 | tf_op jit(solution)/shard_map/ppermute | solution.py:341
  98.4 14.4 %collective-permute-start.4 = (bf16[32,2,1408]{2,1,0:T(2,128)(2,1)S(1)}, bf16[32,2,1408]{2,1,0:T(2,128)(2,1)S(1)}, u32[]{:S(2)}, u32[]{:S(2)}) collective-permute-start(bf16[32,2,1408]{2,1,0:T(2,128)(2,1)S(1)} %collective-permute-done.3.refs_0_), channel_id=1, source_target_pairs={{0,2},{2,0},{4,6},{6,4},{1,3},{3,1},{5,7},{7,5},{8,10},{10,8},{12,... | collective-permute-start | bytes 540680 | tf_op jit(solution)/shard_map/ppermute | solution.py:328
  102.4 10.4 %collective-permute-start.5 = (bf16[32,2,1408]{2,1,0:T(2,128)(2,1)S(1)}, bf16[32,2,1408]{2,1,0:T(2,128)(2,1)S(1)}, u32[]{:S(2)}, u32[]{:S(2)}) collective-permute-start(bf16[32,2,1408]{2,1,0:T(2,128)(2,1)S(1)} %collective-permute-done.3.refs_0_), channel_id=1, source_target_pairs={{0,4},{2,6},{4,0},{6,2},{1,5},{3,7},{5,1},{7,3},{8,12},{10,14},{12... | collective-permute-start | bytes 540680 | tf_op jit(solution)/shard_map/ppermute | solution.py:328
  107.0 8.6 %collective-permute-start.6 = (bf16[32,2,1408]{2,1,0:T(2,128)(2,1)S(1)}, bf16[32,2,1408]{2,1,0:T(2,128)(2,1)S(1)}, u32[]{:S(2)}, u32[]{:S(2)}) collective-permute-start(bf16[32,2,1408]{2,1,0:T(2,128)(2,1)S(1)} %collective-permute-done.3.refs_0_), channel_id=1, source_target_pairs={{0,6},{2,4},{4,2},{6,0},{1,7},{3,5},{5,3},{7,1},{8,14},{10,12},{12... | collective-permute-start | bytes 540680 | tf_op jit(solution)/shard_map/ppermute | solution.py:328
  117.5 14.9 %collective-permute-start.7 = (bf16[64,1408]{1,0:T(8,128)(2,1)S(1)}, bf16[64,1408]{1,0:T(8,128)(2,1)S(1)}, u32[]{:S(2)}, u32[]{:S(2)}) collective-permute-start(bf16[64,1408]{1,0:T(8,128)(2,1)S(1)} %get-tuple-element.22), channel_id=1, source_target_pairs={{0,2},{2,0},{4,6},{6,4},{1,3},{3,1},{5,7},{7,5},{8,10},{10,8},{12,... | collective-permute-start | bytes 540680 | tf_op jit(solution)/shard_map/ppermute | solution.py:328
  119.4 12.9 %collective-permute-start.8 = (bf16[64,1408]{1,0:T(8,128)(2,1)S(1)}, bf16[64,1408]{1,0:T(8,128)(2,1)S(1)}, u32[]{:S(2)}, u32[]{:S(2)}) collective-permute-start(bf16[64,1408]{1,0:T(8,128)(2,1)S(1)} %get-tuple-element.23), channel_id=1, source_target_pairs={{0,6},{2,4},{4,2},{6,0},{1,7},{3,5},{5,3},{7,1},{8,14},{10,12},{12... | collective-permute-start | bytes 540680 | tf_op jit(solution)/shard_map/ppermute | solution.py:328
  123.2 9.2 %collective-permute-start.9 = (bf16[64,1408]{1,0:T(8,128)(2,1)S(1)}, bf16[64,1408]{1,0:T(8,128)(2,1)S(1)}, u32[]{:S(2)}, u32[]{:S(2)}) collective-permute-start(bf16[64,1408]{1,0:T(8,128)(2,1)S(1)} %get-tuple-element.24), channel_id=1, source_target_pairs={{0,4},{2,6},{4,0},{6,2},{1,5},{3,7},{5,1},{7,3},{8,12},{10,14},{12... | collective-permute-start | bytes 540680 | tf_op jit(solution)/shard_map/ppermute | solution.py:328
  128.7 12.6 %all-to-all-start.2 = ((bf16[4,64,1408]{2,1,0:T(8,128)(2,1)}), bf16[4,64,1408]{2,1,0:T(8,128)(2,1)S(1)}, u32[]{:S(2)}, u32[]{:S(2)}) async-start(bf16[4,64,1408]{2,1,0:T(8,128)(2,1)} %keepdown.1), calls=%async_computation.2 | async-start | bytes 1441792 | tf_op jit(solution)/shard_map/all_to_all | solution.py:331
  132.3 14.7 %copy-start = (s32[4,8]{1,0:T(4,128)S(1)}, s32[4,8]{1,0:T(4,128)}, u32[]{:S(2)}) copy-start(s32[4,8]{1,0:T(4,128)} %ids_hbm.1) | copy-start | bytes 388
  132.3 14.7 %copy-start.1 = (s32[4,8]{1,0:T(4,128)S(1)}, s32[4,8]{1,0:T(4,128)}, u32[]{:S(2)}) copy-start(s32[4,8]{1,0:T(4,128)} %code_ref.1) | copy-start | bytes 388
  132.5 9.0 %collective-permute-start.10 = (bf16[64,1408]{1,0:T(8,128)(2,1)S(1)}, bf16[64,1408]{1,0:T(8,128)(2,1)S(1)}, u32[]{:S(2)}, u32[]{:S(2)}) collective-permute-start(bf16[64,1408]{1,0:T(8,128)(2,1)S(1)} %add_convert_fusion.1), channel_id=1, source_target_pairs={{0,8},{8,0},{16,24},{24,16},{32,40},{40,32},{48,56},{56,48},{64,72... | collective-permute-start | bytes 540680 | tf_op jit(solution)/shard_map/ppermute | solution.py:355
  142.3 36.1 %all-to-all-start.3 = ((bf16[32,2,1408]{2,1,0:T(2,128)(2,1)}), bf16[32,2,1408]{2,1,0:T(2,128)(2,1)S(1)}, u32[]{:S(2)}, u32[]{:S(2)}) async-start(bf16[32,2,1408]{2,1,0:T(2,128)(2,1)} %reshape.12), calls=%async_computation.3 | async-start | bytes 360448 | tf_op jit(solution)/shard_map/all_to_all | solution.py:334

commit v9 on v8

--- a/solution.py
+++ b/solution.py
@@ -252,25 +252,35 @@
         down_into(give_refs[k], a_ref[...], b_ref[...], d_ref, at, half)
 
 
-def down_into(o_ref, first, second, d_ref, at, half):
+def down_into(o_ref, first, second, d_ref, at, half, extra=None):
     rows, width = o_ref.shape
     low = width - half
     a = jnp.dot(first, d_ref[:, pl.ds(at, low)], preferred_element_type=F32)
     cols = pl.ds(pl.multiple_of(at + low, 128), half - low)
     b = jnp.dot(second, d_ref[:, cols], preferred_element_type=F32)
-    o_ref[:, :low] = a[:rows].astype(BF)
-    o_ref[:, low:half] = b[:rows].astype(BF)
-    o_ref[:, half : 2 * half - low] = (a[rows:, : half - low] + b[rows:]).astype(BF)
+
+    def put(lo, value):
+        hi = lo + value.shape[1]
+        if extra is not None:
+            value = value + extra[:, lo:hi].astype(F32)
+        o_ref[:, lo:hi] = value.astype(BF)
+
+    put(0, a[:rows])
+    put(low, b[:rows])
+    put(half, a[rows:, : half - low] + b[rows:])
     if 2 * low > half:
-        o_ref[:, 2 * half - low :] = a[rows:, half - low :].astype(BF)
-
-
-def keep_kernel(odd_ref, a_ref, b_ref, d_ref, o_ref):
+        put(2 * half - low, a[rows:, half - low :])
+
+
+def keep_body(far, here_ref, odd_ref, a_ref, b_ref, extra_ref, d_ref, o_ref):
     parts = o_ref.shape[0]
     half = d_ref.shape[1] // (2 * parts)
+    here = here_ref[0]
     for k in range(parts):
-        at = start_of(0, odd_ref[0], half, k, False, False)
-        down_into(o_ref.at[k], a_ref[...], b_ref[...], d_ref, at, half)
+        at = start_of(here, odd_ref[0], half, k, False, True)
+        extra = extra_ref[...] if k == far else None
+        block = o_ref.at[lax.bitwise_xor(here, jnp.int32(k))]
+        down_into(block, a_ref[...], b_ref[...], d_ref, at, half, extra)
 
 
 def experts_of(here, odd, sums, pals, weights):
@@ -295,11 +305,14 @@
     return a, b, give
 
 
-def keep_of(odd, a, b, down, parts, shape):
-    return pl.pallas_call(
-        keep_kernel,
-        out_shape=jax.ShapeDtypeStruct((parts, *shape), BF),
-        in_specs=[SM, VM, VM, VM],
+def keep_of(here, odd, far, a, b, extra, down, parts):
+    def kernel(*refs):
+        keep_body(far, *refs)
+
+    return pl.pallas_call(
+        kernel,
+        out_shape=jax.ShapeDtypeStruct((parts, *extra.shape), BF),
+        in_specs=[SM, SM, VM, VM, VM, VM],
         out_specs=VM,
         cost_estimate=pl.CostEstimate(
             flops=a.size * down.shape[1],
@@ -308,7 +321,7 @@
         ),
         compiler_params=params(24),
         name="keepdown",
-    )(odd, a, b, down)
+    )(here, odd, a, b, extra, down)
 
 
 def shards(tokens, expert_ids, gate_codes, w_gate, w_up, w_down):
@@ -341,15 +354,19 @@
     partner = lax.ppermute(arrived, "expert", swap_pair)
     spread = jnp.broadcast_to(arrived[None], (parts, *arrived.shape))
     spread = across(spread)
-    pals = [partner] + [None] * (parts - 1)
-    for k in swaps(parts):
+    far, near = swaps(parts)
+    pals = {0: partner}
+    for k in near:
         pals[k] = swapped(partner, k)
+    pals[far] = swapped(partner, far)
+    pals = [pals[k] for k in range(parts)]
     *weights, sums = own_part(here, odd, spread, own, other)
     first, second, give = experts_of(here, odd, sums, pals, weights)
+    extra = lax.ppermute(give[far], "expert", swap_pair)
     given = [give[0]]
-    for k in swaps(parts):
+    for k in near:
         given.append(swapped(give[k], k))
-    keep = keep_of(odd, first, second, weights[2], parts, give[0].shape)
+    keep = keep_of(here, odd, far, first, second, extra, weights[2], parts)
     keep = across(keep)
     give = sum(x.astype(F32) for x in given).astype(BF)
     taken = lax.ppermute(give, "expert", swap_pair)
@@ -360,7 +377,8 @@
 
 
 def swaps(parts):
-    return sorted(range(1, parts), key=lambda k: k == parts // 2)
+    far = parts // 2
+    return far, [k for k in range(1, parts) if k != far]
 
 
 def solution(mesh):

time: 180 us -> 180 us (level)
    ppermute x6 -> x5, starting transfers between devices: 20.4 us -> 16.2 us  [swapped(): return lax.ppermute(x, 'tensor', [(i, i ^ k) for i in range(parts)])]
    ppermute x0 -> x1, starting transfers between devices: none -> 2.23 us  [shards(): extra = lax.ppermute(give[far], 'expert', swap_pair)]
where the time goes in v9:
time: 180 us; the launch traced here: 179 us
  starting transfers between devices  89.4 us (50%)
  waiting for transfers between devices  77.3 us (43%)
  Pallas kernels  10.2 us (6%)
  local copies, waits for them, and re-layouts  1.99 us (1%)
    all_to_all x2, waiting for transfers between devices, along(): return lax.all_to_all(x, 'expert', split_axis=0, concat_axis=0, tiled=True)  62.9 us
    all_to_all x2, starting transfers between devices, along(): return lax.all_to_all(x, 'expert', split_axis=0, concat_axis=0, tiled=True)  50.6 us
    ppermute x5, starting transfers between devices, swapped(): return lax.ppermute(x, 'tensor', [(i, i ^ k) for i in range(parts)])  16.2 us
    all_to_all x2, starting transfers between devices, across(): return lax.all_to_all(x, 'tensor', split_axis=0, concat_axis=0, tiled=True)  8.16 us
    all_to_all x2, waiting for transfers between devices, across(): return lax.all_to_all(x, 'tensor', split_axis=0, concat_axis=0, tiled=True)  6.36 us
    ppermute x3, starting transfers between devices, shards(): other = [lax.ppermute(w, 'sub', swap_sub) for w in own]  6.34 us
    ppermute x1, waiting for transfers between devices, shards(): partner = lax.ppermute(arrived, 'expert', swap_pair)  5.18 us
    pallas_call x1, Pallas kernels, own_part(): pl.pallas_call(own_kernel, out_shape=(shape,) * 3 + (jax.ShapeDtypeStruct...  3.76 us
  transfers between devices with their start and end apart: 15, of which 5 were waited for; matrix products, arithmetic and copies ran while one was open for 1% of the time, Pallas kernels for 4%

profile of v9, /device:TPU:40, one launch (start us, length us, event | category | flops | bytes accessed | tf_op | source)
XLA Modules:
  0.0 179.4 jit_solution(17336437594927392723)
XLA Ops:
  0.0 1.9 %collective-permute-start = (bf16[128,7168]{1,0:T(8,128)(2,1)}, bf16[128,7168]{1,0:T(8,128)(2,1)S(1)}, u32[]{:S(2)}, u32[]{:S(2)}) collective-permute-start(bf16[128,7168]{1,0:T(8,128)(2,1)} %bitcast.5), channel_id=1, source_target_pairs={{0,1},{1,0},{2,3},{3,2},{4,5},{5,4},{6,7},{7,6},{8,9},{9,8},{10,11... | collective-permute-start | bytes 5505032 | tf_op jit(solution)/shard_map/ppermute | solution.py:350
  2.0 1.9 %pack.1 = bf16[32,2,1408]{2,1,0:T(2,128)(2,1)} custom-call(s32[1]{0:T(128)} %bitcast.here_ref.refs_0_, s32[4,8]{1,0:T(4,128)} %ids_hbm.1, bf16[4,7168]{1,0:T(4,128)(2,1)} %tok_hbm.1), custom_call_target="tpu_custom_call" | custom-call | tf_op jit(solution)/shard_map/pack/pallas_call | solution.py:82
  3.8 45.8 %all-to-all-start = ((bf16[32,2,1408]{2,1,0:T(2,128)(2,1)}), bf16[32,2,1408]{2,1,0:T(2,128)(2,1)S(1)}, u32[]{:S(2)}, u32[]{:S(2)}) async-start(bf16[32,2,1408]{2,1,0:T(2,128)(2,1)} %pack.1), calls=%async_computation | async-start | bytes 360448 | tf_op jit(solution)/shard_map/all_to_all | solution.py:347
  49.6 2.2 %collective-permute-start.1 = (bf16[128,7168]{1,0:T(8,128)(2,1)}, bf16[128,7168]{1,0:T(8,128)(2,1)}, u32[]{:S(2)}, u32[]{:S(2)}) collective-permute-start(bf16[128,7168]{1,0:T(8,128)(2,1)} %bitcast.7), channel_id=1, source_target_pairs={{0,1},{1,0},{2,3},{3,2},{4,5},{5,4},{6,7},{7,6},{8,9},{9,8},{10,11... | collective-permute-start | bytes 5505032 | tf_op jit(solution)/shard_map/ppermute | solution.py:350
  51.8 2.2 %collective-permute-start.2 = (bf16[128,7168]{1,0:T(8,128)(2,1)}, bf16[128,7168]{1,0:T(8,128)(2,1)}, u32[]{:S(2)}, u32[]{:S(2)}) collective-permute-start(bf16[128,7168]{1,0:T(8,128)(2,1)} %bitcast.9), channel_id=1, source_target_pairs={{0,1},{1,0},{2,3},{3,2},{4,5},{5,4},{6,7},{7,6},{8,9},{9,8},{10,11... | collective-permute-start | bytes 5505032 | tf_op jit(solution)/shard_map/ppermute | solution.py:350
  54.0 31.2 %all-to-all-done = bf16[32,2,1408]{2,1,0:T(2,128)(2,1)S(1)} async-done(((bf16[32,2,1408]{2,1,0:T(2,128)(2,1)}), bf16[32,2,1408]{2,1,0:T(2,128)(2,1)S(1)}, u32[]{:S(2)}, u32[]{:S(2)}) %all-to-all-start) | async-done | bytes 180256 | tf_op jit(solution)/shard_map/all_to_all | solution.py:347
  85.2 1.2 broadcast_in_dim.2
  86.4 4.6 %all-to-all-start.1 = ((bf16[4,32,2,1408]{3,2,1,0:T(2,128)(2,1)}), bf16[4,32,2,1408]{3,2,1,0:T(2,128)(2,1)S(1)}, u32[]{:S(2)}, u32[]{:S(2)}) async-start(bf16[4,32,2,1408]{3,2,1,0:T(2,128)(2,1)} %broadcast_in_dim.2), calls=%async_computation.1 | async-start | bytes 1441792 | tf_op jit(solution)/shard_map/all_to_all | solution.py:344
  91.0 2.2 %collective-permute-start.3 = (bf16[32,2,1408]{2,1,0:T(2,128)(2,1)S(1)}, bf16[32,2,1408]{2,1,0:T(2,128)(2,1)S(1)}, u32[]{:S(2)}, u32[]{:S(2)}) collective-permute-start(bf16[32,2,1408]{2,1,0:T(2,128)(2,1)S(1)} %all-to-all-done), channel_id=1, source_target_pairs={{0,8},{8,0},{16,24},{24,16},{32,40},{40,32},{48,56},{56,48},{64,72... | collective-permute-start | bytes 540680 | tf_op jit(solution)/shard_map/ppermute | solution.py:354
  93.2 5.2 %collective-permute-done.3.refs_0_ = bf16[32,2,1408]{2,1,0:T(2,128)(2,1)S(1)} collective-permute-done((bf16[32,2,1408]{2,1,0:T(2,128)(2,1)S(1)}, bf16[32,2,1408]{2,1,0:T(2,128)(2,1)S(1)}, u32[]{:S(2)}, u32[]{:S(2)}) %collective-permute-start.3) | collective-permute-done | bytes 180256 | tf_op jit(solution)/shard_map/ppermute | solution.py:354
  98.4 4.0 %collective-permute-start.4 = (bf16[32,2,1408]{2,1,0:T(2,128)(2,1)S(1)}, bf16[32,2,1408]{2,1,0:T(2,128)(2,1)S(1)}, u32[]{:S(2)}, u32[]{:S(2)}) collective-permute-start(bf16[32,2,1408]{2,1,0:T(2,128)(2,1)S(1)} %collective-permute-done.3.refs_0_), channel_id=1, source_target_pairs={{0,2},{2,0},{4,6},{6,4},{1,3},{3,1},{5,7},{7,5},{8,10},{10,8},{12,... | collective-permute-start | bytes 540680 | tf_op jit(solution)/shard_map/ppermute | solution.py:341
  102.4 4.6 %collective-permute-start.5 = (bf16[32,2,1408]{2,1,0:T(2,128)(2,1)S(1)}, bf16[32,2,1408]{2,1,0:T(2,128)(2,1)S(1)}, u32[]{:S(2)}, u32[]{:S(2)}) collective-permute-start(bf16[32,2,1408]{2,1,0:T(2,128)(2,1)S(1)} %collective-permute-done.3.refs_0_), channel_id=1, source_target_pairs={{0,4},{2,6},{4,0},{6,2},{1,5},{3,7},{5,1},{7,3},{8,12},{10,14},{12... | collective-permute-start | bytes 540680 | tf_op jit(solution)/shard_map/ppermute | solution.py:341
  107.0 2.0 %collective-permute-start.6 = (bf16[32,2,1408]{2,1,0:T(2,128)(2,1)S(1)}, bf16[32,2,1408]{2,1,0:T(2,128)(2,1)S(1)}, u32[]{:S(2)}, u32[]{:S(2)}) collective-permute-start(bf16[32,2,1408]{2,1,0:T(2,128)(2,1)S(1)} %collective-permute-done.3.refs_0_), channel_id=1, source_target_pairs={{0,6},{2,4},{4,2},{6,0},{1,7},{3,5},{5,3},{7,1},{8,14},{10,12},{12... | collective-permute-start | bytes 540680 | tf_op jit(solution)/shard_map/ppermute | solution.py:341
  109.0 3.8 %ownpart.1 = (bf16[256,7168]{1,0:T(8,128)(2,1)S(1)}, bf16[256,7168]{1,0:T(8,128)(2,1)S(1)}, bf16[256,7168]{1,0:T(8,128)(2,1)S(1)}, f32[4,128,256]{2,1,0:T(8,128)S(1)}) custom-call(s32[1]{0:T(128)} %bitcast.here_ref.refs_0_, s32[1]{0:T(128)} %bitcast.1.odd_ref.refs_1_, bf16[4,32,2,1408]{3,2,1,0:T(2,128)(2,1)S(1)} %all-to-all-done.1.refs_0_, ...), custom_call_target="tpu_custom_call" | custom-call | flops 469762048 | bytes 22020096 | tf_op jit(solution)/shard_map/ownpart/pallas_call | solution.py:207
  112.8 2.8 %collective-permute-done.6.refs_3_ = bf16[32,2,1408]{2,1,0:T(2,128)(2,1)S(1)} collective-permute-done((bf16[32,2,1408]{2,1,0:T(2,128)(2,1)S(1)}, bf16[32,2,1408]{2,1,0:T(2,128)(2,1)S(1)}, u32[]{:S(2)}, u32[]{:S(2)}) %collective-permute-start.6) | collective-permute-done | bytes 180256 | tf_op jit(solution)/shard_map/ppermute | solution.py:341
  115.6 1.8 %experts.1 = (bf16[128,256]{1,0:T(8,128)(2,1)S(1)}, bf16[128,256]{1,0:T(8,128)(2,1)S(1)}, bf16[64,1408]{1,0:T(8,128)(2,1)S(1)}, bf16[64,1408]{1,0:T(8,128)(2,1)S...) custom-call(s32[1]{0:T(128)} %bitcast.here_ref.refs_0_, s32[1]{0:T(128)} %bitcast.1.odd_ref.refs_1_, ...), custom_call_target="tpu_custom_call" | custom-call | flops 704643072 | bytes 11010048 | tf_op jit(solution)/shard_map/experts/pallas_call | solution.py:292
  117.5 2.2 %collective-permute-start.7 = (bf16[64,1408]{1,0:T(8,128)(2,1)S(1)}, bf16[64,1408]{1,0:T(8,128)(2,1)S(1)}, u32[]{:S(2)}, u32[]{:S(2)}) collective-permute-start(bf16[64,1408]{1,0:T(8,128)(2,1)S(1)} %get-tuple-element.21), channel_id=1, source_target_pairs={{0,8},{8,0},{16,24},{24,16},{32,40},{40,32},{48,56},{56,48},{64,72... | collective-permute-start | bytes 540680 | tf_op jit(solution)/shard_map/ppermute | solution.py:365
  119.7 2.0 %collective-permute-start.8 = (bf16[64,1408]{1,0:T(8,128)(2,1)S(1)}, bf16[64,1408]{1,0:T(8,128)(2,1)S(1)}, u32[]{:S(2)}, u32[]{:S(2)}) collective-permute-start(bf16[64,1408]{1,0:T(8,128)(2,1)S(1)} %get-tuple-element.23), channel_id=1, source_target_pairs={{0,2},{2,0},{4,6},{6,4},{1,3},{3,1},{5,7},{7,5},{8,10},{10,8},{12,... | collective-permute-start | bytes 540680 | tf_op jit(solution)/shard_map/ppermute | solution.py:341
  121.6 3.8 %collective-permute-start.9 = (bf16[64,1408]{1,0:T(8,128)(2,1)S(1)}, bf16[64,1408]{1,0:T(8,128)(2,1)S(1)}, u32[]{:S(2)}, u32[]{:S(2)}) collective-permute-start(bf16[64,1408]{1,0:T(8,128)(2,1)S(1)} %get-tuple-element.24), channel_id=1, source_target_pairs={{0,6},{2,4},{4,2},{6,0},{1,7},{3,5},{5,3},{7,1},{8,14},{10,12},{12... | collective-permute-start | bytes 540680 | tf_op jit(solution)/shard_map/ppermute | solution.py:341
  125.4 1.4 keepdown.1
  126.8 3.6 %all-to-all-start.2 = ((bf16[4,64,1408]{2,1,0:T(8,128)(2,1)}), bf16[4,64,1408]{2,1,0:T(8,128)(2,1)S(1)}, u32[]{:S(2)}, u32[]{:S(2)}) async-start(bf16[4,64,1408]{2,1,0:T(8,128)(2,1)} %keepdown.1), calls=%async_computation.2 | async-start | bytes 1441792 | tf_op jit(solution)/shard_map/all_to_all | solution.py:344
  130.4 0.0 copy-start
  130.4 0.0 copy-start.1
  130.4 0.1 add_convert_fusion.1
  130.5 3.7 %collective-permute-start.10 = (bf16[64,1408]{1,0:T(8,128)(2,1)S(1)}, bf16[64,1408]{1,0:T(8,128)(2,1)S(1)}, u32[]{:S(2)}, u32[]{:S(2)}) collective-permute-start(bf16[64,1408]{1,0:T(8,128)(2,1)S(1)} %add_convert_fusion.1), channel_id=1, source_target_pairs={{0,8},{8,0},{16,24},{24,16},{32,40},{40,32},{48,56},{56,48},{64,72... | collective-permute-start | bytes 540680 | tf_op jit(solution)/shard_map/ppermute | solution.py:372
  134.2 6.4 %all-to-all-done.2 = bf16[4,64,1408]{2,1,0:T(8,128)(2,1)S(1)} async-done(((bf16[4,64,1408]{2,1,0:T(8,128)(2,1)}), bf16[4,64,1408]{2,1,0:T(8,128)(2,1)S(1)}, u32[]{:S(2)}, u32[]{:S(2)}) %all-to-all-start.2) | async-done | bytes 720928 | tf_op jit(solution)/shard_map/all_to_all | solution.py:344
  140.5 0.1 convert_reduce_fusion
  140.7 0.7 reshape.12
  141.4 4.8 %all-to-all-start.3 = ((bf16[32,2,1408]{2,1,0:T(2,128)(2,1)}), bf16[32,2,1408]{2,1,0:T(2,128)(2,1)S(1)}, u32[]{:S(2)}, u32[]{:S(2)}) async-start(bf16[32,2,1408]{2,1,0:T(2,128)(2,1)} %reshape.12), calls=%async_computation.3 | async-start | bytes 360448 | tf_op jit(solution)/shard_map/all_to_all | solution.py:347
  146.2 0.6 route.1.w_ref
  146.9 31.7 %all-to-all-done.3.x_ref = bf16[32,2,1408]{2,1,0:T(2,128)(2,1)S(1)} async-done(((bf16[32,2,1408]{2,1,0:T(2,128)(2,1)}), bf16[32,2,1408]{2,1,0:T(2,128)(2,1)S(1)}, u32[]{:S(2)}, u32[]{:S(2)}) %all-to-all-start.3) | async-done | bytes 180256 | tf_op jit(solution)/shard_map/all_to_all | solution.py:347
  178.6 0.8 mix.1
  (13 shorter events, 0.1 us)
Async XLA Ops:
  0.0 107.0 %collective-permute-start = (bf16[128,7168]{1,0:T(8,128)(2,1)}, bf16[128,7168]{1,0:T(8,128)(2,1)S(1)}, u32[]{:S(2)}, u32[]{:S(2)}) collective-permute-start(bf16[128,7168]{1,0:T(8,128)(2,1)} %bitcast.5), channel_id=1, source_target_pairs={{0,1},{1,0},{2,3},{3,2},{4,5},{5,4},{6,7},{7,6},{8,9},{9,8},{10,11... | collective-permute-start | bytes 5505032 | tf_op jit(solution)/shard_map/ppermute | solution.py:350
  3.8 81.4 %all-to-all-start = ((bf16[32,2,1408]{2,1,0:T(2,128)(2,1)}), bf16[32,2,1408]{2,1,0:T(2,128)(2,1)S(1)}, u32[]{:S(2)}, u32[]{:S(2)}) async-start(bf16[32,2,1408]{2,1,0:T(2,128)(2,1)} %pack.1), calls=%async_computation | async-start | bytes 360448 | tf_op jit(solution)/shard_map/all_to_all | solution.py:347
  49.6 59.4 %collective-permute-start.1 = (bf16[128,7168]{1,0:T(8,128)(2,1)}, bf16[128,7168]{1,0:T(8,128)(2,1)}, u32[]{:S(2)}, u32[]{:S(2)}) collective-permute-start(bf16[128,7168]{1,0:T(8,128)(2,1)} %bitcast.7), channel_id=1, source_target_pairs={{0,1},{1,0},{2,3},{3,2},{4,5},{5,4},{6,7},{7,6},{8,9},{9,8},{10,11... | collective-permute-start | bytes 5505032 | tf_op jit(solution)/shard_map/ppermute | solution.py:350
  51.8 57.2 %collective-permute-start.2 = (bf16[128,7168]{1,0:T(8,128)(2,1)}, bf16[128,7168]{1,0:T(8,128)(2,1)}, u32[]{:S(2)}, u32[]{:S(2)}) collective-permute-start(bf16[128,7168]{1,0:T(8,128)(2,1)} %bitcast.9), channel_id=1, source_target_pairs={{0,1},{1,0},{2,3},{3,2},{4,5},{5,4},{6,7},{7,6},{8,9},{9,8},{10,11... | collective-permute-start | bytes 5505032 | tf_op jit(solution)/shard_map/ppermute | solution.py:350
  86.4 22.6 %all-to-all-start.1 = ((bf16[4,32,2,1408]{3,2,1,0:T(2,128)(2,1)}), bf16[4,32,2,1408]{3,2,1,0:T(2,128)(2,1)S(1)}, u32[]{:S(2)}, u32[]{:S(2)}) async-start(bf16[4,32,2,1408]{3,2,1,0:T(2,128)(2,1)} %broadcast_in_dim.2), calls=%async_computation.1 | async-start | bytes 1441792 | tf_op jit(solution)/shard_map/all_to_all | solution.py:344
  91.0 7.4 %collective-permute-start.3 = (bf16[32,2,1408]{2,1,0:T(2,128)(2,1)S(1)}, bf16[32,2,1408]{2,1,0:T(2,128)(2,1)S(1)}, u32[]{:S(2)}, u32[]{:S(2)}) collective-permute-start(bf16[32,2,1408]{2,1,0:T(2,128)(2,1)S(1)} %all-to-all-done), channel_id=1, source_target_pairs={{0,8},{8,0},{16,24},{24,16},{32,40},{40,32},{48,56},{56,48},{64,72... | collective-permute-start | bytes 540680 | tf_op jit(solution)/shard_map/ppermute | solution.py:354
  98.4 14.4 %collective-permute-start.4 = (bf16[32,2,1408]{2,1,0:T(2,128)(2,1)S(1)}, bf16[32,2,1408]{2,1,0:T(2,128)(2,1)S(1)}, u32[]{:S(2)}, u32[]{:S(2)}) collective-permute-start(bf16[32,2,1408]{2,1,0:T(2,128)(2,1)S(1)} %collective-permute-done.3.refs_0_), channel_id=1, source_target_pairs={{0,2},{2,0},{4,6},{6,4},{1,3},{3,1},{5,7},{7,5},{8,10},{10,8},{12,... | collective-permute-start | bytes 540680 | tf_op jit(solution)/shard_map/ppermute | solution.py:341
  102.4 10.4 %collective-permute-start.5 = (bf16[32,2,1408]{2,1,0:T(2,128)(2,1)S(1)}, bf16[32,2,1408]{2,1,0:T(2,128)(2,1)S(1)}, u32[]{:S(2)}, u32[]{:S(2)}) collective-permute-start(bf16[32,2,1408]{2,1,0:T(2,128)(2,1)S(1)} %collective-permute-done.3.refs_0_), channel_id=1, source_target_pairs={{0,4},{2,6},{4,0},{6,2},{1,5},{3,7},{5,1},{7,3},{8,12},{10,14},{12... | collective-permute-start | bytes 540680 | tf_op jit(solution)/shard_map/ppermute | solution.py:341
  107.0 8.6 %collective-permute-start.6 = (bf16[32,2,1408]{2,1,0:T(2,128)(2,1)S(1)}, bf16[32,2,1408]{2,1,0:T(2,128)(2,1)S(1)}, u32[]{:S(2)}, u32[]{:S(2)}) collective-permute-start(bf16[32,2,1408]{2,1,0:T(2,128)(2,1)S(1)} %collective-permute-done.3.refs_0_), channel_id=1, source_target_pairs={{0,6},{2,4},{4,2},{6,0},{1,7},{3,5},{5,3},{7,1},{8,14},{10,12},{12... | collective-permute-start | bytes 540680 | tf_op jit(solution)/shard_map/ppermute | solution.py:341
  117.5 8.0 %collective-permute-start.7 = (bf16[64,1408]{1,0:T(8,128)(2,1)S(1)}, bf16[64,1408]{1,0:T(8,128)(2,1)S(1)}, u32[]{:S(2)}, u32[]{:S(2)}) collective-permute-start(bf16[64,1408]{1,0:T(8,128)(2,1)S(1)} %get-tuple-element.21), channel_id=1, source_target_pairs={{0,8},{8,0},{16,24},{24,16},{32,40},{40,32},{48,56},{56,48},{64,72... | collective-permute-start | bytes 540680 | tf_op jit(solution)/shard_map/ppermute | solution.py:365
  119.7 10.7 %collective-permute-start.8 = (bf16[64,1408]{1,0:T(8,128)(2,1)S(1)}, bf16[64,1408]{1,0:T(8,128)(2,1)S(1)}, u32[]{:S(2)}, u32[]{:S(2)}) collective-permute-start(bf16[64,1408]{1,0:T(8,128)(2,1)S(1)} %get-tuple-element.23), channel_id=1, source_target_pairs={{0,2},{2,0},{4,6},{6,4},{1,3},{3,1},{5,7},{7,5},{8,10},{10,8},{12,... | collective-permute-start | bytes 540680 | tf_op jit(solution)/shard_map/ppermute | solution.py:341
  121.6 8.8 %collective-permute-start.9 = (bf16[64,1408]{1,0:T(8,128)(2,1)S(1)}, bf16[64,1408]{1,0:T(8,128)(2,1)S(1)}, u32[]{:S(2)}, u32[]{:S(2)}) collective-permute-start(bf16[64,1408]{1,0:T(8,128)(2,1)S(1)} %get-tuple-element.24), channel_id=1, source_target_pairs={{0,6},{2,4},{4,2},{6,0},{1,7},{3,5},{5,3},{7,1},{8,14},{10,12},{12... | collective-permute-start | bytes 540680 | tf_op jit(solution)/shard_map/ppermute | solution.py:341
  126.8 13.7 %all-to-all-start.2 = ((bf16[4,64,1408]{2,1,0:T(8,128)(2,1)}), bf16[4,64,1408]{2,1,0:T(8,128)(2,1)S(1)}, u32[]{:S(2)}, u32[]{:S(2)}) async-start(bf16[4,64,1408]{2,1,0:T(8,128)(2,1)} %keepdown.1), calls=%async_computation.2 | async-start | bytes 1441792 | tf_op jit(solution)/shard_map/all_to_all | solution.py:344
  130.4 15.8 %copy-start = (s32[4,8]{1,0:T(4,128)S(1)}, s32[4,8]{1,0:T(4,128)}, u32[]{:S(2)}) copy-start(s32[4,8]{1,0:T(4,128)} %ids_hbm.1) | copy-start | bytes 388
  130.4 15.8 %copy-start.1 = (s32[4,8]{1,0:T(4,128)S(1)}, s32[4,8]{1,0:T(4,128)}, u32[]{:S(2)}) copy-start(s32[4,8]{1,0:T(4,128)} %code_ref.1) | copy-start | bytes 388
  130.5 10.1 %collective-permute-start.10 = (bf16[64,1408]{1,0:T(8,128)(2,1)S(1)}, bf16[64,1408]{1,0:T(8,128)(2,1)S(1)}, u32[]{:S(2)}, u32[]{:S(2)}) collective-permute-start(bf16[64,1408]{1,0:T(8,128)(2,1)S(1)} %add_convert_fusion.1), channel_id=1, source_target_pairs={{0,8},{8,0},{16,24},{24,16},{32,40},{40,32},{48,56},{56,48},{64,72... | collective-permute-start | bytes 540680 | tf_op jit(solution)/shard_map/ppermute | solution.py:372
  141.4 37.2 %all-to-all-start.3 = ((bf16[32,2,1408]{2,1,0:T(2,128)(2,1)}), bf16[32,2,1408]{2,1,0:T(2,128)(2,1)S(1)}, u32[]{:S(2)}, u32[]{:S(2)}) async-start(bf16[32,2,1408]{2,1,0:T(2,128)(2,1)} %reshape.12), calls=%async_computation.3 | async-start | bytes 360448 | tf_op jit(solution)/shard_map/all_to_all | solution.py:347

commit v10 on v9

--- a/solution.py
+++ b/solution.py
@@ -23,9 +23,9 @@
     return -(-half // 256) * 128
 
 
-def routing(ids_ref, rows, axis):
-    shape = (rows, 1) if axis == 0 else (1, rows)
-    row = lax.broadcasted_iota(I32, shape, axis)
+def routing(ids_ref, rows):
+    shape = (1, rows)
+    row = lax.broadcasted_iota(I32, shape, 1)
     expert, side, part = row // 4, (row // 2) % 2, row % 2
     tokens, picks = ids_ref.shape
     count = jnp.zeros(shape, I32)
@@ -52,22 +52,27 @@
     take_ids.start()
     take_tok.start()
     take_ids.wait()
-    routes, side, part = routing(ids_ref, rows, 0)
+    routes, side, part = routing(ids_ref, rows)
+    mains, lowers, uppers = [], [], []
+    for p in range(2):
+        here = (side == p).astype(I32)
+        for _, first, third in routes:
+            mains.append(first * here)
+            lowers.append(third * here * (1 - part))
+            uppers.append(third * here * part)
+    main, tail = (
+        jnp.concatenate(x, axis=0).astype(F32).astype(BF) for x in (mains, lowers + uppers)
+    )
     take_tok.wait()
     tok = tok_ref[...].astype(F32)
-    main = jnp.zeros((rows, half), F32)
-    tail = jnp.zeros((rows, low), F32)
-    for t, (_, first, third) in enumerate(routes):
-        for p in range(2):
-            piece = tok[t : t + 1, p * half : (p + 1) * half]
-            here = (side == p).astype(I32)
-            main = main + (first * here).astype(F32) * piece
-            rest = piece[:, low:]
-            if 2 * low > half:
-                rest = jnp.concatenate([rest, jnp.zeros((1, 2 * low - half), F32)], axis=1)
-            third_here = third * here
-            tail = tail + (third_here * (1 - part)).astype(F32) * piece[:, :low]
-            tail = tail + (third_here * part).astype(F32) * rest
+    both = jnp.concatenate([tok[:, :half], tok[:, half:]], axis=0)
+    rest = both[:, low:]
+    if 2 * low > half:
+        rest = jnp.concatenate([rest, jnp.zeros((rest.shape[0], 2 * low - half), F32)], axis=1)
+    ends = jnp.concatenate([both[:, :low], rest], axis=0)
+    pick = (((0,), (0,)), ((), ()))
+    main = lax.dot_general(main, both.astype(BF), pick, preferred_element_type=F32)
+    tail = lax.dot_general(tail, ends.astype(BF), pick, preferred_element_type=F32)
     o_ref[:, :, :half] = main.astype(BF).reshape(owners, 2, half)
     o_ref[:, :, half:] = tail.astype(BF).reshape(owners, 2, low)
 
@@ -95,7 +100,7 @@
 
 
 def route_kernel(ids_ref, code_ref, w_ref):
-    routes, side, part = routing(ids_ref, w_ref.shape[1], 1)
+    routes, side, part = routing(ids_ref, w_ref.shape[1])
     mains, lowers, uppers = [], [], []
     for p in range(2):
         for t, (hits, first, third) in enumerate(routes):

time: 180 us -> 180 us (level)
  no operation moved by 1% of the time
where the time goes in v10:
time: 180 us; the launch traced here: 179 us
  starting transfers between devices  89.4 us (50%)
  waiting for transfers between devices  77.3 us (43%)
  Pallas kernels  10 us (6%)
  local copies, waits for them, and re-layouts  1.99 us (1%)
    all_to_all x2, waiting for transfers between devices, along(): return lax.all_to_all(x, 'expert', split_axis=0, concat_axis=0, tiled=True)  62.9 us
    all_to_all x2, starting transfers between devices, along(): return lax.all_to_all(x, 'expert', split_axis=0, concat_axis=0, tiled=True)  50.5 us
    ppermute x5, starting transfers between devices, swapped(): return lax.ppermute(x, 'tensor', [(i, i ^ k) for i in range(parts)])  16.2 us
    all_to_all x2, starting transfers between devices, across(): return lax.all_to_all(x, 'tensor', split_axis=0, concat_axis=0, tiled=True)  8.15 us
    all_to_all x2, waiting for transfers between devices, across(): return lax.all_to_all(x, 'tensor', split_axis=0, concat_axis=0, tiled=True)  6.37 us
    ppermute x3, starting transfers between devices, shards(): other = [lax.ppermute(w, 'sub', swap_sub) for w in own]  6.34 us
    ppermute x1, waiting for transfers between devices, shards(): partner = lax.ppermute(arrived, 'expert', swap_pair)  5.18 us
    pallas_call x1, Pallas kernels, own_part(): pl.pallas_call(own_kernel, out_shape=(shape,) * 3 + (jax.ShapeDtypeStruct...  3.76 us
  transfers between devices with their start and end apart: 15, of which 5 were waited for; matrix products, arithmetic and copies ran while one was open for 1% of the time, Pallas kernels for 4%

profile of v10, /device:TPU:40, one launch (start us, length us, event | category | flops | bytes accessed | tf_op | source)
XLA Modules:
  0.0 179.2 jit_solution(5959572353863228261)
XLA Ops:
  0.0 1.9 %collective-permute-start = (bf16[128,7168]{1,0:T(8,128)(2,1)}, bf16[128,7168]{1,0:T(8,128)(2,1)S(1)}, u32[]{:S(2)}, u32[]{:S(2)}) collective-permute-start(bf16[128,7168]{1,0:T(8,128)(2,1)} %bitcast.5), channel_id=1, source_target_pairs={{0,1},{1,0},{2,3},{3,2},{4,5},{5,4},{6,7},{7,6},{8,9},{9,8},{10,11... | collective-permute-start | bytes 5505032 | tf_op jit(solution)/shard_map/ppermute | solution.py:355
  2.0 1.7 pack.1
  3.6 45.8 %all-to-all-start = ((bf16[32,2,1408]{2,1,0:T(2,128)(2,1)}), bf16[32,2,1408]{2,1,0:T(2,128)(2,1)S(1)}, u32[]{:S(2)}, u32[]{:S(2)}) async-start(bf16[32,2,1408]{2,1,0:T(2,128)(2,1)} %pack.1), calls=%async_computation | async-start | bytes 360448 | tf_op jit(solution)/shard_map/all_to_all | solution.py:352
  49.4 2.2 %collective-permute-start.1 = (bf16[128,7168]{1,0:T(8,128)(2,1)}, bf16[128,7168]{1,0:T(8,128)(2,1)}, u32[]{:S(2)}, u32[]{:S(2)}) collective-permute-start(bf16[128,7168]{1,0:T(8,128)(2,1)} %bitcast.7), channel_id=1, source_target_pairs={{0,1},{1,0},{2,3},{3,2},{4,5},{5,4},{6,7},{7,6},{8,9},{9,8},{10,11... | collective-permute-start | bytes 5505032 | tf_op jit(solution)/shard_map/ppermute | solution.py:355
  51.6 2.2 %collective-permute-start.2 = (bf16[128,7168]{1,0:T(8,128)(2,1)}, bf16[128,7168]{1,0:T(8,128)(2,1)}, u32[]{:S(2)}, u32[]{:S(2)}) collective-permute-start(bf16[128,7168]{1,0:T(8,128)(2,1)} %bitcast.9), channel_id=1, source_target_pairs={{0,1},{1,0},{2,3},{3,2},{4,5},{5,4},{6,7},{7,6},{8,9},{9,8},{10,11... | collective-permute-start | bytes 5505032 | tf_op jit(solution)/shard_map/ppermute | solution.py:355
  53.8 31.2 %all-to-all-done = bf16[32,2,1408]{2,1,0:T(2,128)(2,1)S(1)} async-done(((bf16[32,2,1408]{2,1,0:T(2,128)(2,1)}), bf16[32,2,1408]{2,1,0:T(2,128)(2,1)S(1)}, u32[]{:S(2)}, u32[]{:S(2)}) %all-to-all-start) | async-done | bytes 180256 | tf_op jit(solution)/shard_map/all_to_all | solution.py:352
  85.0 1.2 broadcast_in_dim.2
  86.2 4.6 %all-to-all-start.1 = ((bf16[4,32,2,1408]{3,2,1,0:T(2,128)(2,1)}), bf16[4,32,2,1408]{3,2,1,0:T(2,128)(2,1)S(1)}, u32[]{:S(2)}, u32[]{:S(2)}) async-start(bf16[4,32,2,1408]{3,2,1,0:T(2,128)(2,1)} %broadcast_in_dim.2), calls=%async_computation.1 | async-start | bytes 1441792 | tf_op jit(solution)/shard_map/all_to_all | solution.py:349
  90.8 2.2 %collective-permute-start.3 = (bf16[32,2,1408]{2,1,0:T(2,128)(2,1)S(1)}, bf16[32,2,1408]{2,1,0:T(2,128)(2,1)S(1)}, u32[]{:S(2)}, u32[]{:S(2)}) collective-permute-start(bf16[32,2,1408]{2,1,0:T(2,128)(2,1)S(1)} %all-to-all-done), channel_id=1, source_target_pairs={{0,8},{8,0},{16,24},{24,16},{32,40},{40,32},{48,56},{56,48},{64,72... | collective-permute-start | bytes 540680 | tf_op jit(solution)/shard_map/ppermute | solution.py:359
  93.0 5.2 %collective-permute-done.3.refs_0_ = bf16[32,2,1408]{2,1,0:T(2,128)(2,1)S(1)} collective-permute-done((bf16[32,2,1408]{2,1,0:T(2,128)(2,1)S(1)}, bf16[32,2,1408]{2,1,0:T(2,128)(2,1)S(1)}, u32[]{:S(2)}, u32[]{:S(2)}) %collective-permute-start.3) | collective-permute-done | bytes 180256 | tf_op jit(solution)/shard_map/ppermute | solution.py:359
  98.2 4.0 %collective-permute-start.4 = (bf16[32,2,1408]{2,1,0:T(2,128)(2,1)S(1)}, bf16[32,2,1408]{2,1,0:T(2,128)(2,1)S(1)}, u32[]{:S(2)}, u32[]{:S(2)}) collective-permute-start(bf16[32,2,1408]{2,1,0:T(2,128)(2,1)S(1)} %collective-permute-done.3.refs_0_), channel_id=1, source_target_pairs={{0,2},{2,0},{4,6},{6,4},{1,3},{3,1},{5,7},{7,5},{8,10},{10,8},{12,... | collective-permute-start | bytes 540680 | tf_op jit(solution)/shard_map/ppermute | solution.py:346
  102.2 4.6 %collective-permute-start.5 = (bf16[32,2,1408]{2,1,0:T(2,128)(2,1)S(1)}, bf16[32,2,1408]{2,1,0:T(2,128)(2,1)S(1)}, u32[]{:S(2)}, u32[]{:S(2)}) collective-permute-start(bf16[32,2,1408]{2,1,0:T(2,128)(2,1)S(1)} %collective-permute-done.3.refs_0_), channel_id=1, source_target_pairs={{0,4},{2,6},{4,0},{6,2},{1,5},{3,7},{5,1},{7,3},{8,12},{10,14},{12... | collective-permute-start | bytes 540680 | tf_op jit(solution)/shard_map/ppermute | solution.py:346
  106.8 2.0 %collective-permute-start.6 = (bf16[32,2,1408]{2,1,0:T(2,128)(2,1)S(1)}, bf16[32,2,1408]{2,1,0:T(2,128)(2,1)S(1)}, u32[]{:S(2)}, u32[]{:S(2)}) collective-permute-start(bf16[32,2,1408]{2,1,0:T(2,128)(2,1)S(1)} %collective-permute-done.3.refs_0_), channel_id=1, source_target_pairs={{0,6},{2,4},{4,2},{6,0},{1,7},{3,5},{5,3},{7,1},{8,14},{10,12},{12... | collective-permute-start | bytes 540680 | tf_op jit(solution)/shard_map/ppermute | solution.py:346
  108.8 3.8 %ownpart.1 = (bf16[256,7168]{1,0:T(8,128)(2,1)S(1)}, bf16[256,7168]{1,0:T(8,128)(2,1)S(1)}, bf16[256,7168]{1,0:T(8,128)(2,1)S(1)}, f32[4,128,256]{2,1,0:T(8,128)S(1)}) custom-call(s32[1]{0:T(128)} %bitcast.here_ref.refs_0_, s32[1]{0:T(128)} %bitcast.1.odd_ref.refs_1_, bf16[4,32,2,1408]{3,2,1,0:T(2,128)(2,1)S(1)} %all-to-all-done.1.refs_0_, ...), custom_call_target="tpu_custom_call" | custom-call | flops 469762048 | bytes 22020096 | tf_op jit(solution)/shard_map/ownpart/pallas_call | solution.py:212
  112.6 2.8 %collective-permute-done.6.refs_3_ = bf16[32,2,1408]{2,1,0:T(2,128)(2,1)S(1)} collective-permute-done((bf16[32,2,1408]{2,1,0:T(2,128)(2,1)S(1)}, bf16[32,2,1408]{2,1,0:T(2,128)(2,1)S(1)}, u32[]{:S(2)}, u32[]{:S(2)}) %collective-permute-start.6) | collective-permute-done | bytes 180256 | tf_op jit(solution)/shard_map/ppermute | solution.py:346
  115.4 1.8 %experts.1 = (bf16[128,256]{1,0:T(8,128)(2,1)S(1)}, bf16[128,256]{1,0:T(8,128)(2,1)S(1)}, bf16[64,1408]{1,0:T(8,128)(2,1)S(1)}, bf16[64,1408]{1,0:T(8,128)(2,1)S...) custom-call(s32[1]{0:T(128)} %bitcast.here_ref.refs_0_, s32[1]{0:T(128)} %bitcast.1.odd_ref.refs_1_, ...), custom_call_target="tpu_custom_call" | custom-call | flops 704643072 | bytes 11010048 | tf_op jit(solution)/shard_map/experts/pallas_call | solution.py:297
  117.2 2.2 %collective-permute-start.7 = (bf16[64,1408]{1,0:T(8,128)(2,1)S(1)}, bf16[64,1408]{1,0:T(8,128)(2,1)S(1)}, u32[]{:S(2)}, u32[]{:S(2)}) collective-permute-start(bf16[64,1408]{1,0:T(8,128)(2,1)S(1)} %get-tuple-element.21), channel_id=1, source_target_pairs={{0,8},{8,0},{16,24},{24,16},{32,40},{40,32},{48,56},{56,48},{64,72... | collective-permute-start | bytes 540680 | tf_op jit(solution)/shard_map/ppermute | solution.py:370
  119.5 2.0 %collective-permute-start.8 = (bf16[64,1408]{1,0:T(8,128)(2,1)S(1)}, bf16[64,1408]{1,0:T(8,128)(2,1)S(1)}, u32[]{:S(2)}, u32[]{:S(2)}) collective-permute-start(bf16[64,1408]{1,0:T(8,128)(2,1)S(1)} %get-tuple-element.23), channel_id=1, source_target_pairs={{0,2},{2,0},{4,6},{6,4},{1,3},{3,1},{5,7},{7,5},{8,10},{10,8},{12,... | collective-permute-start | bytes 540680 | tf_op jit(solution)/shard_map/ppermute | solution.py:346
  121.4 3.8 %collective-permute-start.9 = (bf16[64,1408]{1,0:T(8,128)(2,1)S(1)}, bf16[64,1408]{1,0:T(8,128)(2,1)S(1)}, u32[]{:S(2)}, u32[]{:S(2)}) collective-permute-start(bf16[64,1408]{1,0:T(8,128)(2,1)S(1)} %get-tuple-element.24), channel_id=1, source_target_pairs={{0,6},{2,4},{4,2},{6,0},{1,7},{3,5},{5,3},{7,1},{8,14},{10,12},{12... | collective-permute-start | bytes 540680 | tf_op jit(solution)/shard_map/ppermute | solution.py:346
  125.2 1.4 keepdown.1
  126.6 3.6 %all-to-all-start.2 = ((bf16[4,64,1408]{2,1,0:T(8,128)(2,1)}), bf16[4,64,1408]{2,1,0:T(8,128)(2,1)S(1)}, u32[]{:S(2)}, u32[]{:S(2)}) async-start(bf16[4,64,1408]{2,1,0:T(8,128)(2,1)} %keepdown.1), calls=%async_computation.2 | async-start | bytes 1441792 | tf_op jit(solution)/shard_map/all_to_all | solution.py:349
  130.2 0.0 copy-start
  130.2 0.0 copy-start.1
  130.2 0.1 add_convert_fusion.1
  130.3 3.7 %collective-permute-start.10 = (bf16[64,1408]{1,0:T(8,128)(2,1)S(1)}, bf16[64,1408]{1,0:T(8,128)(2,1)S(1)}, u32[]{:S(2)}, u32[]{:S(2)}) collective-permute-start(bf16[64,1408]{1,0:T(8,128)(2,1)S(1)} %add_convert_fusion.1), channel_id=1, source_target_pairs={{0,8},{8,0},{16,24},{24,16},{32,40},{40,32},{48,56},{56,48},{64,72... | collective-permute-start | bytes 540680 | tf_op jit(solution)/shard_map/ppermute | solution.py:377
  134.0 6.4 %all-to-all-done.2 = bf16[4,64,1408]{2,1,0:T(8,128)(2,1)S(1)} async-done(((bf16[4,64,1408]{2,1,0:T(8,128)(2,1)}), bf16[4,64,1408]{2,1,0:T(8,128)(2,1)S(1)}, u32[]{:S(2)}, u32[]{:S(2)}) %all-to-all-start.2) | async-done | bytes 720928 | tf_op jit(solution)/shard_map/all_to_all | solution.py:349
  140.3 0.1 convert_reduce_fusion
  140.5 0.7 reshape.12
  141.2 4.8 %all-to-all-start.3 = ((bf16[32,2,1408]{2,1,0:T(2,128)(2,1)}), bf16[32,2,1408]{2,1,0:T(2,128)(2,1)S(1)}, u32[]{:S(2)}, u32[]{:S(2)}) async-start(bf16[32,2,1408]{2,1,0:T(2,128)(2,1)} %reshape.12), calls=%async_computation.3 | async-start | bytes 360448 | tf_op jit(solution)/shard_map/all_to_all | solution.py:352
  146.0 0.6 route.1.w_ref
  146.7 31.7 %all-to-all-done.3.x_ref = bf16[32,2,1408]{2,1,0:T(2,128)(2,1)S(1)} async-done(((bf16[32,2,1408]{2,1,0:T(2,128)(2,1)}), bf16[32,2,1408]{2,1,0:T(2,128)(2,1)S(1)}, u32[]{:S(2)}, u32[]{:S(2)}) %all-to-all-start.3) | async-done | bytes 180256 | tf_op jit(solution)/shard_map/all_to_all | solution.py:352
  178.4 0.8 mix.1
  (13 shorter events, 0.1 us)
Async XLA Ops:
  0.0 106.8 %collective-permute-start = (bf16[128,7168]{1,0:T(8,128)(2,1)}, bf16[128,7168]{1,0:T(8,128)(2,1)S(1)}, u32[]{:S(2)}, u32[]{:S(2)}) collective-permute-start(bf16[128,7168]{1,0:T(8,128)(2,1)} %bitcast.5), channel_id=1, source_target_pairs={{0,1},{1,0},{2,3},{3,2},{4,5},{5,4},{6,7},{7,6},{8,9},{9,8},{10,11... | collective-permute-start | bytes 5505032 | tf_op jit(solution)/shard_map/ppermute | solution.py:355
  3.6 81.4 %all-to-all-start = ((bf16[32,2,1408]{2,1,0:T(2,128)(2,1)}), bf16[32,2,1408]{2,1,0:T(2,128)(2,1)S(1)}, u32[]{:S(2)}, u32[]{:S(2)}) async-start(bf16[32,2,1408]{2,1,0:T(2,128)(2,1)} %pack.1), calls=%async_computation | async-start | bytes 360448 | tf_op jit(solution)/shard_map/all_to_all | solution.py:352
  49.4 59.4 %collective-permute-start.1 = (bf16[128,7168]{1,0:T(8,128)(2,1)}, bf16[128,7168]{1,0:T(8,128)(2,1)}, u32[]{:S(2)}, u32[]{:S(2)}) collective-permute-start(bf16[128,7168]{1,0:T(8,128)(2,1)} %bitcast.7), channel_id=1, source_target_pairs={{0,1},{1,0},{2,3},{3,2},{4,5},{5,4},{6,7},{7,6},{8,9},{9,8},{10,11... | collective-permute-start | bytes 5505032 | tf_op jit(solution)/shard_map/ppermute | solution.py:355
  51.6 57.2 %collective-permute-start.2 = (bf16[128,7168]{1,0:T(8,128)(2,1)}, bf16[128,7168]{1,0:T(8,128)(2,1)}, u32[]{:S(2)}, u32[]{:S(2)}) collective-permute-start(bf16[128,7168]{1,0:T(8,128)(2,1)} %bitcast.9), channel_id=1, source_target_pairs={{0,1},{1,0},{2,3},{3,2},{4,5},{5,4},{6,7},{7,6},{8,9},{9,8},{10,11... | collective-permute-start | bytes 5505032 | tf_op jit(solution)/shard_map/ppermute | solution.py:355
  86.2 22.6 %all-to-all-start.1 = ((bf16[4,32,2,1408]{3,2,1,0:T(2,128)(2,1)}), bf16[4,32,2,1408]{3,2,1,0:T(2,128)(2,1)S(1)}, u32[]{:S(2)}, u32[]{:S(2)}) async-start(bf16[4,32,2,1408]{3,2,1,0:T(2,128)(2,1)} %broadcast_in_dim.2), calls=%async_computation.1 | async-start | bytes 1441792 | tf_op jit(solution)/shard_map/all_to_all | solution.py:349
  90.8 7.4 %collective-permute-start.3 = (bf16[32,2,1408]{2,1,0:T(2,128)(2,1)S(1)}, bf16[32,2,1408]{2,1,0:T(2,128)(2,1)S(1)}, u32[]{:S(2)}, u32[]{:S(2)}) collective-permute-start(bf16[32,2,1408]{2,1,0:T(2,128)(2,1)S(1)} %all-to-all-done), channel_id=1, source_target_pairs={{0,8},{8,0},{16,24},{24,16},{32,40},{40,32},{48,56},{56,48},{64,72... | collective-permute-start | bytes 540680 | tf_op jit(solution)/shard_map/ppermute | solution.py:359
  98.2 14.4 %collective-permute-start.4 = (bf16[32,2,1408]{2,1,0:T(2,128)(2,1)S(1)}, bf16[32,2,1408]{2,1,0:T(2,128)(2,1)S(1)}, u32[]{:S(2)}, u32[]{:S(2)}) collective-permute-start(bf16[32,2,1408]{2,1,0:T(2,128)(2,1)S(1)} %collective-permute-done.3.refs_0_), channel_id=1, source_target_pairs={{0,2},{2,0},{4,6},{6,4},{1,3},{3,1},{5,7},{7,5},{8,10},{10,8},{12,... | collective-permute-start | bytes 540680 | tf_op jit(solution)/shard_map/ppermute | solution.py:346
  102.2 10.4 %collective-permute-start.5 = (bf16[32,2,1408]{2,1,0:T(2,128)(2,1)S(1)}, bf16[32,2,1408]{2,1,0:T(2,128)(2,1)S(1)}, u32[]{:S(2)}, u32[]{:S(2)}) collective-permute-start(bf16[32,2,1408]{2,1,0:T(2,128)(2,1)S(1)} %collective-permute-done.3.refs_0_), channel_id=1, source_target_pairs={{0,4},{2,6},{4,0},{6,2},{1,5},{3,7},{5,1},{7,3},{8,12},{10,14},{12... | collective-permute-start | bytes 540680 | tf_op jit(solution)/shard_map/ppermute | solution.py:346
  106.8 8.6 %collective-permute-start.6 = (bf16[32,2,1408]{2,1,0:T(2,128)(2,1)S(1)}, bf16[32,2,1408]{2,1,0:T(2,128)(2,1)S(1)}, u32[]{:S(2)}, u32[]{:S(2)}) collective-permute-start(bf16[32,2,1408]{2,1,0:T(2,128)(2,1)S(1)} %collective-permute-done.3.refs_0_), channel_id=1, source_target_pairs={{0,6},{2,4},{4,2},{6,0},{1,7},{3,5},{5,3},{7,1},{8,14},{10,12},{12... | collective-permute-start | bytes 540680 | tf_op jit(solution)/shard_map/ppermute | solution.py:346
  117.2 8.0 %collective-permute-start.7 = (bf16[64,1408]{1,0:T(8,128)(2,1)S(1)}, bf16[64,1408]{1,0:T(8,128)(2,1)S(1)}, u32[]{:S(2)}, u32[]{:S(2)}) collective-permute-start(bf16[64,1408]{1,0:T(8,128)(2,1)S(1)} %get-tuple-element.21), channel_id=1, source_target_pairs={{0,8},{8,0},{16,24},{24,16},{32,40},{40,32},{48,56},{56,48},{64,72... | collective-permute-start | bytes 540680 | tf_op jit(solution)/shard_map/ppermute | solution.py:370
  119.5 10.7 %collective-permute-start.8 = (bf16[64,1408]{1,0:T(8,128)(2,1)S(1)}, bf16[64,1408]{1,0:T(8,128)(2,1)S(1)}, u32[]{:S(2)}, u32[]{:S(2)}) collective-permute-start(bf16[64,1408]{1,0:T(8,128)(2,1)S(1)} %get-tuple-element.23), channel_id=1, source_target_pairs={{0,2},{2,0},{4,6},{6,4},{1,3},{3,1},{5,7},{7,5},{8,10},{10,8},{12,... | collective-permute-start | bytes 540680 | tf_op jit(solution)/shard_map/ppermute | solution.py:346
  121.4 8.8 %collective-permute-start.9 = (bf16[64,1408]{1,0:T(8,128)(2,1)S(1)}, bf16[64,1408]{1,0:T(8,128)(2,1)S(1)}, u32[]{:S(2)}, u32[]{:S(2)}) collective-permute-start(bf16[64,1408]{1,0:T(8,128)(2,1)S(1)} %get-tuple-element.24), channel_id=1, source_target_pairs={{0,6},{2,4},{4,2},{6,0},{1,7},{3,5},{5,3},{7,1},{8,14},{10,12},{12... | collective-permute-start | bytes 540680 | tf_op jit(solution)/shard_map/ppermute | solution.py:346
  126.6 13.8 %all-to-all-start.2 = ((bf16[4,64,1408]{2,1,0:T(8,128)(2,1)}), bf16[4,64,1408]{2,1,0:T(8,128)(2,1)S(1)}, u32[]{:S(2)}, u32[]{:S(2)}) async-start(bf16[4,64,1408]{2,1,0:T(8,128)(2,1)} %keepdown.1), calls=%async_computation.2 | async-start | bytes 1441792 | tf_op jit(solution)/shard_map/all_to_all | solution.py:349
  130.2 15.8 %copy-start = (s32[4,8]{1,0:T(4,128)S(1)}, s32[4,8]{1,0:T(4,128)}, u32[]{:S(2)}) copy-start(s32[4,8]{1,0:T(4,128)} %ids_hbm.1) | copy-start | bytes 388
  130.2 15.8 %copy-start.1 = (s32[4,8]{1,0:T(4,128)S(1)}, s32[4,8]{1,0:T(4,128)}, u32[]{:S(2)}) copy-start(s32[4,8]{1,0:T(4,128)} %code_ref.1) | copy-start | bytes 388
  130.3 10.1 %collective-permute-start.10 = (bf16[64,1408]{1,0:T(8,128)(2,1)S(1)}, bf16[64,1408]{1,0:T(8,128)(2,1)S(1)}, u32[]{:S(2)}, u32[]{:S(2)}) collective-permute-start(bf16[64,1408]{1,0:T(8,128)(2,1)S(1)} %add_convert_fusion.1), channel_id=1, source_target_pairs={{0,8},{8,0},{16,24},{24,16},{32,40},{40,32},{48,56},{56,48},{64,72... | collective-permute-start | bytes 540680 | tf_op jit(solution)/shard_map/ppermute | solution.py:377
  141.2 37.2 %all-to-all-start.3 = ((bf16[32,2,1408]{2,1,0:T(2,128)(2,1)}), bf16[32,2,1408]{2,1,0:T(2,128)(2,1)S(1)}, u32[]{:S(2)}, u32[]{:S(2)}) async-start(bf16[32,2,1408]{2,1,0:T(2,128)(2,1)} %reshape.12), calls=%async_computation.3 | async-start | bytes 360448 | tf_op jit(solution)/shard_map/all_to_all | solution.py:352
